TPU v7x, 128 devices: a whole 4x4x4 slice. The times are simulated.
128 devices in a mesh: member: 8 (over y, core), region: 16 (over x, z).
Axes of the slice: x: 4, y: 4, z: 4, core: 2. Of those that a mesh axis runs over, the one named last changes fastest.
Arguments:
- state: float32 [256, 8, 16384], P('member', None, 'region'), may hold values from -6 to 6
- adjacent_columns: int32 [6, 16384], P(None, 'region'), may hold values from 0 to 16383, as said below
- adjacent_rates: float32 [6, 16384], P(None, 'region'), may hold values from 0.02 to 0.16
- amplification_speed: float32 [16384], P('region'), may hold values from 0.05 to 0.5
- obs_patch: int32 [32768], P(('member', 'region')), may hold values from -1 to 127, as said below
- obs_row: int32 [32768], P(('member', 'region')), may hold values from 0 to 1023
- obs_value: float32 [32768], P(('member', 'region')), may hold values from -6 to 6
- obs_error: float32 [32768], P(('member', 'region')), may hold values from 0.5 to 2
Outputs:
- analysis: bfloat16 [256, 8, 16384], P('member', None, 'region')
Inputs may be any that keep to these rules, and one draw needn't show every extreme that they name: `adjacent_columns`: each neighbour lies within 256 positions of its column along the closed order of columns (index modulo 16384) and is never the column itself. `obs_patch`: at most 256 rows name one patch. Within the 256 rows of one device, at most 2 rows name any one patch; -1 marks a row without an observation.
All inputs are finite; a program needn't handle non-finite values.
Results may differ from a plain program's by a relative error of at most 0.01.
Values may be sent and summed in bfloat16 or wider, within the bound.
No kernel may reach another device: no remote copies, remote signals or barrier semaphores. Data moves between devices by JAX's collectives and lax.ppermute only.
A program may use at most 64 MiB of HBM per device.

v0:
```python
import functools
import math

import jax
import jax.numpy as jnp
from jax import lax
from jax.experimental import pallas as pl
from jax.experimental.pallas import tpu as pltpu
from jax.sharding import PartitionSpec as P

PATCH_CELLS = 128
RIM = 256
STEPS = 3
NS_ITERS = 6
LEVELS = 8
BLOCK = 256
WINDOW = BLOCK + 2 * RIM
HALO = STEPS * RIM
COEF_ROWS = 16


def high(value):
    return value.astype(jnp.bfloat16)


def low(value):
    return (value - high(value).astype(jnp.float32)).astype(jnp.bfloat16)


def dot_f32(a, b, dims=(((1,), (0,)), ((), ()))):
    return lax.dot_general(a, b, dims, preferred_element_type=jnp.float32)


def dot_split(a, b, dims=(((1,), (0,)), ((), ()))):
    ah, al, bh, bl = high(a), low(a), high(b), low(b)
    return dot_f32(ah, bh, dims) + (dot_f32(ah, bl, dims) + dot_f32(al, bh, dims))


def build_matrix(matrix_ref, index, offsets, rates, rows=32):
    column = lax.broadcasted_iota(jnp.int32, (1, BLOCK), 1)
    local = [
        jnp.broadcast_to(offsets[k : k + 1] + RIM + column, (8, BLOCK)) for k in range(6)
    ]
    rate = [jnp.broadcast_to(rates[k : k + 1], (8, BLOCK)) for k in range(6)]

    def chunk(step, carry):
        base = step * rows
        parts = []
        for part in range(rows // 8):
            row = lax.broadcasted_iota(jnp.int32, (8, BLOCK), 0) + (base + part * 8)
            total = jnp.where(row == local[0], rate[0], 0.0)
            for k in range(1, 6):
                total = total + jnp.where(row == local[k], rate[k], 0.0)
            parts.append(total)
        block = jnp.concatenate(parts, axis=0).astype(jnp.bfloat16)
        matrix_ref[index, pl.ds(pl.multiple_of(base, rows), rows), :] = block
        return carry

    lax.fori_loop(0, WINDOW // rows, chunk, 0)


def forecast_kernel(
    state_ref, left_ref, right_ref, offset_ref, rate_ref, speed_ref, out_ref,
    matrix_ref, field_a, field_b, wide_ref,
):
    rows, cells = state_ref.shape
    own_blocks = cells // BLOCK
    side_blocks = (STEPS - 1) * RIM // BLOCK
    blocks = own_blocks + 2 * side_blocks
    keep, speed = [], []
    for b in range(blocks):
        if b < side_blocks or b >= side_blocks + own_blocks:
            ref = left_ref if b < side_blocks else right_ref
            start = RIM + b * BLOCK if b < side_blocks else (b - side_blocks - own_blocks) * BLOCK
            coef = ref[rows:, start : start + BLOCK].astype(jnp.float32)
            offsets = coef[0:6].astype(jnp.int32)
            rates = coef[6:12]
            total = coef[12:13] + coef[13:14]
            quick = coef[14:15] + coef[15:16]
        else:
            start = (b - side_blocks) * BLOCK
            offsets = offset_ref[:, start : start + BLOCK]
            rates = rate_ref[:, start : start + BLOCK]
            total = jnp.sum(rates, axis=0, keepdims=True)
            quick = speed_ref[:, start : start + BLOCK]
        build_matrix(matrix_ref, b, offsets, rates)
        keep.append(1.0 - total)
        speed.append(quick)
    field_a[:, :HALO] = left_ref[:rows]
    field_a[:, HALO : HALO + cells] = state_ref[...].astype(jnp.bfloat16)
    field_a[:, HALO + cells :] = right_ref[:rows]
    source, target = field_a, field_b
    for step in range(STEPS):
        for b in range(step, blocks - step):
            first = b * BLOCK
            middle = slice(first + RIM, first + RIM + BLOCK)
            summed = dot_f32(source[:, first : first + WINDOW], matrix_ref[b])
            if step > 0:
                centre = wide_ref[:, middle]
            elif side_blocks <= b < side_blocks + own_blocks:
                own = (b - side_blocks) * BLOCK
                centre = state_ref[:, own : own + BLOCK]
            else:
                centre = source[:, middle].astype(jnp.float32)
            blended = centre * keep[b] + summed
            result = blended + speed[b] * jnp.tanh(blended)
            if step < STEPS - 1:
                wide_ref[:, middle] = result
                target[:, middle] = result.astype(jnp.bfloat16)
            else:
                patch = (first + RIM - HALO) // PATCH_CELLS
                for half in range(BLOCK // PATCH_CELLS):
                    piece = result[:, half * PATCH_CELLS : (half + 1) * PATCH_CELLS]
                    out_ref[patch + half] = piece.astype(jnp.bfloat16)
        source, target = target, source


def forecast(state, left, right, offsets, rates, speed):
    rows, cells = state.shape
    blocks = (cells + 2 * (STEPS - 1) * RIM) // BLOCK
    padded = cells + 2 * HALO
    return pl.pallas_call(
        forecast_kernel,
        out_shape=jax.ShapeDtypeStruct((cells // PATCH_CELLS, rows, PATCH_CELLS), jnp.bfloat16),
        in_specs=[pl.BlockSpec(memory_space=pltpu.VMEM)] * 6,
        out_specs=pl.BlockSpec(memory_space=pltpu.VMEM),
        scratch_shapes=[
            pltpu.VMEM((blocks, WINDOW, BLOCK), jnp.bfloat16),
            pltpu.VMEM((rows, padded), jnp.bfloat16),
            pltpu.VMEM((rows, padded), jnp.bfloat16),
            pltpu.VMEM((rows, padded), jnp.float32),
        ],
        name="forecast",
    )(state, left, right, offsets, rates, speed)


def analysis_kernel(x_ref, message_ref, out_ref, wide_ref, x2_ref, select_ref):
    members = x_ref.shape[0] // LEVELS
    span = LEVELS * PATCH_CELLS
    wide_ref[...] = x_ref[...].astype(jnp.float32)
    for level in range(LEVELS):
        part = wide_ref[pl.ds(level, members, stride=LEVELS), :]
        x2_ref[:, level * PATCH_CELLS : (level + 1) * PATCH_CELLS] = part.astype(jnp.bfloat16)
    location = jnp.concatenate([message_ref[0:1], message_ref[3:4]], axis=1) - 1.0
    value = jnp.concatenate([message_ref[1:2], message_ref[4:5]], axis=1)
    weight = jnp.concatenate([message_ref[2:3], message_ref[5:6]], axis=1)
    slots = location.shape[1]
    location = location.astype(jnp.int32)
    for first in range(0, span, PATCH_CELLS):
        row = lax.broadcasted_iota(jnp.int32, (PATCH_CELLS, slots), 0) + first
        hot = jnp.where(row == location, 1.0, 0.0)
        select_ref[first : first + PATCH_CELLS, :] = hot.astype(jnp.bfloat16)
    seen = dot_f32(x2_ref[...], select_ref[...])
    seen_mean = jnp.sum(seen, axis=0, keepdims=True) * (1.0 / members)
    rooted = jnp.sqrt(weight)
    spread = 1.0 / math.sqrt(members - 1.0)
    scaled = (seen - seen_mean) * (rooted * spread)
    row = lax.broadcasted_iota(jnp.int32, (members, members), 0)
    column = lax.broadcasted_iota(jnp.int32, (members, members), 1)
    diagonal = jnp.where(row == column, 1.0, 0.0)
    system = diagonal + dot_split(scaled, scaled, (((1,), (1,)), ((), ())))
    square = jnp.sum(jnp.sum(system * system, axis=0, keepdims=True), axis=1, keepdims=True)
    inverse_scale = lax.rsqrt(square)
    innovation = rooted * (value - seen_mean) * spread
    forcing = jnp.sum(scaled * innovation, axis=1, keepdims=True)
    iterate = system * inverse_scale
    factor = 1.5 * diagonal - 0.5 * iterate
    inverse_root = factor
    iterate = dot_split(iterate, factor)
    for sweep in range(1, NS_ITERS):
        factor = 1.5 * diagonal - 0.5 * dot_split(inverse_root, iterate)
        if sweep < NS_ITERS - 1:
            iterate = dot_split(iterate, factor)
        inverse_root = dot_split(factor, inverse_root)
    inner = jnp.sum(inverse_root * forcing, axis=0, keepdims=True)
    shift = jnp.sum(inverse_root * inner, axis=1, keepdims=True) * inverse_scale
    transform = (inverse_root * jnp.sqrt(inverse_scale)).astype(jnp.bfloat16)
    for level in range(LEVELS):
        part = x2_ref[:, level * PATCH_CELLS : (level + 1) * PATCH_CELLS].astype(jnp.float32)
        mean = jnp.sum(part, axis=0, keepdims=True) * (1.0 / members)
        anomaly = part - mean
        moved = mean + jnp.sum(anomaly * shift, axis=0, keepdims=True)
        updated = moved + dot_f32(transform, anomaly.astype(jnp.bfloat16), (((0,), (0,)), ((), ())))
        wide_ref[pl.ds(level, members, stride=LEVELS), :] = updated
    out_ref[...] = wide_ref[...].astype(jnp.bfloat16)


def analysis(x, message):
    rows = x.shape[0]
    members = rows // LEVELS
    slots = 2 * message.shape[1]
    return pl.pallas_call(
        analysis_kernel,
        out_shape=jax.ShapeDtypeStruct(x.shape, jnp.bfloat16),
        in_specs=[pl.BlockSpec(memory_space=pltpu.VMEM)] * 2,
        out_specs=pl.BlockSpec(memory_space=pltpu.VMEM),
        scratch_shapes=[
            pltpu.VMEM((rows, PATCH_CELLS), jnp.float32),
            pltpu.VMEM((members, LEVELS * PATCH_CELLS), jnp.bfloat16),
            pltpu.VMEM((LEVELS * PATCH_CELLS, slots), jnp.bfloat16),
        ],
        name="analysis",
    )(x, message)


def observation_message(groups, regions, obs_patch, obs_row, obs_value, obs_error):
    devices = groups * regions
    target = jnp.arange(devices, dtype=jnp.int32)
    wanted = target % regions * groups + target // regions
    before = jnp.arange(obs_patch.shape[0], dtype=jnp.int32)
    earlier = (obs_patch[:, None] == obs_patch[None, :]) & (before[:, None] < before[None, :])
    rank = jnp.sum(earlier.astype(jnp.int32), axis=0)
    hit = obs_patch[None, :] == wanted[:, None]
    fields = jnp.stack([(obs_row + 1).astype(jnp.float32), obs_value, 1.0 / (obs_error * obs_error)])
    parts = []
    for slot in range(2):
        chosen = (hit & (rank[None, :] == slot)).astype(jnp.float32)
        parts.append(
            lax.dot_general(
                chosen, fields, (((1,), (1,)), ((), ())), precision=lax.Precision.HIGHEST
            )
        )
    return jnp.concatenate(parts + [jnp.zeros((devices, 2), jnp.float32)], axis=1)


def on_device(
    state, adjacent_columns, adjacent_rates, amplification_speed,
    obs_patch, obs_row, obs_value, obs_error,
):
    members, levels, cells = state.shape
    regions = lax.axis_size("region")
    groups = lax.axis_size("member")
    total = cells * regions
    first = lax.axis_index("region") * cells
    cell_index = first + jnp.arange(cells, dtype=jnp.int32)
    offsets = (adjacent_columns - cell_index[None, :] + total // 2) % total - total // 2
    flat = state.reshape(members * levels, cells)
    rate_sum = jnp.sum(adjacent_rates, axis=0, keepdims=True)
    speed = amplification_speed[None, :]
    sides = []
    for part in (slice(cells - HALO, cells), slice(0, HALO)):
        sides.append(
            jnp.concatenate(
                [
                    flat[:, part].astype(jnp.bfloat16),
                    offsets[:, part].astype(jnp.bfloat16),
                    adjacent_rates[:, part].astype(jnp.bfloat16),
                    high(rate_sum[:, part]),
                    low(rate_sum[:, part]),
                    high(speed[:, part]),
                    low(speed[:, part]),
                ],
                axis=0,
            )
        )
    up = [(i, (i + 1) % regions) for i in range(regions)]
    left = lax.ppermute(sides[0], "region", up)
    right = lax.ppermute(sides[1], "region", [(j, i) for i, j in up])
    message = observation_message(groups, regions, obs_patch, obs_row, obs_value, obs_error)
    message = lax.all_to_all(message, ("member", "region"), 0, 0, tiled=True)
    rounded = forecast(flat, left, right, offsets, adjacent_rates, speed)
    patched = lax.all_to_all(rounded, "member", 0, 0, tiled=True)
    analysed = analysis(patched.reshape(-1, PATCH_CELLS), message.T)
    returned = analysed.reshape(groups, members * levels, PATCH_CELLS)
    back = lax.all_to_all(returned, "member", 0, 0, tiled=True)
    return back.transpose(1, 0, 2).reshape(members, levels, cells)


def solution(mesh):
    placed = (
        P("member", None, "region"),
        P(None, "region"),
        P(None, "region"),
        P("region"),
        P(("member", "region")),
        P(("member", "region")),
        P(("member", "region")),
        P(("member", "region")),
    )
    return jax.shard_map(
        on_device, mesh=mesh, in_specs=placed, out_specs=P("member", None, "region"), check_vma=False
    )
```

profile of v0, /device:TPU:1, one launch (start us, length us, event | category | flops | bytes accessed | tf_op | source)
XLA Modules:
  0.0 69.3 jit_solution(14209396947687432636)
XLA Ops:
  0.0 0.8 %fusion.18 = (f32[1024]{0:T(1024)S(1)}, bf16[6,1024]{1,0:T(8,128)(2,1)S(1)}) fusion(f32[6,1024]{1,0:T(8,128)} %rate_ref.1), kind=kLoop, calls=%fused_computation.45 | loop fusion | flops 11264 | bytes 40960 | tf_op jit(solution)/shard_map/reduce_sum | solution.py:238
  0.8 0.0 copy-start.3
  0.9 0.7 copy-done.3
  1.6 1.3 %bitcast_convert_fusion = bf16[256,1024]{1,0:T(8,128)(2,1)S(1)} fusion(f32[32,8,1024]{2,1,0:T(8,128)} %param.8), kind=kLoop, calls=%fused_computation.42 | loop fusion | flops 262144 | bytes 1572864 | tf_op jit(solution)/shard_map/convert.5
  2.9 0.0 copy-start.4
  2.9 0.1 fusion.17
  3.0 0.7 copy-done.4
  3.6 0.6 fusion.15
  4.3 0.3 concatenate.9
  4.5 2.5 %collective-permute-start = (bf16[272,768]{1,0:T(8,128)(2,1)S(1)}, bf16[272,768]{1,0:T(8,128)(2,1)S(1)}, u32[]{:S(2)}, u32[]{:S(2)}) collective-permute-start(bf16[272,768]{1,0:T(8,128)(2,1)S(1)} %concatenate.9), channel_id=1, source_target_pairs={{0,1},{1,2},{2,3},{3,4},{4,5},{5,6},{6,7},{7,8},{8,9},{9,10},{10,1... | collective-permute-start | bytes 1253384 | tf_op jit(solution)/shard_map/ppermute | solution.py:257
  7.1 0.3 concatenate.10
  7.3 0.0 copy-start.5
  7.3 4.4 %collective-permute-start.1 = (bf16[272,768]{1,0:T(8,128)(2,1)S(1)}, bf16[272,768]{1,0:T(8,128)(2,1)S(1)}, u32[]{:S(2)}, u32[]{:S(2)}) collective-permute-start(bf16[272,768]{1,0:T(8,128)(2,1)S(1)} %concatenate.10), channel_id=1, source_target_pairs={{1,0},{2,1},{3,2},{4,3},{5,4},{6,5},{7,6},{8,7},{9,8},{10,9},{11,1... | collective-permute-start | bytes 1253384 | tf_op jit(solution)/shard_map/ppermute | solution.py:258
  11.7 0.0 copy-done.5
  11.7 0.1 convert_reduce_fusion
  11.9 0.0 copy-start.6
  11.9 0.7 copy-done.6
  12.5 0.0 copy-start.7
  12.6 0.7 copy-done.7
  13.2 0.1 pad.2.clone
  13.3 0.0 copy-start.8
  13.3 0.7 copy-done.8
  14.0 0.2 fusion.2
  14.2 0.3 fusion.1
  14.4 0.1 maximum_bitcast_fusion
  14.5 0.8 %copy.13 = f32[128,1,8]{2,1,0:T(1,128)} copy(f32[128,1,8]{0,2,1:T(8,128)S(1)} %maximum_bitcast_fusion) | data formatting | bytes 8192 | tf_op jit(solution)/shard_map/all_to_all | solution.py:260
  15.3 6.7 %all-to-all-start.1 = ((f32[128,1,8]{2,1,0:T(1,128)}), f32[128,1,8]{2,1,0:T(1,128)S(1)}, u32[]{:S(2)}, u32[]{:S(2)}) async-start(f32[128,1,8]{2,1,0:T(1,128)} %copy.13), calls=%async_computation.1 | async-start | bytes 131072 | tf_op jit(solution)/shard_map/all_to_all | solution.py:260
  22.1 0.0 collective-permute-done.left_ref
  22.1 0.0 copy-start.1
  22.1 0.0 collective-permute-done.1.right_ref
  22.1 0.0 copy-start.2
  22.1 0.7 %copy-done.1 = bf16[272,768]{1,0:T(8,128)(2,1)} copy-done((bf16[272,768]{1,0:T(8,128)(2,1)}, bf16[272,768]{1,0:T(8,128)(2,1)S(1)}, u32[]{:S(2)}) %copy-start.1) | copy-done | bytes 417816
  22.8 0.2 copy-done.2
  23.0 9.2 %forecast.1 = bf16[8,256,128]{2,1,0:T(8,128)(2,1)} custom-call(f32[256,1024]{1,0:T(8,128)} %bitcast.15, bf16[272,768]{1,0:T(8,128)(2,1)} %copy-done.1, bf16[272,768]{1,0:T(8,128)(2,1)} %copy-done.2, s32[6,1024]{1,0:T(8,128)} %get-tuple-element.6.offset_ref, f32[6,1024]{1,0:T(8,128)} %rate_ref.1, f32[1,1024]{1,0:T(1,128)} %bitcast.19), custom_call_target="tpu_custom_call" | custom-call | tf_op jit(solution)/shard_map/forecast/pallas_call | solution.py:122
  32.2 0.0 all-to-all-done.1
  32.2 4.8 %all-to-all-start = ((bf16[8,256,128]{2,1,0:T(8,128)(2,1)}), bf16[8,256,128]{2,1,0:T(8,128)(2,1)S(1)}, u32[]{:S(2)}, u32[]{:S(2)}) async-start(bf16[8,256,128]{2,1,0:T(8,128)(2,1)} %forecast.1), calls=%async_computation | async-start | bytes 1048576 | tf_op jit(solution)/shard_map/all_to_all | solution.py:262
  37.0 0.7 copy.14
  37.6 8.7 %all-to-all-done = bf16[8,256,128]{2,1,0:T(8,128)(2,1)S(1)} async-done(((bf16[8,256,128]{2,1,0:T(8,128)(2,1)}), bf16[8,256,128]{2,1,0:T(8,128)(2,1)S(1)}, u32[]{:S(2)}, u32[]{:S(2)}) %all-to-all-start) | async-done | bytes 524320 | tf_op jit(solution)/shard_map/all_to_all | solution.py:262
  46.3 0.0 copy-start
  46.3 0.8 %copy-done = bf16[8,256,128]{2,1,0:T(8,128)(2,1)} copy-done((bf16[8,256,128]{2,1,0:T(8,128)(2,1)}, bf16[8,256,128]{2,1,0:T(8,128)(2,1)S(1)}, u32[]{:S(2)}) %copy-start) | copy-done | bytes 524312
  47.1 7.1 %analysis.1 = bf16[2048,128]{1,0:T(8,128)(2,1)} custom-call(bf16[2048,128]{1,0:T(8,128)(2,1)} %bitcast.16, f32[8,128]{1,0:T(8,128)} %bitcast.24), custom_call_target="tpu_custom_call" | custom-call | tf_op jit(solution)/shard_map/analysis/pallas_call | solution.py:192
  54.2 13.7 %all_to_all.22 = bf16[8,256,128]{2,1,0:T(8,128)(2,1)S(1)} all-to-all(bf16[8,256,128]{2,1,0:T(8,128)(2,1)} %bitcast.17), channel_id=1, replica_groups=mesh['member'=8,'region'=16] {'member'}, dimensions={0} | all-to-all | bytes 1048576 | tf_op jit(solution)/shard_map/all_to_all | solution.py:265
  67.9 0.3 copy.15
  68.3 1.0 %reshape.53 = bf16[32,8,1024]{2,1,0:T(8,128)(2,1)} reshape(bf16[256,8,128]{2,1,0:T(8,128)(2,1)S(1)} %copy.15) | data formatting | bytes 1048576 | tf_op jit(solution)/shard_map/reshape | solution.py:266
  (9 shorter events, 0.0 us)
Async XLA Ops:
  0.8 0.7 copy-start.3
  2.9 0.8 %copy-start.4 = (s32[6,1024]{1,0:T(8,128)S(1)}, s32[6,1024]{1,0:T(8,128)}, u32[]{:S(2)}) copy-start(s32[6,1024]{1,0:T(8,128)} %param.9) | copy-start | bytes 73732
  4.5 17.5 %collective-permute-start = (bf16[272,768]{1,0:T(8,128)(2,1)S(1)}, bf16[272,768]{1,0:T(8,128)(2,1)S(1)}, u32[]{:S(2)}, u32[]{:S(2)}) collective-permute-start(bf16[272,768]{1,0:T(8,128)(2,1)S(1)} %concatenate.9), channel_id=1, source_target_pairs={{0,1},{1,2},{2,3},{3,4},{4,5},{5,6},{6,7},{7,8},{8,9},{9,10},{10,1... | collective-permute-start | bytes 1253384 | tf_op jit(solution)/shard_map/ppermute | solution.py:257
  7.3 4.4 %copy-start.5 = (s32[256]{0:T(256)S(1)}, s32[256]{0:T(256)}, u32[]{:S(2)}) copy-start(s32[256]{0:T(256)} %param.12) | copy-start | bytes 3076
  7.3 14.8 %collective-permute-start.1 = (bf16[272,768]{1,0:T(8,128)(2,1)S(1)}, bf16[272,768]{1,0:T(8,128)(2,1)S(1)}, u32[]{:S(2)}, u32[]{:S(2)}) collective-permute-start(bf16[272,768]{1,0:T(8,128)(2,1)S(1)} %concatenate.10), channel_id=1, source_target_pairs={{1,0},{2,1},{3,2},{4,3},{5,4},{6,5},{7,6},{8,7},{9,8},{10,9},{11,1... | collective-permute-start | bytes 1253384 | tf_op jit(solution)/shard_map/ppermute | solution.py:258
  11.9 0.7 copy-start.6
  12.5 0.7 copy-start.7
  13.3 0.7 copy-start.8
  15.3 16.9 %all-to-all-start.1 = ((f32[128,1,8]{2,1,0:T(1,128)}), f32[128,1,8]{2,1,0:T(1,128)S(1)}, u32[]{:S(2)}, u32[]{:S(2)}) async-start(f32[128,1,8]{2,1,0:T(1,128)} %copy.13), calls=%async_computation.1 | async-start | bytes 131072 | tf_op jit(solution)/shard_map/all_to_all | solution.py:260
  22.1 0.8 %copy-start.1 = (bf16[272,768]{1,0:T(8,128)(2,1)}, bf16[272,768]{1,0:T(8,128)(2,1)S(1)}, u32[]{:S(2)}) copy-start(bf16[272,768]{1,0:T(8,128)(2,1)S(1)} %collective-permute-done.left_ref) | copy-start | bytes 1253380
  22.1 0.9 %copy-start.2 = (bf16[272,768]{1,0:T(8,128)(2,1)}, bf16[272,768]{1,0:T(8,128)(2,1)S(1)}, u32[]{:S(2)}) copy-start(bf16[272,768]{1,0:T(8,128)(2,1)S(1)} %collective-permute-done.1.right_ref) | copy-start | bytes 1253380
  32.2 14.2 %all-to-all-start = ((bf16[8,256,128]{2,1,0:T(8,128)(2,1)}), bf16[8,256,128]{2,1,0:T(8,128)(2,1)S(1)}, u32[]{:S(2)}, u32[]{:S(2)}) async-start(bf16[8,256,128]{2,1,0:T(8,128)(2,1)} %forecast.1), calls=%async_computation | async-start | bytes 1048576 | tf_op jit(solution)/shard_map/all_to_all | solution.py:262
  46.3 0.8 %copy-start = (bf16[8,256,128]{2,1,0:T(8,128)(2,1)}, bf16[8,256,128]{2,1,0:T(8,128)(2,1)S(1)}, u32[]{:S(2)}) copy-start(bf16[8,256,128]{2,1,0:T(8,128)(2,1)S(1)} %all-to-all-done) | copy-start | bytes 1572868
where the time goes:
time: 69.9 us; the launch traced here: 69.3 us
  starting transfers between devices  18.5 us (26%)
  Pallas kernels  16.3 us (23%)
  blocking collectives  13.7 us (20%)
  waiting for transfers between devices  8.7 us (12%)
  local copies, waits for them, and re-layouts  8.51 us (12%)
  other arithmetic  3.02 us (4%)
    all_to_all x1, blocking collectives, on_device(): back = lax.all_to_all(returned, 'member', 0, 0, tiled=True)  13.7 us
    pallas_call x1, Pallas kernels, forecast(): pl.pallas_call(forecast_kernel, out_shape=jax.ShapeDtypeStruct((cells //...  9.19 us
    all_to_all x1, waiting for transfers between devices, on_device(): patched = lax.all_to_all(rounded, 'member', 0, 0, tiled=True)  8.69 us
    pallas_call x1, Pallas kernels, analysis(): pl.pallas_call(analysis_kernel, out_shape=jax.ShapeDtypeStruct(x.shape, j...  7.09 us
    all_to_all x1, starting transfers between devices, on_device(): message = lax.all_to_all(message, ('member', 'region'), 0, 0, tiled=True)  6.75 us
    unnamed x18, local copies, waits for them, and re-layouts  5.06 us
    all_to_all x1, starting transfers between devices, on_device(): patched = lax.all_to_all(rounded, 'member', 0, 0, tiled=True)  4.82 us
    ppermute x1, starting transfers between devices, on_device(): right = lax.ppermute(sides[1], 'region', [(j, i) for i, j in up])  4.41 us
  transfers between devices with their start and end apart: 4, of which 1 were waited for; matrix products, arithmetic and copies ran while one was open for 4% of the time, Pallas kernels for 13%

commit v1 on v0

v1 whole, which is shorter than its diff:
```python
import functools
import math

import jax
import jax.numpy as jnp
from jax import lax
from jax.experimental import pallas as pl
from jax.experimental.pallas import tpu as pltpu
from jax.sharding import PartitionSpec as P

PATCH_CELLS = 128
RIM = 256
STEPS = 3
NS_ITERS = 6
LEVELS = 8
BLOCK = 256
WINDOW = BLOCK + 2 * RIM
HALO = STEPS * RIM
COEF_ROWS = 16
TILE = 128


def high(value):
    return value.astype(jnp.bfloat16)


def low(value):
    return (value - high(value).astype(jnp.float32)).astype(jnp.bfloat16)


def dot_f32(a, b, dims=(((1,), (0,)), ((), ()))):
    return lax.dot_general(a, b, dims, preferred_element_type=jnp.float32)


def dot_split(a, b, dims=(((1,), (0,)), ((), ()))):
    ah, al, bh, bl = high(a), low(a), high(b), low(b)
    return dot_f32(ah, bh, dims) + (dot_f32(ah, bl, dims) + dot_f32(al, bh, dims))


def cell_offsets(columns, first, total):
    cell = first + lax.broadcasted_iota(jnp.int32, columns.shape, 1)
    offset = columns - cell
    offset = jnp.where(offset > total // 2, offset - total, offset)
    return jnp.where(offset < -(total // 2), offset + total, offset)


def build_matrix(matrix_ref, index, offsets, rates):
    zero = jnp.zeros((TILE, TILE), jnp.bfloat16)
    row = lax.broadcasted_iota(jnp.int32, (TILE, TILE), 0).astype(jnp.float32)
    row = row.astype(jnp.bfloat16)
    lane = lax.broadcasted_iota(jnp.int32, (1, TILE), 1).astype(jnp.float32)
    reach = (TILE + 2 * RIM) // TILE
    for part in range(BLOCK // TILE):
        lanes = slice(part * TILE, (part + 1) * TILE)
        local = offsets[:, lanes] + (lane + float(RIM))
        rate = [
            jnp.broadcast_to(rates[k : k + 1, lanes].astype(jnp.bfloat16), (TILE, TILE))
            for k in range(6)
        ]
        for tile in range(WINDOW // TILE):
            rows = slice(tile * TILE, (tile + 1) * TILE)
            step = tile - part
            if step < 0 or step >= reach:
                matrix_ref[index, rows, lanes] = zero
                continue
            total = None
            for k in range(6):
                near = (local[k : k + 1] - float(step * TILE)).astype(jnp.bfloat16)
                hit = row == jnp.broadcast_to(near, (TILE, TILE))
                term = jnp.where(hit, rate[k], zero)
                total = term if total is None else total + term
            matrix_ref[index, rows, lanes] = total


def prepare_kernel(first_ref, state_ref, column_ref, rate_ref, speed_ref, up_ref, down_ref, *, total):
    rows, cells = state_ref.shape
    offsets = cell_offsets(column_ref[...], first_ref[0], total).astype(jnp.float32)
    rates = rate_ref[...]
    rate_sum = jnp.sum(rates, axis=0, keepdims=True)
    speed = speed_ref[...]
    coef = jnp.concatenate(
        [
            offsets,
            rates,
            high(rate_sum).astype(jnp.float32),
            low(rate_sum).astype(jnp.float32),
            high(speed).astype(jnp.float32),
            low(speed).astype(jnp.float32),
        ],
        axis=0,
    ).astype(jnp.bfloat16)
    for ref, begin in ((up_ref, cells - HALO), (down_ref, 0)):
        ref[:rows] = state_ref[:, begin : begin + HALO].astype(jnp.bfloat16)
        ref[rows:] = coef[:, begin : begin + HALO]


def vmem(count):
    return [pl.BlockSpec(memory_space=pltpu.VMEM)] * count


def prepare(first, state, columns, rates, speed, total):
    rows, cells = state.shape
    side = jax.ShapeDtypeStruct((rows + COEF_ROWS, HALO), jnp.bfloat16)
    return pl.pallas_call(
        functools.partial(prepare_kernel, total=total),
        out_shape=(side, side),
        in_specs=[pl.BlockSpec(memory_space=pltpu.SMEM)] + vmem(4),
        out_specs=tuple(vmem(2)),
        compiler_params=pltpu.CompilerParams(vmem_limit_bytes=8 << 20),
        name="prepare",
    )(first, state, columns, rates, speed)


def local_kernel(
    first_ref, column_ref, rate_ref, patch_ref, row_ref, value_ref, error_ref,
    matrix_ref, message_ref, *, total, regions, groups,
):
    cells = column_ref.shape[1]
    offsets = cell_offsets(column_ref[...], first_ref[0], total).astype(jnp.float32)
    rates = rate_ref[...]
    for b in range(cells // BLOCK):
        part = slice(b * BLOCK, (b + 1) * BLOCK)
        build_matrix(matrix_ref, b, offsets[:, part], rates[:, part])
    devices, count = message_ref.shape[0], patch_ref.shape[1]
    target = lax.broadcasted_iota(jnp.int32, (devices, count), 0)
    wanted = target % regions * groups + target // regions
    hit = jnp.where(patch_ref[...] == wanted, 1.0, 0.0)
    before = lax.broadcasted_iota(jnp.int32, (count, count), 0)
    after = lax.broadcasted_iota(jnp.int32, (count, count), 1)
    earlier = jnp.where(before < after, 1.0, 0.0).astype(jnp.bfloat16)
    rank = dot_f32(hit.astype(jnp.bfloat16), earlier)
    field = lax.broadcasted_iota(jnp.int32, (message_ref.shape[1], count), 0)
    location = row_ref[...].astype(jnp.float32) + 1.0
    weight = 1.0 / (error_ref[...] * error_ref[...])
    message = None
    for slot in range(2):
        chosen = jnp.where(rank == float(slot), hit, 0.0).astype(jnp.bfloat16)
        values = jnp.zeros(field.shape, jnp.float32)
        for k, item in enumerate((location, value_ref[...], weight)):
            values = jnp.where(field == 3 * slot + k, item, values)
        for _ in range(3):
            piece = high(values)
            values = values - piece.astype(jnp.float32)
            term = dot_f32(chosen, piece, (((1,), (1,)), ((), ())))
            message = term if message is None else message + term
    message_ref[...] = message


def local_work(first, columns, rates, patch, row, value, error, total, regions, groups):
    cells = columns.shape[1]
    return pl.pallas_call(
        functools.partial(local_kernel, total=total, regions=regions, groups=groups),
        out_shape=(
            jax.ShapeDtypeStruct((cells // BLOCK, WINDOW, BLOCK), jnp.bfloat16),
            jax.ShapeDtypeStruct((regions * groups, TILE), jnp.float32),
        ),
        in_specs=[pl.BlockSpec(memory_space=pltpu.SMEM)] + vmem(6),
        out_specs=tuple(vmem(2)),
        compiler_params=pltpu.CompilerParams(vmem_limit_bytes=8 << 20),
        name="local_work",
    )(first, columns, rates, patch, row, value, error)


def forecast_kernel(
    state_ref, left_ref, right_ref, own_ref, rate_ref, speed_ref, out_ref,
    matrix_ref, field_a, field_b, wide_ref,
):
    rows, cells = state_ref.shape
    own_blocks = cells // BLOCK
    side_blocks = (STEPS - 1) * RIM // BLOCK
    blocks = own_blocks + 2 * side_blocks
    keep, speed, matrices = [], [], []
    for b in range(blocks):
        if b < side_blocks or b >= side_blocks + own_blocks:
            ref = left_ref if b < side_blocks else right_ref
            start = RIM + b * BLOCK if b < side_blocks else (b - side_blocks - own_blocks) * BLOCK
            index = b if b < side_blocks else b - own_blocks
            coef = ref[rows:, start : start + BLOCK].astype(jnp.float32)
            build_matrix(matrix_ref, index, coef[0:6], coef[6:12])
            total = coef[12:13] + coef[13:14]
            quick = coef[14:15] + coef[15:16]
            matrices.append((matrix_ref, index))
        else:
            start = (b - side_blocks) * BLOCK
            total = jnp.sum(rate_ref[:, start : start + BLOCK], axis=0, keepdims=True)
            quick = speed_ref[:, start : start + BLOCK]
            matrices.append((own_ref, b - side_blocks))
        keep.append(1.0 - total)
        speed.append(quick)
    field_a[:, :HALO] = left_ref[:rows]
    field_a[:, HALO : HALO + cells] = state_ref[...].astype(jnp.bfloat16)
    field_a[:, HALO + cells :] = right_ref[:rows]
    source, target = field_a, field_b
    for step in range(STEPS):
        for b in range(step, blocks - step):
            first = b * BLOCK
            middle = slice(first + RIM, first + RIM + BLOCK)
            holder, index = matrices[b]
            summed = dot_f32(source[:, first : first + WINDOW], holder[index])
            if step > 0:
                centre = wide_ref[:, middle]
            elif side_blocks <= b < side_blocks + own_blocks:
                own = (b - side_blocks) * BLOCK
                centre = state_ref[:, own : own + BLOCK]
            else:
                centre = source[:, middle].astype(jnp.float32)
            blended = centre * keep[b] + summed
            result = blended + speed[b] * jnp.tanh(blended)
            if step < STEPS - 1:
                wide_ref[:, middle] = result
                target[:, middle] = result.astype(jnp.bfloat16)
            else:
                patch = (first + RIM - HALO) // PATCH_CELLS
                for half in range(BLOCK // PATCH_CELLS):
                    piece = result[:, half * PATCH_CELLS : (half + 1) * PATCH_CELLS]
                    out_ref[patch + half] = piece.astype(jnp.bfloat16)
        source, target = target, source


def forecast(state, left, right, own, rates, speed):
    rows, cells = state.shape
    sides = 2 * (STEPS - 1) * RIM // BLOCK
    padded = cells + 2 * HALO
    return pl.pallas_call(
        forecast_kernel,
        out_shape=jax.ShapeDtypeStruct((cells // PATCH_CELLS, rows, PATCH_CELLS), jnp.bfloat16),
        in_specs=vmem(6),
        out_specs=pl.BlockSpec(memory_space=pltpu.VMEM),
        scratch_shapes=[
            pltpu.VMEM((sides, WINDOW, BLOCK), jnp.bfloat16),
            pltpu.VMEM((rows, padded), jnp.bfloat16),
            pltpu.VMEM((rows, padded), jnp.bfloat16),
            pltpu.VMEM((rows, padded), jnp.float32),
        ],
        compiler_params=pltpu.CompilerParams(vmem_limit_bytes=20 << 20),
        name="forecast",
    )(state, left, right, own, rates, speed)


def analysis_kernel(x_ref, message_ref, out_ref, wide_ref, x2_ref, select_ref):
    members = x_ref.shape[0] // LEVELS
    span = LEVELS * PATCH_CELLS
    wide_ref[...] = x_ref[...].astype(jnp.float32)
    for level in range(LEVELS):
        part = wide_ref[pl.ds(level, members, stride=LEVELS), :]
        x2_ref[:, level * PATCH_CELLS : (level + 1) * PATCH_CELLS] = part.astype(jnp.bfloat16)
    message = jnp.transpose(message_ref[...])
    location = jnp.concatenate([message[0:1], message[3:4]], axis=1) - 1.0
    value = jnp.concatenate([message[1:2], message[4:5]], axis=1)
    weight = jnp.concatenate([message[2:3], message[5:6]], axis=1)
    slots = location.shape[1]
    location = location.astype(jnp.int32)
    for first in range(0, span, PATCH_CELLS):
        row = lax.broadcasted_iota(jnp.int32, (PATCH_CELLS, slots), 0) + first
        hot = jnp.where(row == location, 1.0, 0.0)
        select_ref[first : first + PATCH_CELLS, :] = hot.astype(jnp.bfloat16)
    seen = dot_f32(x2_ref[...], select_ref[...])
    seen_mean = jnp.sum(seen, axis=0, keepdims=True) * (1.0 / members)
    rooted = jnp.sqrt(weight)
    spread = 1.0 / math.sqrt(members - 1.0)
    scaled = (seen - seen_mean) * (rooted * spread)
    row = lax.broadcasted_iota(jnp.int32, (members, members), 0)
    column = lax.broadcasted_iota(jnp.int32, (members, members), 1)
    diagonal = jnp.where(row == column, 1.0, 0.0)
    system = diagonal + dot_split(scaled, scaled, (((1,), (1,)), ((), ())))
    square = jnp.sum(jnp.sum(system * system, axis=0, keepdims=True), axis=1, keepdims=True)
    inverse_scale = lax.rsqrt(square)
    innovation = rooted * (value - seen_mean) * spread
    forcing = jnp.sum(scaled * innovation, axis=1, keepdims=True)
    iterate = system * inverse_scale
    factor = 1.5 * diagonal - 0.5 * iterate
    inverse_root = factor
    iterate = dot_split(iterate, factor)
    for sweep in range(1, NS_ITERS):
        factor = 1.5 * diagonal - 0.5 * dot_split(inverse_root, iterate)
        if sweep < NS_ITERS - 1:
            iterate = dot_split(iterate, factor)
        inverse_root = dot_split(factor, inverse_root)
    inner = jnp.sum(inverse_root * forcing, axis=0, keepdims=True)
    shift = jnp.sum(inverse_root * inner, axis=1, keepdims=True) * inverse_scale
    transform = (inverse_root * jnp.sqrt(inverse_scale)).astype(jnp.bfloat16)
    for level in range(LEVELS):
        part = x2_ref[:, level * PATCH_CELLS : (level + 1) * PATCH_CELLS].astype(jnp.float32)
        mean = jnp.sum(part, axis=0, keepdims=True) * (1.0 / members)
        anomaly = part - mean
        moved = mean + jnp.sum(anomaly * shift, axis=0, keepdims=True)
        updated = moved + dot_f32(transform, anomaly.astype(jnp.bfloat16), (((0,), (0,)), ((), ())))
        wide_ref[pl.ds(level, members, stride=LEVELS), :] = updated
    out_ref[...] = wide_ref[...].astype(jnp.bfloat16)


def analysis(x, message):
    rows = x.shape[0]
    members = rows // LEVELS
    slots = 2 * message.shape[0]
    return pl.pallas_call(
        analysis_kernel,
        out_shape=jax.ShapeDtypeStruct(x.shape, jnp.bfloat16),
        in_specs=vmem(2),
        out_specs=pl.BlockSpec(memory_space=pltpu.VMEM),
        compiler_params=pltpu.CompilerParams(vmem_limit_bytes=12 << 20),
        scratch_shapes=[
            pltpu.VMEM((rows, PATCH_CELLS), jnp.float32),
            pltpu.VMEM((members, LEVELS * PATCH_CELLS), jnp.bfloat16),
            pltpu.VMEM((LEVELS * PATCH_CELLS, slots), jnp.bfloat16),
        ],
        name="analysis",
    )(x, message)


def on_device(
    state, adjacent_columns, adjacent_rates, amplification_speed,
    obs_patch, obs_row, obs_value, obs_error,
):
    members, levels, cells = state.shape
    regions = lax.axis_size("region")
    groups = lax.axis_size("member")
    total = cells * regions
    first = (lax.axis_index("region") * cells).astype(jnp.int32).reshape(1)
    flat = state.reshape(members * levels, cells)
    speed = amplification_speed[None, :]
    sides = prepare(first, flat, adjacent_columns, adjacent_rates, speed, total)
    up = [(i, (i + 1) % regions) for i in range(regions)]
    left = lax.ppermute(sides[0], "region", up)
    right = lax.ppermute(sides[1], "region", [(j, i) for i, j in up])
    own, message = local_work(
        first, adjacent_columns, adjacent_rates, obs_patch[None, :], obs_row[None, :],
        obs_value[None, :], obs_error[None, :], total, regions, groups,
    )
    message = lax.all_to_all(message, ("member", "region"), 0, 0, tiled=True)
    rounded = forecast(flat, left, right, own, adjacent_rates, speed)
    patched = lax.all_to_all(rounded, "member", 0, 0, tiled=True)
    analysed = analysis(patched.reshape(-1, PATCH_CELLS), message)
    returned = analysed.reshape(groups, members * levels, PATCH_CELLS)
    back = lax.all_to_all(returned, "member", 0, 0, tiled=True)
    back = back.reshape(groups, members, levels, PATCH_CELLS)
    return back.transpose(1, 2, 0, 3).reshape(members, levels, cells)


def solution(mesh):
    placed = (
        P("member", None, "region"),
        P(None, "region"),
        P(None, "region"),
        P("region"),
        P(("member", "region")),
        P(("member", "region")),
        P(("member", "region")),
        P(("member", "region")),
    )
    return jax.shard_map(
        on_device, mesh=mesh, in_specs=placed, out_specs=P("member", None, "region"), check_vma=False
    )
```

time: 69.9 us -> 64.5 us (0.923)
  blocking collectives: 13.7 us -> 25.5 us
  waiting for transfers between devices: 8.7 us -> 2.38 us
  starting transfers between devices: 18.5 us -> 13.5 us
  Pallas kernels: 16.3 us -> 12.1 us
  other arithmetic: 3.02 us -> 0 us
  local copies, waits for them, and re-layouts: 8.51 us -> 10.2 us
    all_to_all x0 -> x1, blocking collectives: none -> 12.8 us  [on_device(): patched = lax.all_to_all(rounded, 'member', 0, 0, tiled=True)]
    all_to_all x1 -> x0, waiting for transfers between devices: 8.69 us -> none  [on_device(): patched = lax.all_to_all(rounded, 'member', 0, 0, tiled=True)]
    pallas_call x1, Pallas kernels: 9.19 us -> 3.94 us  [forecast(): pl.pallas_call(forecast_kernel, out_shape=jax.ShapeDtypeStruct((cells //...]
    all_to_all x1 -> x0, starting transfers between devices: 4.82 us -> none  [on_device(): patched = lax.all_to_all(rounded, 'member', 0, 0, tiled=True)]
    unnamed x18 -> x26, local copies, waits for them, and re-layouts: 5.06 us -> 9.34 us
    pallas_call x0 -> x2, Pallas kernels: none -> 2.95 us  [the longest x1 1.96 us: local_work(): pl.pallas_call(functools.partial(local_kernel, total=total, regions=regio...]
    all_to_all x1, waiting for transfers between devices: 0.01 us -> 2.37 us  [on_device(): message = lax.all_to_all(message, ('member', 'region'), 0, 0, tiled=True)]
    another operation x2 -> x0, other arithmetic: 1.92 us -> none
  transfers between devices with their start and end apart: 4 -> 3, of which waited for: 1 -> 1; matrix products, arithmetic and copies ran while one was open for 4% -> 0% of each run, Pallas kernels for 13% -> 9%
where the time goes in v1:
time: 64.5 us; the launch traced here: 63.8 us
  blocking collectives  25.5 us (40%)
  starting transfers between devices  13.5 us (21%)
  Pallas kernels  12.1 us (19%)
  local copies, waits for them, and re-layouts  10.2 us (16%)
  waiting for transfers between devices  2.38 us (4%)
    all_to_all x1, blocking collectives, on_device(): back = lax.all_to_all(returned, 'member', 0, 0, tiled=True)  12.8 us
    all_to_all x1, blocking collectives, on_device(): patched = lax.all_to_all(rounded, 'member', 0, 0, tiled=True)  12.8 us
    unnamed x26, local copies, waits for them, and re-layouts  9.34 us
    all_to_all x1, starting transfers between devices, on_device(): message = lax.all_to_all(message, ('member', 'region'), 0, 0, tiled=True)  6.74 us
    pallas_call x1, Pallas kernels, analysis(): pl.pallas_call(analysis_kernel, out_shape=jax.ShapeDtypeStruct(x.shape, j...  5.25 us
    ppermute x1, starting transfers between devices, on_device(): right = lax.ppermute(sides[1], 'region', [(j, i) for i, j in up])  4.32 us
    pallas_call x1, Pallas kernels, forecast(): pl.pallas_call(forecast_kernel, out_shape=jax.ShapeDtypeStruct((cells //...  3.94 us
    ppermute x1, starting transfers between devices, on_device(): left = lax.ppermute(sides[0], 'region', up)  2.46 us
  transfers between devices with their start and end apart: 3, of which 1 were waited for; matrix products, arithmetic and copies ran while one was open for 0% of the time, Pallas kernels for 9%

profile of v1, /device:TPU:1, one launch (start us, length us, event | category | flops | bytes accessed | tf_op | source)
XLA Modules:
  0.0 63.8 jit_solution(10157547780686093026)
XLA Ops:
  0.0 0.0 copy-start
  0.0 1.2 %copy-done = f32[32,8,1024]{2,1,0:T(8,128)S(1)} copy-done((f32[32,8,1024]{2,1,0:T(8,128)S(1)}, f32[32,8,1024]{2,1,0:T(8,128)}, u32[]{:S(2)}) %copy-start) | copy-done | bytes 1048600
  1.2 0.0 copy-start.4
  1.2 0.8 %copy-done.4 = f32[6,1024]{1,0:T(8,128)S(1)} copy-done((f32[6,1024]{1,0:T(8,128)S(1)}, f32[6,1024]{1,0:T(8,128)}, u32[]{:S(2)}) %copy-start.4) | copy-done | bytes 24600
  2.0 0.0 copy-start.6
  2.0 0.8 %copy-done.6 = s32[6,1024]{1,0:T(8,128)S(1)} copy-done((s32[6,1024]{1,0:T(8,128)S(1)}, s32[6,1024]{1,0:T(8,128)}, u32[]{:S(2)}) %copy-start.6) | copy-done | bytes 24600
  2.7 0.0 copy-start.7
  2.7 0.7 %copy-done.7 = f32[1024]{0:T(1024)S(1)} copy-done((f32[1024]{0:T(1024)S(1)}, f32[1024]{0:T(1024)}, u32[]{:S(2)}) %copy-start.7) | copy-done | bytes 4120
  3.4 0.0 copy-start.1
  3.4 1.0 %prepare.1 = (bf16[272,768]{1,0:T(8,128)(2,1)}, bf16[272,768]{1,0:T(8,128)(2,1)}) custom-call(s32[1]{0:T(128)} %bitcast.1.first_ref, f32[256,1024]{1,0:T(8,128)S(1)} %bitcast.20, s32[6,1024]{1,0:T(8,128)S(1)} %copy-done.6, f32[6,1024]{1,0:T(8,128)S(1)} %copy-done.4, f32[1,1024]{1,0:T(1,128)S(1)} %bitcast.25), custom_call_target="tpu_custom_call" | custom-call | tf_op jit(solution)/shard_map/prepare/pallas_call | solution.py:104
  4.4 2.5 %collective-permute-start = (bf16[272,768]{1,0:T(8,128)(2,1)}, bf16[272,768]{1,0:T(8,128)(2,1)S(1)}, u32[]{:S(2)}, u32[]{:S(2)}) collective-permute-start(bf16[272,768]{1,0:T(8,128)(2,1)} %get-tuple-element.9), channel_id=1, source_target_pairs={{0,1},{1,2},{2,3},{3,4},{4,5},{5,6},{6,7},{7,8},{8,9},{9,10},{10,1... | collective-permute-start | bytes 1253384 | tf_op jit(solution)/shard_map/ppermute | solution.py:324
  6.9 4.3 %collective-permute-start.1 = (bf16[272,768]{1,0:T(8,128)(2,1)}, bf16[272,768]{1,0:T(8,128)(2,1)}, u32[]{:S(2)}, u32[]{:S(2)}) collective-permute-start(bf16[272,768]{1,0:T(8,128)(2,1)} %get-tuple-element.10), channel_id=1, source_target_pairs={{1,0},{2,1},{3,2},{4,3},{5,4},{6,5},{7,6},{8,7},{9,8},{10,9},{11,1... | collective-permute-start | bytes 1253384 | tf_op jit(solution)/shard_map/ppermute | solution.py:325
  11.2 0.0 copy-start.9
  11.2 0.7 %copy-done.9 = s32[256]{0:T(256)S(1)} copy-done((s32[256]{0:T(256)S(1)}, s32[256]{0:T(256)}, u32[]{:S(2)}) %copy-start.9) | copy-done | bytes 1048
  11.9 0.0 copy-start.10
  11.9 0.7 %copy-done.10 = s32[256]{0:T(256)S(1)} copy-done((s32[256]{0:T(256)S(1)}, s32[256]{0:T(256)}, u32[]{:S(2)}) %copy-start.10) | copy-done | bytes 1048
  12.6 0.0 copy-start.11
  12.6 0.7 %copy-done.11 = f32[256]{0:T(256)S(1)} copy-done((f32[256]{0:T(256)S(1)}, f32[256]{0:T(256)}, u32[]{:S(2)}) %copy-start.11) | copy-done | bytes 1048
  13.2 0.0 copy-start.12
  13.2 0.7 %copy-done.12 = f32[256]{0:T(256)S(1)} copy-done((f32[256]{0:T(256)S(1)}, f32[256]{0:T(256)}, u32[]{:S(2)}) %copy-start.12) | copy-done | bytes 1048
  13.9 2.0 %local_work.1 = (bf16[4,768,256]{2,1,0:T(8,128)(2,1)S(1)}, f32[128,128]{1,0:T(8,128)}) custom-call(s32[1]{0:T(128)} %bitcast.1.first_ref, s32[6,1024]{1,0:T(8,128)S(1)} %copy-done.6, f32[6,1024]{1,0:T(8,128)S(1)} %copy-done.4, s32[1,256]{1,0:T(1,128)S(1)} %bitcast.27, s32[1,256]{1,0:T(1,128)S(1)} %bitcast.28, f32[1,256]{1,0:T(1,128)S(1)} %bitcast.29, ...), custom_call_target="tpu_custom_call" | custom-call | tf_op jit(solution)/shard_map/local_work/pallas_call | solution.py:151
  15.9 6.7 %all-to-all-start.1 = ((f32[128,1,128]{2,1,0:T(1,128)}), f32[128,1,128]{2,1,0:T(1,128)S(1)}, u32[]{:S(2)}, u32[]{:S(2)}) async-start(f32[128,1,128]{2,1,0:T(1,128)} %bitcast.9), calls=%async_computation.1 | async-start | bytes 131072 | tf_op jit(solution)/shard_map/all_to_all | solution.py:330
  22.6 0.0 collective-permute-done.left_ref
  22.6 0.0 copy-start.2
  22.6 0.7 %copy-done.2 = bf16[272,768]{1,0:T(8,128)(2,1)} copy-done((bf16[272,768]{1,0:T(8,128)(2,1)}, bf16[272,768]{1,0:T(8,128)(2,1)S(1)}, u32[]{:S(2)}) %copy-start.2) | copy-done | bytes 417816
  23.4 0.0 collective-permute-done.1.right_ref
  23.4 0.0 copy-done.1
  23.4 0.0 copy-start.3
  23.4 1.0 %copy-done.3 = bf16[272,768]{1,0:T(8,128)(2,1)S(1)} copy-done((bf16[272,768]{1,0:T(8,128)(2,1)S(1)}, bf16[272,768]{1,0:T(8,128)(2,1)}, u32[]{:S(2)}) %copy-start.3) | copy-done | bytes 417816
  24.4 0.0 copy-start.5
  24.4 0.8 %copy-done.5 = f32[6,1024]{1,0:T(8,128)S(1)} copy-done((f32[6,1024]{1,0:T(8,128)S(1)}, f32[6,1024]{1,0:T(8,128)}, u32[]{:S(2)}) %copy-start.5) | copy-done | bytes 24600
  25.2 0.0 copy-start.8
  25.2 0.7 %copy-done.8 = f32[1024]{0:T(1024)S(1)} copy-done((f32[1024]{0:T(1024)S(1)}, f32[1024]{0:T(1024)}, u32[]{:S(2)}) %copy-start.8) | copy-done | bytes 4120
  25.8 3.9 %forecast.1 = bf16[8,256,128]{2,1,0:T(8,128)(2,1)S(1)} custom-call(f32[256,1024]{1,0:T(8,128)S(1)} %bitcast.21, bf16[272,768]{1,0:T(8,128)(2,1)S(1)} %copy-done.3, bf16[272,768]{1,0:T(8,128)(2,1)} %collective-permute-done.1.right_ref, bf16[4,768,256]{2,1,0:T(8,128)(2,1)S(1)} %get-tuple-element.11.own_ref, f32[6,1024]{1,0:T(8,128)S(1)} %copy-done.5, ...), custom_call_target="tpu_custom_call" | custom-call | tf_op jit(solution)/shard_map/forecast/pallas_call | solution.py:224
  29.8 2.4 %all-to-all-done.1 = f32[128,1,128]{2,1,0:T(1,128)S(1)} async-done(((f32[128,1,128]{2,1,0:T(1,128)}), f32[128,1,128]{2,1,0:T(1,128)S(1)}, u32[]{:S(2)}, u32[]{:S(2)}) %all-to-all-start.1) | async-done | bytes 65568 | tf_op jit(solution)/shard_map/all_to_all | solution.py:330
  32.2 12.8 %all_to_all.21 = bf16[8,256,128]{2,1,0:T(8,128)(2,1)S(1)} all-to-all(bf16[8,256,128]{2,1,0:T(8,128)(2,1)S(1)} %forecast.1), channel_id=1, replica_groups=mesh['member'=8,'region'=16] {'member'}, dimensions={0} | all-to-all | bytes 1048576 | tf_op jit(solution)/shard_map/all_to_all | solution.py:332
  44.9 5.2 %analysis.1 = bf16[2048,128]{1,0:T(8,128)(2,1)S(1)} custom-call(bf16[2048,128]{1,0:T(8,128)(2,1)S(1)} %bitcast.22, f32[128,128]{1,0:T(8,128)S(1)} %bitcast.24), custom_call_target="tpu_custom_call" | custom-call | tf_op jit(solution)/shard_map/analysis/pallas_call | solution.py:296
  50.2 12.8 %all_to_all.22 = bf16[8,256,128]{2,1,0:T(8,128)(2,1)S(1)} all-to-all(bf16[8,256,128]{2,1,0:T(8,128)(2,1)S(1)} %bitcast.23), channel_id=1, replica_groups=mesh['member'=8,'region'=16] {'member'}, dimensions={0} | all-to-all | bytes 1048576 | tf_op jit(solution)/shard_map/all_to_all | solution.py:335
  62.9 0.9 %copy_bitcast_fusion = bf16[32,8,1024]{2,1,0:T(8,128)(2,1)} fusion(bf16[8,256,128]{2,1,0:T(8,128)(2,1)S(1)} %all_to_all.22), kind=kLoop, calls=%fused_computation | loop fusion | bytes 1048576 | tf_op jit(solution)/shard_map/reshape | solution.py:337
Async XLA Ops:
  0.0 1.2 %copy-start = (f32[32,8,1024]{2,1,0:T(8,128)S(1)}, f32[32,8,1024]{2,1,0:T(8,128)}, u32[]{:S(2)}) copy-start(f32[32,8,1024]{2,1,0:T(8,128)} %param.8) | copy-start | bytes 3145732
  1.2 0.8 %copy-start.4 = (f32[6,1024]{1,0:T(8,128)S(1)}, f32[6,1024]{1,0:T(8,128)}, u32[]{:S(2)}) copy-start(f32[6,1024]{1,0:T(8,128)} %rate_ref.5) | copy-start | bytes 73732
  2.0 0.8 %copy-start.6 = (s32[6,1024]{1,0:T(8,128)S(1)}, s32[6,1024]{1,0:T(8,128)}, u32[]{:S(2)}) copy-start(s32[6,1024]{1,0:T(8,128)} %column_ref.3) | copy-start | bytes 73732
  2.7 0.7 %copy-start.7 = (f32[1024]{0:T(1024)S(1)}, f32[1024]{0:T(1024)}, u32[]{:S(2)}) copy-start(f32[1024]{0:T(1024)} %param.11) | copy-start | bytes 12292
  3.4 20.0 %copy-start.1 = (f32[32,8,1024]{2,1,0:T(8,128)S(1)}, f32[32,8,1024]{2,1,0:T(8,128)}, u32[]{:S(2)}) copy-start(f32[32,8,1024]{2,1,0:T(8,128)} %param.8) | copy-start | bytes 3145732
  4.4 18.2 %collective-permute-start = (bf16[272,768]{1,0:T(8,128)(2,1)}, bf16[272,768]{1,0:T(8,128)(2,1)S(1)}, u32[]{:S(2)}, u32[]{:S(2)}) collective-permute-start(bf16[272,768]{1,0:T(8,128)(2,1)} %get-tuple-element.9), channel_id=1, source_target_pairs={{0,1},{1,2},{2,3},{3,4},{4,5},{5,6},{6,7},{7,8},{8,9},{9,10},{10,1... | collective-permute-start | bytes 1253384 | tf_op jit(solution)/shard_map/ppermute | solution.py:324
  6.9 16.5 %collective-permute-start.1 = (bf16[272,768]{1,0:T(8,128)(2,1)}, bf16[272,768]{1,0:T(8,128)(2,1)}, u32[]{:S(2)}, u32[]{:S(2)}) collective-permute-start(bf16[272,768]{1,0:T(8,128)(2,1)} %get-tuple-element.10), channel_id=1, source_target_pairs={{1,0},{2,1},{3,2},{4,3},{5,4},{6,5},{7,6},{8,7},{9,8},{10,9},{11,1... | collective-permute-start | bytes 1253384 | tf_op jit(solution)/shard_map/ppermute | solution.py:325
  11.2 0.7 %copy-start.9 = (s32[256]{0:T(256)S(1)}, s32[256]{0:T(256)}, u32[]{:S(2)}) copy-start(s32[256]{0:T(256)} %param.12) | copy-start | bytes 3076
  11.9 0.7 %copy-start.10 = (s32[256]{0:T(256)S(1)}, s32[256]{0:T(256)}, u32[]{:S(2)}) copy-start(s32[256]{0:T(256)} %param.13) | copy-start | bytes 3076
  12.6 0.7 %copy-start.11 = (f32[256]{0:T(256)S(1)}, f32[256]{0:T(256)}, u32[]{:S(2)}) copy-start(f32[256]{0:T(256)} %param.14) | copy-start | bytes 3076
  13.2 0.7 %copy-start.12 = (f32[256]{0:T(256)S(1)}, f32[256]{0:T(256)}, u32[]{:S(2)}) copy-start(f32[256]{0:T(256)} %param.15) | copy-start | bytes 3076
  15.9 16.3 %all-to-all-start.1 = ((f32[128,1,128]{2,1,0:T(1,128)}), f32[128,1,128]{2,1,0:T(1,128)S(1)}, u32[]{:S(2)}, u32[]{:S(2)}) async-start(f32[128,1,128]{2,1,0:T(1,128)} %bitcast.9), calls=%async_computation.1 | async-start | bytes 131072 | tf_op jit(solution)/shard_map/all_to_all | solution.py:330
  22.6 0.8 %copy-start.2 = (bf16[272,768]{1,0:T(8,128)(2,1)}, bf16[272,768]{1,0:T(8,128)(2,1)S(1)}, u32[]{:S(2)}) copy-start(bf16[272,768]{1,0:T(8,128)(2,1)S(1)} %collective-permute-done.left_ref) | copy-start | bytes 1253380
  23.4 1.0 %copy-start.3 = (bf16[272,768]{1,0:T(8,128)(2,1)S(1)}, bf16[272,768]{1,0:T(8,128)(2,1)}, u32[]{:S(2)}) copy-start(bf16[272,768]{1,0:T(8,128)(2,1)} %copy-done.2) | copy-start | bytes 1253380
  24.4 0.8 %copy-start.5 = (f32[6,1024]{1,0:T(8,128)S(1)}, f32[6,1024]{1,0:T(8,128)}, u32[]{:S(2)}) copy-start(f32[6,1024]{1,0:T(8,128)} %rate_ref.5) | copy-start | bytes 73732
  25.2 0.7 %copy-start.8 = (f32[1024]{0:T(1024)S(1)}, f32[1024]{0:T(1024)}, u32[]{:S(2)}) copy-start(f32[1024]{0:T(1024)} %param.11) | copy-start | bytes 12292

commit v2 on v1

--- a/solution.py
+++ b/solution.py
@@ -18,6 +18,7 @@
 HALO = STEPS * RIM
 COEF_ROWS = 16
 TILE = 128
+STATE_CHUNKS = 4
 
 
 def high(value):
@@ -32,9 +33,8 @@
     return lax.dot_general(a, b, dims, preferred_element_type=jnp.float32)
 
 
-def dot_split(a, b, dims=(((1,), (0,)), ((), ()))):
-    ah, al, bh, bl = high(a), low(a), high(b), low(b)
-    return dot_f32(ah, bh, dims) + (dot_f32(ah, bl, dims) + dot_f32(al, bh, dims))
+def dot_half(a, b, dims=(((1,), (0,)), ((), ()))):
+    return dot_f32(high(a), high(b), dims)
 
 
 def cell_offsets(columns, first, total):
@@ -72,13 +72,50 @@
             matrix_ref[index, rows, lanes] = total
 
 
-def prepare_kernel(first_ref, state_ref, column_ref, rate_ref, speed_ref, up_ref, down_ref, *, total):
+def prepare_kernel(
+    state_hbm, column_hbm, rate_hbm, speed_hbm, patch_hbm, row_hbm, value_hbm, error_hbm,
+    wide_pair_ref, near_pair_ref, state_ref, coef_ref, message_ref,
+    column_ref, rate_ref, speed_ref, patch_ref, row_ref, value_ref, error_ref, small_sem, state_sem,
+    *, total, regions, groups,
+):
     rows, cells = state_ref.shape
-    offsets = cell_offsets(column_ref[...], first_ref[0], total).astype(jnp.float32)
+    small = [
+        pltpu.make_async_copy(source, target, small_sem.at[i])
+        for i, (source, target) in enumerate(
+            (
+                (column_hbm, column_ref),
+                (rate_hbm, rate_ref),
+                (speed_hbm, speed_ref),
+                (patch_hbm, patch_ref),
+                (row_hbm, row_ref),
+                (value_hbm, value_ref),
+                (error_hbm, error_ref),
+            )
+        )
+    ]
+    chunk = rows // STATE_CHUNKS
+    large = [
+        pltpu.make_async_copy(
+            state_hbm.at[pl.ds(i * chunk, chunk)],
+            state_ref.at[pl.ds(i * chunk, chunk)],
+            state_sem.at[i],
+        )
+        for i in range(STATE_CHUNKS)
+    ]
+    for copy in small + large:
+        copy.start()
+    for copy in small:
+        copy.wait()
+    region = lax.axis_index("region")
+    odd = region % 2
+    last = cells - HALO
+    wide_first = pl.multiple_of(odd * last, TILE)
+    near_first = pl.multiple_of((1 - odd) * last, TILE)
+    offsets = cell_offsets(column_ref[...], region * cells, total).astype(jnp.float32)
     rates = rate_ref[...]
     rate_sum = jnp.sum(rates, axis=0, keepdims=True)
     speed = speed_ref[...]
-    coef = jnp.concatenate(
+    coef_ref[...] = jnp.concatenate(
         [
             offsets,
             rates,
@@ -88,39 +125,9 @@
             low(speed).astype(jnp.float32),
         ],
         axis=0,
-    ).astype(jnp.bfloat16)
-    for ref, begin in ((up_ref, cells - HALO), (down_ref, 0)):
-        ref[:rows] = state_ref[:, begin : begin + HALO].astype(jnp.bfloat16)
-        ref[rows:] = coef[:, begin : begin + HALO]
-
-
-def vmem(count):
-    return [pl.BlockSpec(memory_space=pltpu.VMEM)] * count
-
-
-def prepare(first, state, columns, rates, speed, total):
-    rows, cells = state.shape
-    side = jax.ShapeDtypeStruct((rows + COEF_ROWS, HALO), jnp.bfloat16)
-    return pl.pallas_call(
-        functools.partial(prepare_kernel, total=total),
-        out_shape=(side, side),
-        in_specs=[pl.BlockSpec(memory_space=pltpu.SMEM)] + vmem(4),
-        out_specs=tuple(vmem(2)),
-        compiler_params=pltpu.CompilerParams(vmem_limit_bytes=8 << 20),
-        name="prepare",
-    )(first, state, columns, rates, speed)
-
-
-def local_kernel(
-    first_ref, column_ref, rate_ref, patch_ref, row_ref, value_ref, error_ref,
-    matrix_ref, message_ref, *, total, regions, groups,
-):
-    cells = column_ref.shape[1]
-    offsets = cell_offsets(column_ref[...], first_ref[0], total).astype(jnp.float32)
-    rates = rate_ref[...]
-    for b in range(cells // BLOCK):
-        part = slice(b * BLOCK, (b + 1) * BLOCK)
-        build_matrix(matrix_ref, b, offsets[:, part], rates[:, part])
+    )
+    wide_pair_ref[rows:] = coef_ref[:, pl.ds(wide_first, HALO)].astype(jnp.bfloat16)
+    near_pair_ref[rows:] = coef_ref[:, pl.ds(near_first, HALO)].astype(jnp.bfloat16)
     devices, count = message_ref.shape[0], patch_ref.shape[1]
     target = lax.broadcasted_iota(jnp.int32, (devices, count), 0)
     wanted = target % regions * groups + target // regions
@@ -144,52 +151,101 @@
             term = dot_f32(chosen, piece, (((1,), (1,)), ((), ())))
             message = term if message is None else message + term
     message_ref[...] = message
-
-
-def local_work(first, columns, rates, patch, row, value, error, total, regions, groups):
-    cells = columns.shape[1]
+    for i, copy in enumerate(large):
+        copy.wait()
+        part = pl.ds(i * chunk, chunk)
+        wide_pair_ref[part] = state_ref[part, pl.ds(wide_first, HALO)].astype(jnp.bfloat16)
+        near_pair_ref[part] = state_ref[part, pl.ds(near_first, HALO)].astype(jnp.bfloat16)
+
+
+def vmem(count):
+    return [pl.BlockSpec(memory_space=pltpu.VMEM)] * count
+
+
+def in_vmem(*values):
+    return [pltpu.with_memory_space_constraint(value, pltpu.VMEM) for value in values]
+
+
+def in_hbm(*values):
+    return [pltpu.with_memory_space_constraint(value, pltpu.HBM) for value in values]
+
+
+def prepare(state, columns, rates, speed, patch, row, value, error, total, regions, groups):
+    rows, cells = state.shape
+    count = patch.shape[1]
+    side = pltpu.VMEM((rows + COEF_ROWS, HALO), jnp.bfloat16)
     return pl.pallas_call(
-        functools.partial(local_kernel, total=total, regions=regions, groups=groups),
+        functools.partial(prepare_kernel, total=total, regions=regions, groups=groups),
         out_shape=(
-            jax.ShapeDtypeStruct((cells // BLOCK, WINDOW, BLOCK), jnp.bfloat16),
+            side,
+            side,
+            pltpu.VMEM((rows, cells), jnp.float32),
+            pltpu.VMEM((COEF_ROWS, cells), jnp.float32),
             jax.ShapeDtypeStruct((regions * groups, TILE), jnp.float32),
         ),
-        in_specs=[pl.BlockSpec(memory_space=pltpu.SMEM)] + vmem(6),
-        out_specs=tuple(vmem(2)),
+        in_specs=[pl.BlockSpec(memory_space=pltpu.HBM)] * 8,
+        out_specs=tuple(vmem(5)),
+        scratch_shapes=[
+            pltpu.VMEM(columns.shape, jnp.int32),
+            pltpu.VMEM(rates.shape, jnp.float32),
+            pltpu.VMEM(speed.shape, jnp.float32),
+            pltpu.VMEM((1, count), jnp.int32),
+            pltpu.VMEM((1, count), jnp.int32),
+            pltpu.VMEM((1, count), jnp.float32),
+            pltpu.VMEM((1, count), jnp.float32),
+            pltpu.SemaphoreType.DMA((7,)),
+            pltpu.SemaphoreType.DMA((STATE_CHUNKS,)),
+        ],
         compiler_params=pltpu.CompilerParams(vmem_limit_bytes=8 << 20),
-        name="local_work",
-    )(first, columns, rates, patch, row, value, error)
+        name="prepare",
+    )(*in_hbm(state, columns, rates, speed, patch, row, value, error))
+
+
+def matrices_kernel(coef_ref, matrix_ref):
+    for b in range(matrix_ref.shape[0]):
+        part = slice(b * BLOCK, (b + 1) * BLOCK)
+        build_matrix(matrix_ref, b, coef_ref[0:6, part], coef_ref[6:12, part])
+
+
+def own_matrices(coef):
+    shape = (coef.shape[1] // BLOCK, WINDOW, BLOCK)
+    return pl.pallas_call(
+        matrices_kernel,
+        out_shape=pltpu.VMEM(shape, jnp.bfloat16),
+        in_specs=vmem(1),
+        out_specs=vmem(1)[0],
+        compiler_params=pltpu.CompilerParams(vmem_limit_bytes=4 << 20),
+        name="own_matrices",
+    )(*in_vmem(coef))
 
 
 def forecast_kernel(
-    state_ref, left_ref, right_ref, own_ref, rate_ref, speed_ref, out_ref,
-    matrix_ref, field_a, field_b, wide_ref,
+    state_ref, wide_pair_ref, near_pair_ref, own_ref, own_coef_ref, out_ref,
+    matrix_ref, coef_ref, field_a, field_b, wide_ref,
 ):
     rows, cells = state_ref.shape
     own_blocks = cells // BLOCK
     side_blocks = (STEPS - 1) * RIM // BLOCK
     blocks = own_blocks + 2 * side_blocks
+    odd = lax.axis_index("region") % 2
+    far = HALO + cells
+    for ref, begin in ((wide_pair_ref, odd * far), (near_pair_ref, (1 - odd) * far)):
+        begin = pl.multiple_of(begin, TILE)
+        coef_ref[:, pl.ds(begin, HALO)] = ref[rows:].astype(jnp.float32)
+        field_a[:, pl.ds(begin, HALO)] = ref[:rows]
+    coef_ref[:, HALO:far] = own_coef_ref[...]
+    field_a[:, HALO:far] = state_ref[...].astype(jnp.bfloat16)
     keep, speed, matrices = [], [], []
     for b in range(blocks):
-        if b < side_blocks or b >= side_blocks + own_blocks:
-            ref = left_ref if b < side_blocks else right_ref
-            start = RIM + b * BLOCK if b < side_blocks else (b - side_blocks - own_blocks) * BLOCK
+        part = slice(RIM + b * BLOCK, RIM + (b + 1) * BLOCK)
+        if side_blocks <= b < side_blocks + own_blocks:
+            matrices.append((own_ref, b - side_blocks))
+        else:
             index = b if b < side_blocks else b - own_blocks
-            coef = ref[rows:, start : start + BLOCK].astype(jnp.float32)
-            build_matrix(matrix_ref, index, coef[0:6], coef[6:12])
-            total = coef[12:13] + coef[13:14]
-            quick = coef[14:15] + coef[15:16]
+            build_matrix(matrix_ref, index, coef_ref[0:6, part], coef_ref[6:12, part])
             matrices.append((matrix_ref, index))
-        else:
-            start = (b - side_blocks) * BLOCK
-            total = jnp.sum(rate_ref[:, start : start + BLOCK], axis=0, keepdims=True)
-            quick = speed_ref[:, start : start + BLOCK]
-            matrices.append((own_ref, b - side_blocks))
-        keep.append(1.0 - total)
-        speed.append(quick)
-    field_a[:, :HALO] = left_ref[:rows]
-    field_a[:, HALO : HALO + cells] = state_ref[...].astype(jnp.bfloat16)
-    field_a[:, HALO + cells :] = right_ref[:rows]
+        keep.append(1.0 - (coef_ref[12:13, part] + coef_ref[13:14, part]))
+        speed.append(coef_ref[14:15, part] + coef_ref[15:16, part])
     source, target = field_a, field_b
     for step in range(STEPS):
         for b in range(step, blocks - step):
@@ -217,24 +273,25 @@
         source, target = target, source
 
 
-def forecast(state, left, right, own, rates, speed):
+def forecast(state, wide_pair, near_pair, own, coef):
     rows, cells = state.shape
     sides = 2 * (STEPS - 1) * RIM // BLOCK
     padded = cells + 2 * HALO
     return pl.pallas_call(
         forecast_kernel,
-        out_shape=jax.ShapeDtypeStruct((cells // PATCH_CELLS, rows, PATCH_CELLS), jnp.bfloat16),
-        in_specs=vmem(6),
+        out_shape=pltpu.VMEM((cells // PATCH_CELLS, rows, PATCH_CELLS), jnp.bfloat16),
+        in_specs=vmem(5),
         out_specs=pl.BlockSpec(memory_space=pltpu.VMEM),
         scratch_shapes=[
             pltpu.VMEM((sides, WINDOW, BLOCK), jnp.bfloat16),
+            pltpu.VMEM((COEF_ROWS, padded), jnp.float32),
             pltpu.VMEM((rows, padded), jnp.bfloat16),
             pltpu.VMEM((rows, padded), jnp.bfloat16),
             pltpu.VMEM((rows, padded), jnp.float32),
         ],
-        compiler_params=pltpu.CompilerParams(vmem_limit_bytes=20 << 20),
+        compiler_params=pltpu.CompilerParams(vmem_limit_bytes=16 << 20),
         name="forecast",
-    )(state, left, right, own, rates, speed)
+    )(*in_vmem(state, wide_pair, near_pair, own, coef))
 
 
 def analysis_kernel(x_ref, message_ref, out_ref, wide_ref, x2_ref, select_ref):
@@ -262,30 +319,48 @@
     row = lax.broadcasted_iota(jnp.int32, (members, members), 0)
     column = lax.broadcasted_iota(jnp.int32, (members, members), 1)
     diagonal = jnp.where(row == column, 1.0, 0.0)
-    system = diagonal + dot_split(scaled, scaled, (((1,), (1,)), ((), ())))
+    product = dot_half(scaled, scaled, (((1,), (1,)), ((), ())))
+    system = diagonal + product
     square = jnp.sum(jnp.sum(system * system, axis=0, keepdims=True), axis=1, keepdims=True)
-    inverse_scale = lax.rsqrt(square)
+    inverse_scale = jnp.broadcast_to(lax.rsqrt(square), (1, members))
     innovation = rooted * (value - seen_mean) * spread
     forcing = jnp.sum(scaled * innovation, axis=1, keepdims=True)
-    iterate = system * inverse_scale
-    factor = 1.5 * diagonal - 0.5 * iterate
-    inverse_root = factor
-    iterate = dot_split(iterate, factor)
-    for sweep in range(1, NS_ITERS):
-        factor = 1.5 * diagonal - 0.5 * dot_split(inverse_root, iterate)
+    p, z = inverse_scale, jnp.ones_like(inverse_scale)
+    both = product * inverse_scale
+    root = None
+    for sweep in range(NS_ITERS):
+        f = 1.5 - 0.5 * p
+        factor = -0.5 * both
+        narrow = factor.astype(jnp.bfloat16)
+        if root is None:
+            new_root = factor
+        else:
+            new_root = z * factor + f * root + dot_f32(high(root), narrow)
         if sweep < NS_ITERS - 1:
-            iterate = dot_split(iterate, factor)
-        inverse_root = dot_split(factor, inverse_root)
-    inner = jnp.sum(inverse_root * forcing, axis=0, keepdims=True)
-    shift = jnp.sum(inverse_root * inner, axis=1, keepdims=True) * inverse_scale
-    transform = (inverse_root * jnp.sqrt(inverse_scale)).astype(jnp.bfloat16)
-    for level in range(LEVELS):
-        part = x2_ref[:, level * PATCH_CELLS : (level + 1) * PATCH_CELLS].astype(jnp.float32)
-        mean = jnp.sum(part, axis=0, keepdims=True) * (1.0 / members)
-        anomaly = part - mean
-        moved = mean + jnp.sum(anomaly * shift, axis=0, keepdims=True)
-        updated = moved + dot_f32(transform, anomaly.astype(jnp.bfloat16), (((0,), (0,)), ((), ())))
-        wide_ref[pl.ds(level, members, stride=LEVELS), :] = updated
+            once = p * factor + f * both + dot_f32(high(both), narrow)
+            q = p * f
+            both = q * factor + f * once + dot_f32(high(once), narrow)
+            p = q * f
+        root, z = new_root, z * f
+    whole = root + z * diagonal
+    inner = jnp.sum(whole * forcing, axis=0, keepdims=True)
+    shift = jnp.sum(whole * inner, axis=1, keepdims=True) * inverse_scale[:, 0:1]
+    half_scale = jnp.sqrt(inverse_scale)
+    transform = (root * half_scale).astype(jnp.bfloat16)
+    direct = (z * half_scale)[:, 0:PATCH_CELLS]
+    pair = 2
+    for level in range(0, LEVELS, pair):
+        pieces = []
+        for k in range(level, level + pair):
+            part = x2_ref[:, k * PATCH_CELLS : (k + 1) * PATCH_CELLS].astype(jnp.float32)
+            mean = jnp.sum(part, axis=0, keepdims=True) * (1.0 / members)
+            anomaly = part - mean
+            base = mean + jnp.sum(anomaly * shift, axis=0, keepdims=True) + direct * anomaly
+            pieces.append((anomaly.astype(jnp.bfloat16), base))
+        moved = dot_f32(transform, jnp.concatenate([piece[0] for piece in pieces], axis=1))
+        for k in range(pair):
+            updated = pieces[k][1] + moved[:, k * PATCH_CELLS : (k + 1) * PATCH_CELLS]
+            wide_ref[pl.ds(level + k, members, stride=LEVELS), :] = updated
     out_ref[...] = wide_ref[...].astype(jnp.bfloat16)
 
 
@@ -295,7 +370,7 @@
     slots = 2 * message.shape[0]
     return pl.pallas_call(
         analysis_kernel,
-        out_shape=jax.ShapeDtypeStruct(x.shape, jnp.bfloat16),
+        out_shape=pltpu.VMEM(x.shape, jnp.bfloat16),
         in_specs=vmem(2),
         out_specs=pl.BlockSpec(memory_space=pltpu.VMEM),
         compiler_params=pltpu.CompilerParams(vmem_limit_bytes=12 << 20),
@@ -305,7 +380,7 @@
             pltpu.VMEM((LEVELS * PATCH_CELLS, slots), jnp.bfloat16),
         ],
         name="analysis",
-    )(x, message)
+    )(*in_vmem(x, message))
 
 
 def on_device(
@@ -316,19 +391,20 @@
     regions = lax.axis_size("region")
     groups = lax.axis_size("member")
     total = cells * regions
-    first = (lax.axis_index("region") * cells).astype(jnp.int32).reshape(1)
     flat = state.reshape(members * levels, cells)
-    speed = amplification_speed[None, :]
-    sides = prepare(first, flat, adjacent_columns, adjacent_rates, speed, total)
-    up = [(i, (i + 1) % regions) for i in range(regions)]
-    left = lax.ppermute(sides[0], "region", up)
-    right = lax.ppermute(sides[1], "region", [(j, i) for i, j in up])
-    own, message = local_work(
-        first, adjacent_columns, adjacent_rates, obs_patch[None, :], obs_row[None, :],
-        obs_value[None, :], obs_error[None, :], total, regions, groups,
+    wide_pair, near_pair, kept, coef, message = prepare(
+        flat, adjacent_columns, adjacent_rates, amplification_speed[None, :],
+        obs_patch[None, :], obs_row[None, :], obs_value[None, :], obs_error[None, :],
+        total, regions, groups,
     )
+    pairs = [(i, (i + 1) % regions) for i in range(regions)]
+    wide_swap = [edge for i, j in pairs[1::2] for edge in ((i, j), (j, i))]
+    near_swap = [edge for i, j in pairs[0::2] for edge in ((i, j), (j, i))]
+    wide_pair = lax.ppermute(wide_pair, "region", wide_swap)
+    near_pair = lax.ppermute(near_pair, "region", near_swap)
     message = lax.all_to_all(message, ("member", "region"), 0, 0, tiled=True)
-    rounded = forecast(flat, left, right, own, adjacent_rates, speed)
+    own = own_matrices(coef)
+    rounded = forecast(kept, wide_pair, near_pair, own, coef)
     patched = lax.all_to_all(rounded, "member", 0, 0, tiled=True)
     analysed = analysis(patched.reshape(-1, PATCH_CELLS), message)
     returned = analysed.reshape(groups, members * levels, PATCH_CELLS)

time: 64.5 us -> 55.5 us (0.86)
  local copies, waits for them, and re-layouts: 10.2 us -> 0.88 us
  waiting for transfers between devices: 2.38 us -> 5.53 us
  Pallas kernels: 12.1 us -> 9.45 us
    unnamed x26 -> x0, local copies, waits for them, and re-layouts: 9.34 us -> none
    pallas_call x4, Pallas kernels: 12.1 us -> 9.45 us  [the longest x1 3.27 us: analysis(): pl.pallas_call(analysis_kernel, out_shape=pltpu.VMEM(x.shape, jnp.bfloat1...]
    ppermute x2, waiting for transfers between devices: 0.01 us -> 2.61 us  [the longest x1 1.67 us: on_device(): wide_pair = lax.ppermute(wide_pair, 'region', wide_swap)]
  transfers between devices with their start and end apart: 3 -> 3, of which waited for: 1 -> 3; matrix products, arithmetic and copies ran while one was open for 0% -> 0% of each run, Pallas kernels for 9% -> 7%
where the time goes in v2:
time: 55.5 us; the launch traced here: 55.3 us
  blocking collectives  25.8 us (46%)
  starting transfers between devices  13.6 us (25%)
  Pallas kernels  9.45 us (17%)
  waiting for transfers between devices  5.53 us (10%)
  local copies, waits for them, and re-layouts  0.88 us (2%)
    all_to_all x1, blocking collectives, on_device(): patched = lax.all_to_all(rounded, 'member', 0, 0, tiled=True)  13.1 us
    all_to_all x1, blocking collectives, on_device(): back = lax.all_to_all(returned, 'member', 0, 0, tiled=True)  12.8 us
    ppermute x1, starting transfers between devices, on_device(): wide_pair = lax.ppermute(wide_pair, 'region', wide_swap)  6.85 us
    all_to_all x1, starting transfers between devices, on_device(): message = lax.all_to_all(message, ('member', 'region'), 0, 0, tiled=True)  6.74 us
    pallas_call x1, Pallas kernels, analysis(): pl.pallas_call(analysis_kernel, out_shape=pltpu.VMEM(x.shape, jnp.bfloat1...  3.27 us
    pallas_call x1, Pallas kernels, forecast(): pl.pallas_call(forecast_kernel, out_shape=pltpu.VMEM((cells // PATCH_CELL...  3.02 us
    all_to_all x1, waiting for transfers between devices, on_device(): message = lax.all_to_all(message, ('member', 'region'), 0, 0, tiled=True)  2.92 us
    pallas_call x1, Pallas kernels, prepare(): pl.pallas_call(functools.partial(prepare_kernel, total=total, regions=reg...  2.25 us
  transfers between devices with their start and end apart: 3, of which 3 were waited for; matrix products, arithmetic and copies ran while one was open for 0% of the time, Pallas kernels for 7%

profile of v2, /device:TPU:1, one launch (start us, length us, event | category | flops | bytes accessed | tf_op | source)
XLA Modules:
  0.0 55.3 jit_solution(7415266137941856682)
XLA Ops:
  0.0 2.2 %prepare.1 = (bf16[272,768]{1,0:T(8,128)(2,1)S(1)}, bf16[272,768]{1,0:T(8,128)(2,1)S(1)}, f32[256,1024]{1,0:T(8,128)S(1)}, f32[16,1024]{1,0:T(8,128)S(1)}, f32[128,128]{1,0:T(8,128)}) custom-call(f32[256,1024]{1,0:T(8,128)} %bitcast.22, s32[6,1024]{1,0:T(8,128)} %column_hbm.1, f32[6,1024]{1,0:T(8,128)} %rate_hbm.1, f32[1,1024]{1,0:T(1,128)} %bitcast.23, ...), custom_call_target="tpu_custom_call" | custom-call | tf_op jit(solution)/shard_map/prepare/pallas_call | solution.py:177
  2.3 6.8 %collective-permute-start = (bf16[272,768]{1,0:T(8,128)(2,1)S(1)}, bf16[272,768]{1,0:T(8,128)(2,1)S(1)}, u32[]{:S(2)}, u32[]{:S(2)}) collective-permute-start(bf16[272,768]{1,0:T(8,128)(2,1)S(1)} %get-tuple-element.11), channel_id=1, source_target_pairs={{1,2},{2,1},{3,4},{4,3},{5,6},{6,5},{7,8},{8,7},{9,10},{10,9},{11,... | collective-permute-start | bytes 1253384 | tf_op jit(solution)/shard_map/ppermute | solution.py:403
  9.1 0.0 collective-permute-start.1
  9.1 6.7 %all-to-all-start.1 = ((f32[128,1,128]{2,1,0:T(1,128)}), f32[128,1,128]{2,1,0:T(1,128)S(1)}, u32[]{:S(2)}, u32[]{:S(2)}) async-start(f32[128,1,128]{2,1,0:T(1,128)} %bitcast.8), calls=%async_computation.1 | async-start | bytes 131072 | tf_op jit(solution)/shard_map/all_to_all | solution.py:405
  15.9 0.9 %own_matrices.1.own_ref = bf16[4,768,256]{2,1,0:T(8,128)(2,1)S(1)} custom-call(f32[16,1024]{1,0:T(8,128)S(1)} %get-tuple-element.13.coef_ref.own_coef_ref), custom_call_target="tpu_custom_call" | custom-call | tf_op jit(solution)/shard_map/own_matrices/pallas_call | solution.py:212
  16.8 1.7 %collective-permute-done.wide_pair_ref = bf16[272,768]{1,0:T(8,128)(2,1)S(1)} collective-permute-done((bf16[272,768]{1,0:T(8,128)(2,1)S(1)}, bf16[272,768]{1,0:T(8,128)(2,1)S(1)}, u32[]{:S(2)}, u32[]{:S(2)}) %collective-permute-start) | collective-permute-done | bytes 417824 | tf_op jit(solution)/shard_map/ppermute | solution.py:403
  18.5 0.9 %collective-permute-done.1.near_pair_ref = bf16[272,768]{1,0:T(8,128)(2,1)S(1)} collective-permute-done((bf16[272,768]{1,0:T(8,128)(2,1)S(1)}, bf16[272,768]{1,0:T(8,128)(2,1)S(1)}, u32[]{:S(2)}, u32[]{:S(2)}) %collective-permute-start.1) | collective-permute-done | bytes 417824 | tf_op jit(solution)/shard_map/ppermute | solution.py:404
  19.4 3.0 %forecast.1 = bf16[8,256,128]{2,1,0:T(8,128)(2,1)S(1)} custom-call(f32[256,1024]{1,0:T(8,128)S(1)} %get-tuple-element.10.state_ref, bf16[272,768]{1,0:T(8,128)(2,1)S(1)} %collective-permute-done.wide_pair_ref, bf16[272,768]{1,0:T(8,128)(2,1)S(1)} %collective-permute-done.1.near_pair_ref, bf16[4,768,256]{2,1,0:T(8,128)(2,1)S(1)} %own_matrices.1.own_ref, ...), custom_call_target="tpu_custom_call" | custom-call | tf_op jit(solution)/shard_map/forecast/pallas_call | solution.py:280
  22.4 2.9 %all-to-all-done.1 = f32[128,1,128]{2,1,0:T(1,128)S(1)} async-done(((f32[128,1,128]{2,1,0:T(1,128)}), f32[128,1,128]{2,1,0:T(1,128)S(1)}, u32[]{:S(2)}, u32[]{:S(2)}) %all-to-all-start.1) | async-done | bytes 65568 | tf_op jit(solution)/shard_map/all_to_all | solution.py:405
  25.3 13.1 %all_to_all.21 = bf16[8,256,128]{2,1,0:T(8,128)(2,1)S(1)} all-to-all(bf16[8,256,128]{2,1,0:T(8,128)(2,1)S(1)} %forecast.1), channel_id=1, replica_groups=mesh['member'=8,'region'=16] {'member'}, dimensions={0} | all-to-all | bytes 1048576 | tf_op jit(solution)/shard_map/all_to_all | solution.py:408
  38.4 3.3 %analysis.1 = bf16[2048,128]{1,0:T(8,128)(2,1)S(1)} custom-call(bf16[2048,128]{1,0:T(8,128)(2,1)S(1)} %bitcast.19, f32[128,128]{1,0:T(8,128)S(1)} %bitcast.21), custom_call_target="tpu_custom_call" | custom-call | tf_op jit(solution)/shard_map/analysis/pallas_call | solution.py:371
  41.7 12.8 %all_to_all.22 = bf16[8,256,128]{2,1,0:T(8,128)(2,1)S(1)} all-to-all(bf16[8,256,128]{2,1,0:T(8,128)(2,1)S(1)} %bitcast.20), channel_id=1, replica_groups=mesh['member'=8,'region'=16] {'member'}, dimensions={0} | all-to-all | bytes 1048576 | tf_op jit(solution)/shard_map/all_to_all | solution.py:411
  54.5 0.9 %copy_bitcast_fusion = bf16[32,8,1024]{2,1,0:T(8,128)(2,1)} fusion(bf16[8,256,128]{2,1,0:T(8,128)(2,1)S(1)} %all_to_all.22), kind=kLoop, calls=%fused_computation | loop fusion | bytes 1048576 | tf_op jit(solution)/shard_map/reshape | solution.py:413
Async XLA Ops:
  2.3 16.2 %collective-permute-start = (bf16[272,768]{1,0:T(8,128)(2,1)S(1)}, bf16[272,768]{1,0:T(8,128)(2,1)S(1)}, u32[]{:S(2)}, u32[]{:S(2)}) collective-permute-start(bf16[272,768]{1,0:T(8,128)(2,1)S(1)} %get-tuple-element.11), channel_id=1, source_target_pairs={{1,2},{2,1},{3,4},{4,3},{5,6},{6,5},{7,8},{8,7},{9,10},{10,9},{11,... | collective-permute-start | bytes 1253384 | tf_op jit(solution)/shard_map/ppermute | solution.py:403
  9.1 10.3 %collective-permute-start.1 = (bf16[272,768]{1,0:T(8,128)(2,1)S(1)}, bf16[272,768]{1,0:T(8,128)(2,1)S(1)}, u32[]{:S(2)}, u32[]{:S(2)}) collective-permute-start(bf16[272,768]{1,0:T(8,128)(2,1)S(1)} %get-tuple-element.12), channel_id=1, source_target_pairs={{0,1},{1,0},{2,3},{3,2},{4,5},{5,4},{6,7},{7,6},{8,9},{9,8},{10,11... | collective-permute-start | bytes 1253384 | tf_op jit(solution)/shard_map/ppermute | solution.py:404
  9.1 16.2 %all-to-all-start.1 = ((f32[128,1,128]{2,1,0:T(1,128)}), f32[128,1,128]{2,1,0:T(1,128)S(1)}, u32[]{:S(2)}, u32[]{:S(2)}) async-start(f32[128,1,128]{2,1,0:T(1,128)} %bitcast.8), calls=%async_computation.1 | async-start | bytes 131072 | tf_op jit(solution)/shard_map/all_to_all | solution.py:405

commit v3 on v2

--- a/solution.py
+++ b/solution.py
@@ -7,6 +7,7 @@
 from jax.experimental import pallas as pl
 from jax.experimental.pallas import tpu as pltpu
 from jax.sharding import PartitionSpec as P
+
 
 PATCH_CELLS = 128
 RIM = 256
@@ -19,6 +20,7 @@
 COEF_ROWS = 16
 TILE = 128
 STATE_CHUNKS = 4
+SHIFTS = 4
 
 
 def high(value):
@@ -72,27 +74,21 @@
             matrix_ref[index, rows, lanes] = total
 
 
+def fetches(sources, targets, sem):
+    return [
+        pltpu.make_async_copy(source, target, sem.at[i])
+        for i, (source, target) in enumerate(zip(sources, targets))
+    ]
+
+
 def prepare_kernel(
-    state_hbm, column_hbm, rate_hbm, speed_hbm, patch_hbm, row_hbm, value_hbm, error_hbm,
-    wide_pair_ref, near_pair_ref, state_ref, coef_ref, message_ref,
-    column_ref, rate_ref, speed_ref, patch_ref, row_ref, value_ref, error_ref, small_sem, state_sem,
-    *, total, regions, groups,
+    state_hbm, column_hbm, rate_hbm, speed_hbm, wide_pair_ref, near_pair_ref, state_ref, coef_ref,
+    column_ref, rate_ref, speed_ref, small_sem, state_sem, *, total,
 ):
     rows, cells = state_ref.shape
-    small = [
-        pltpu.make_async_copy(source, target, small_sem.at[i])
-        for i, (source, target) in enumerate(
-            (
-                (column_hbm, column_ref),
-                (rate_hbm, rate_ref),
-                (speed_hbm, speed_ref),
-                (patch_hbm, patch_ref),
-                (row_hbm, row_ref),
-                (value_hbm, value_ref),
-                (error_hbm, error_ref),
-            )
-        )
-    ]
+    small = fetches(
+        (column_hbm, rate_hbm, speed_hbm), (column_ref, rate_ref, speed_ref), small_sem
+    )
     chunk = rows // STATE_CHUNKS
     large = [
         pltpu.make_async_copy(
@@ -128,6 +124,79 @@
     )
     wide_pair_ref[rows:] = coef_ref[:, pl.ds(wide_first, HALO)].astype(jnp.bfloat16)
     near_pair_ref[rows:] = coef_ref[:, pl.ds(near_first, HALO)].astype(jnp.bfloat16)
+    for i, copy in enumerate(large):
+        copy.wait()
+        part = pl.ds(i * chunk, chunk)
+        wide_pair_ref[part] = state_ref[part, pl.ds(wide_first, HALO)].astype(jnp.bfloat16)
+        near_pair_ref[part] = state_ref[part, pl.ds(near_first, HALO)].astype(jnp.bfloat16)
+
+
+def vmem(count):
+    return [pl.BlockSpec(memory_space=pltpu.VMEM)] * count
+
+
+def in_vmem(*values):
+    return [pltpu.with_memory_space_constraint(value, pltpu.VMEM) for value in values]
+
+
+def in_hbm(*values):
+    return [pltpu.with_memory_space_constraint(value, pltpu.HBM) for value in values]
+
+
+def prepare(state, columns, rates, speed, total):
+    rows, cells = state.shape
+    side = pltpu.VMEM((rows + COEF_ROWS, HALO), jnp.bfloat16)
+    return pl.pallas_call(
+        functools.partial(prepare_kernel, total=total),
+        out_shape=(
+            side,
+            side,
+            pltpu.VMEM((rows, cells), jnp.float32),
+            pltpu.VMEM((COEF_ROWS, cells), jnp.float32),
+        ),
+        in_specs=[pl.BlockSpec(memory_space=pltpu.HBM)] * 4,
+        out_specs=tuple(vmem(4)),
+        scratch_shapes=[
+            pltpu.VMEM(columns.shape, jnp.int32),
+            pltpu.VMEM(rates.shape, jnp.float32),
+            pltpu.VMEM(speed.shape, jnp.float32),
+            pltpu.SemaphoreType.DMA((3,)),
+            pltpu.SemaphoreType.DMA((STATE_CHUNKS,)),
+        ],
+        compiler_params=pltpu.CompilerParams(vmem_limit_bytes=8 << 20),
+        name="prepare",
+    )(*in_hbm(state, columns, rates, speed))
+
+
+def matrices_kernel(coef_ref, matrix_ref):
+    for b in range(matrix_ref.shape[0]):
+        part = slice(b * BLOCK, (b + 1) * BLOCK)
+        build_matrix(matrix_ref, b, coef_ref[0:6, part], coef_ref[6:12, part])
+
+
+def own_matrices(coef):
+    shape = (coef.shape[1] // BLOCK, WINDOW, BLOCK)
+    return pl.pallas_call(
+        matrices_kernel,
+        out_shape=pltpu.VMEM(shape, jnp.bfloat16),
+        in_specs=vmem(1),
+        out_specs=vmem(1)[0],
+        compiler_params=pltpu.CompilerParams(vmem_limit_bytes=4 << 20),
+        name="own_matrices",
+    )(*in_vmem(coef))
+
+
+def message_kernel(
+    patch_hbm, row_hbm, value_hbm, error_hbm, message_ref,
+    patch_ref, row_ref, value_ref, error_ref, sem, *, regions, groups,
+):
+    small = fetches(
+        (patch_hbm, row_hbm, value_hbm, error_hbm), (patch_ref, row_ref, value_ref, error_ref), sem
+    )
+    for copy in small:
+        copy.start()
+    for copy in small:
+        copy.wait()
     devices, count = message_ref.shape[0], patch_ref.shape[1]
     target = lax.broadcasted_iota(jnp.int32, (devices, count), 0)
     wanted = target % regions * groups + target // regions
@@ -151,77 +220,30 @@
             term = dot_f32(chosen, piece, (((1,), (1,)), ((), ())))
             message = term if message is None else message + term
     message_ref[...] = message
-    for i, copy in enumerate(large):
-        copy.wait()
-        part = pl.ds(i * chunk, chunk)
-        wide_pair_ref[part] = state_ref[part, pl.ds(wide_first, HALO)].astype(jnp.bfloat16)
-        near_pair_ref[part] = state_ref[part, pl.ds(near_first, HALO)].astype(jnp.bfloat16)
-
-
-def vmem(count):
-    return [pl.BlockSpec(memory_space=pltpu.VMEM)] * count
-
-
-def in_vmem(*values):
-    return [pltpu.with_memory_space_constraint(value, pltpu.VMEM) for value in values]
-
-
-def in_hbm(*values):
-    return [pltpu.with_memory_space_constraint(value, pltpu.HBM) for value in values]
-
-
-def prepare(state, columns, rates, speed, patch, row, value, error, total, regions, groups):
-    rows, cells = state.shape
+
+
+def observation_message(patch, row, value, error, regions, groups):
     count = patch.shape[1]
-    side = pltpu.VMEM((rows + COEF_ROWS, HALO), jnp.bfloat16)
     return pl.pallas_call(
-        functools.partial(prepare_kernel, total=total, regions=regions, groups=groups),
-        out_shape=(
-            side,
-            side,
-            pltpu.VMEM((rows, cells), jnp.float32),
-            pltpu.VMEM((COEF_ROWS, cells), jnp.float32),
-            jax.ShapeDtypeStruct((regions * groups, TILE), jnp.float32),
-        ),
-        in_specs=[pl.BlockSpec(memory_space=pltpu.HBM)] * 8,
-        out_specs=tuple(vmem(5)),
+        functools.partial(message_kernel, regions=regions, groups=groups),
+        out_shape=jax.ShapeDtypeStruct((regions * groups, TILE), jnp.float32),
+        in_specs=[pl.BlockSpec(memory_space=pltpu.HBM)] * 4,
+        out_specs=vmem(1)[0],
         scratch_shapes=[
-            pltpu.VMEM(columns.shape, jnp.int32),
-            pltpu.VMEM(rates.shape, jnp.float32),
-            pltpu.VMEM(speed.shape, jnp.float32),
             pltpu.VMEM((1, count), jnp.int32),
             pltpu.VMEM((1, count), jnp.int32),
             pltpu.VMEM((1, count), jnp.float32),
             pltpu.VMEM((1, count), jnp.float32),
-            pltpu.SemaphoreType.DMA((7,)),
-            pltpu.SemaphoreType.DMA((STATE_CHUNKS,)),
+            pltpu.SemaphoreType.DMA((4,)),
         ],
-        compiler_params=pltpu.CompilerParams(vmem_limit_bytes=8 << 20),
-        name="prepare",
-    )(*in_hbm(state, columns, rates, speed, patch, row, value, error))
-
-
-def matrices_kernel(coef_ref, matrix_ref):
-    for b in range(matrix_ref.shape[0]):
-        part = slice(b * BLOCK, (b + 1) * BLOCK)
-        build_matrix(matrix_ref, b, coef_ref[0:6, part], coef_ref[6:12, part])
-
-
-def own_matrices(coef):
-    shape = (coef.shape[1] // BLOCK, WINDOW, BLOCK)
-    return pl.pallas_call(
-        matrices_kernel,
-        out_shape=pltpu.VMEM(shape, jnp.bfloat16),
-        in_specs=vmem(1),
-        out_specs=vmem(1)[0],
         compiler_params=pltpu.CompilerParams(vmem_limit_bytes=4 << 20),
-        name="own_matrices",
-    )(*in_vmem(coef))
+        name="message",
+    )(*in_hbm(patch, row, value, error))
 
 
 def forecast_kernel(
-    state_ref, wide_pair_ref, near_pair_ref, own_ref, own_coef_ref, out_ref,
-    matrix_ref, coef_ref, field_a, field_b, wide_ref,
+    state_ref, wide_pair_ref, near_pair_ref, own_ref, own_coef_ref, own_0, own_1, own_2, own_3,
+    swap_ref, matrix_ref, coef_ref, field_a, field_b, wide_ref,
 ):
     rows, cells = state_ref.shape
     own_blocks = cells // BLOCK
@@ -247,7 +269,7 @@
         keep.append(1.0 - (coef_ref[12:13, part] + coef_ref[13:14, part]))
         speed.append(coef_ref[14:15, part] + coef_ref[15:16, part])
     source, target = field_a, field_b
-    for step in range(STEPS):
+    for step in range(STEPS - 1):
         for b in range(step, blocks - step):
             first = b * BLOCK
             middle = slice(first + RIM, first + RIM + BLOCK)
@@ -262,15 +284,29 @@
                 centre = source[:, middle].astype(jnp.float32)
             blended = centre * keep[b] + summed
             result = blended + speed[b] * jnp.tanh(blended)
-            if step < STEPS - 1:
-                wide_ref[:, middle] = result
-                target[:, middle] = result.astype(jnp.bfloat16)
-            else:
-                patch = (first + RIM - HALO) // PATCH_CELLS
-                for half in range(BLOCK // PATCH_CELLS):
-                    piece = result[:, half * PATCH_CELLS : (half + 1) * PATCH_CELLS]
-                    out_ref[patch + half] = piece.astype(jnp.bfloat16)
+            wide_ref[:, middle] = result
+            target[:, middle] = result.astype(jnp.bfloat16)
         source, target = target, source
+    member = lax.axis_index("member")
+    row, core = member // 2, member % 2
+    for shift, own_out in enumerate((own_0, own_1, own_2, own_3)):
+        block = (row + shift) % own_blocks
+        first = pl.multiple_of(block * BLOCK + (HALO - RIM), TILE)
+        middle = pl.ds(pl.multiple_of(block * BLOCK + HALO, TILE), BLOCK)
+        summed = dot_f32(source[:, pl.ds(first, WINDOW)], own_ref[block])
+        kept = 1.0 - (coef_ref[12:13, middle] + coef_ref[13:14, middle])
+        quick = coef_ref[14:15, middle] + coef_ref[15:16, middle]
+        blended = wide_ref[:, middle] * kept + summed
+        result = (blended + quick * jnp.tanh(blended)).astype(jnp.bfloat16)
+        even, odd_half = result[:, :PATCH_CELLS], result[:, PATCH_CELLS:]
+        own_out[...] = jnp.where(core == 0, even, odd_half)
+        swap_ref[shift] = jnp.where(core == 0, odd_half, even)
+
+
+def exchange_shapes(rows):
+    return (pltpu.VMEM((rows, PATCH_CELLS), jnp.bfloat16),) * SHIFTS + (
+        pltpu.VMEM((SHIFTS, rows, PATCH_CELLS), jnp.bfloat16),
+    )
 
 
 def forecast(state, wide_pair, near_pair, own, coef):
@@ -279,9 +315,9 @@
     padded = cells + 2 * HALO
     return pl.pallas_call(
         forecast_kernel,
-        out_shape=pltpu.VMEM((cells // PATCH_CELLS, rows, PATCH_CELLS), jnp.bfloat16),
+        out_shape=exchange_shapes(rows),
         in_specs=vmem(5),
-        out_specs=pl.BlockSpec(memory_space=pltpu.VMEM),
+        out_specs=tuple(vmem(SHIFTS + 1)),
         scratch_shapes=[
             pltpu.VMEM((sides, WINDOW, BLOCK), jnp.bfloat16),
             pltpu.VMEM((COEF_ROWS, padded), jnp.float32),
@@ -294,10 +330,43 @@
     )(*in_vmem(state, wide_pair, near_pair, own, coef))
 
 
-def analysis_kernel(x_ref, message_ref, out_ref, wide_ref, x2_ref, select_ref):
-    members = x_ref.shape[0] // LEVELS
+def merge_kernel(own_1, own_2, own_3, got_ref, out_1, out_2, out_3):
+    for shift, own, out in ((1, own_1, out_1), (2, own_2, out_2), (3, own_3, out_3)):
+        out[0] = own[...]
+        out[1] = got_ref[shift]
+
+
+def exchange(parts, sign):
+    rows = parts[0].shape[0]
+    groups = lax.axis_size("member")
+    got = lax.ppermute(parts[SHIFTS], "member", [(i, i ^ 1) for i in range(groups)])
+    merged = pl.pallas_call(
+        merge_kernel,
+        out_shape=(pltpu.VMEM((2, rows, PATCH_CELLS), jnp.bfloat16),) * (SHIFTS - 1),
+        in_specs=vmem(SHIFTS),
+        out_specs=tuple(vmem(SHIFTS - 1)),
+        compiler_params=pltpu.CompilerParams(vmem_limit_bytes=2 << 20),
+        name="merge",
+    )(*in_vmem(*parts[1:SHIFTS], got))
+    moved = [None] * (SHIFTS - 1)
+    for shift in (2, 1, 3):
+        edges = [(i, (i + sign * 2 * shift) % groups) for i in range(groups)]
+        moved[shift - 1] = lax.ppermute(merged[shift - 1], "member", edges)
+    return parts[0], got, *moved
+
+
+def analysis_kernel(
+    self_ref, got_ref, from_1, from_2, from_3, message_ref, own_0, own_1, own_2, own_3, swap_ref,
+    wide_ref, x2_ref, select_ref,
+):
+    rows = self_ref.shape[0]
+    members = wide_ref.shape[0] // LEVELS
     span = LEVELS * PATCH_CELLS
-    wide_ref[...] = x_ref[...].astype(jnp.float32)
+    arrived = [self_ref[...], got_ref[0]]
+    for ref in (from_1, from_2, from_3):
+        arrived += [ref[0], ref[1]]
+    for i, piece in enumerate(arrived):
+        wide_ref[i * rows : (i + 1) * rows] = piece.astype(jnp.float32)
     for level in range(LEVELS):
         part = wide_ref[pl.ds(level, members, stride=LEVELS), :]
         x2_ref[:, level * PATCH_CELLS : (level + 1) * PATCH_CELLS] = part.astype(jnp.bfloat16)
@@ -361,26 +430,60 @@
         for k in range(pair):
             updated = pieces[k][1] + moved[:, k * PATCH_CELLS : (k + 1) * PATCH_CELLS]
             wide_ref[pl.ds(level + k, members, stride=LEVELS), :] = updated
-    out_ref[...] = wide_ref[...].astype(jnp.bfloat16)
-
-
-def analysis(x, message):
-    rows = x.shape[0]
-    members = rows // LEVELS
+    for shift, own in enumerate((own_0, own_1, own_2, own_3)):
+        first = 2 * shift * rows
+        own[...] = wide_ref[first : first + rows].astype(jnp.bfloat16)
+        swap_ref[shift] = wide_ref[first + rows : first + 2 * rows].astype(jnp.bfloat16)
+
+
+def analysis(received, message):
+    rows = received[0].shape[0]
+    wide = 2 * SHIFTS * rows
+    members = wide // LEVELS
     slots = 2 * message.shape[0]
     return pl.pallas_call(
         analysis_kernel,
-        out_shape=pltpu.VMEM(x.shape, jnp.bfloat16),
-        in_specs=vmem(2),
-        out_specs=pl.BlockSpec(memory_space=pltpu.VMEM),
+        out_shape=exchange_shapes(rows),
+        in_specs=vmem(SHIFTS + 2),
+        out_specs=tuple(vmem(SHIFTS + 1)),
         compiler_params=pltpu.CompilerParams(vmem_limit_bytes=12 << 20),
         scratch_shapes=[
-            pltpu.VMEM((rows, PATCH_CELLS), jnp.float32),
+            pltpu.VMEM((wide, PATCH_CELLS), jnp.float32),
             pltpu.VMEM((members, LEVELS * PATCH_CELLS), jnp.bfloat16),
             pltpu.VMEM((LEVELS * PATCH_CELLS, slots), jnp.bfloat16),
         ],
         name="analysis",
-    )(*in_vmem(x, message))
+    )(*in_vmem(*received, message))
+
+
+def place_kernel(self_ref, got_ref, from_1, from_2, from_3, out_hbm, sem):
+    member = lax.axis_index("member")
+    row, core = member // 2, member % 2
+    copies = []
+    pieces = [self_ref, got_ref.at[0]]
+    for ref in (from_1, from_2, from_3):
+        pieces += [ref.at[0], ref.at[1]]
+    for i, piece in enumerate(pieces):
+        patch = (row + i // 2) % SHIFTS * 2 + (core + i) % 2
+        lanes = pl.ds(pl.multiple_of(patch * PATCH_CELLS, PATCH_CELLS), PATCH_CELLS)
+        copies.append(pltpu.make_async_copy(piece, out_hbm.at[:, lanes], sem.at[i]))
+    for copy in copies:
+        copy.start()
+    for copy in copies:
+        copy.wait()
+
+
+def place(received, cells):
+    rows = received[0].shape[0]
+    return pl.pallas_call(
+        place_kernel,
+        out_shape=jax.ShapeDtypeStruct((rows, cells), jnp.bfloat16),
+        in_specs=vmem(SHIFTS + 1),
+        out_specs=pl.BlockSpec(memory_space=pltpu.HBM),
+        scratch_shapes=[pltpu.SemaphoreType.DMA((2 * SHIFTS,))],
+        compiler_params=pltpu.CompilerParams(vmem_limit_bytes=2 << 20),
+        name="place",
+    )(*in_vmem(*received))
 
 
 def on_device(
@@ -392,25 +495,24 @@
     groups = lax.axis_size("member")
     total = cells * regions
     flat = state.reshape(members * levels, cells)
-    wide_pair, near_pair, kept, coef, message = prepare(
-        flat, adjacent_columns, adjacent_rates, amplification_speed[None, :],
-        obs_patch[None, :], obs_row[None, :], obs_value[None, :], obs_error[None, :],
-        total, regions, groups,
+    wide_pair, near_pair, kept, coef = prepare(
+        flat, adjacent_columns, adjacent_rates, amplification_speed[None, :], total
     )
     pairs = [(i, (i + 1) % regions) for i in range(regions)]
     wide_swap = [edge for i, j in pairs[1::2] for edge in ((i, j), (j, i))]
     near_swap = [edge for i, j in pairs[0::2] for edge in ((i, j), (j, i))]
+    near_pair = lax.ppermute(near_pair, "region", near_swap)
     wide_pair = lax.ppermute(wide_pair, "region", wide_swap)
-    near_pair = lax.ppermute(near_pair, "region", near_swap)
+    message = observation_message(
+        obs_patch[None, :], obs_row[None, :], obs_value[None, :], obs_error[None, :],
+        regions, groups,
+    )
     message = lax.all_to_all(message, ("member", "region"), 0, 0, tiled=True)
     own = own_matrices(coef)
-    rounded = forecast(kept, wide_pair, near_pair, own, coef)
-    patched = lax.all_to_all(rounded, "member", 0, 0, tiled=True)
-    analysed = analysis(patched.reshape(-1, PATCH_CELLS), message)
-    returned = analysed.reshape(groups, members * levels, PATCH_CELLS)
-    back = lax.all_to_all(returned, "member", 0, 0, tiled=True)
-    back = back.reshape(groups, members, levels, PATCH_CELLS)
-    return back.transpose(1, 2, 0, 3).reshape(members, levels, cells)
+    parts = forecast(kept, wide_pair, near_pair, own, coef)
+    received = exchange(parts, 1)
+    back = exchange(analysis(received, message), -1)
+    return place(back, cells).reshape(members, levels, cells)
 
 
 def solution(mesh):
@@ -424,6 +526,7 @@
         P(("member", "region")),
         P(("member", "region")),
     )
+
     return jax.shard_map(
         on_device, mesh=mesh, in_specs=placed, out_specs=P("member", None, "region"), check_vma=False
     )

time: 55.5 us -> 63.1 us (1.14)
  waiting for transfers between devices: 5.53 us -> 19.8 us
  blocking collectives: 25.8 us -> 15.2 us
  starting transfers between devices: 13.6 us -> 17.1 us
  Pallas kernels: 9.45 us -> 10.8 us
  local copies, waits for them, and re-layouts: 0.88 us -> 0 us
    all_to_all x2 -> x1, blocking collectives: 25.8 us -> 15.2 us  [on_device(): message = lax.all_to_all(message, ('member', 'region'), 0, 0, tiled=True)]
    ppermute x0 -> x8, waiting for transfers between devices: none -> 10.5 us  [the longest x6 8.15 us: exchange(): moved[shift - 1] = lax.ppermute(merged[shift - 1], 'member', edges)]
    ppermute x0 -> x8, starting transfers between devices: none -> 10.3 us  [the longest x6 7.26 us: exchange(): moved[shift - 1] = lax.ppermute(merged[shift - 1], 'member', edges)]
    ppermute x1, waiting for transfers between devices: 1.67 us -> 8.43 us  [on_device(): wide_pair = lax.ppermute(wide_pair, 'region', wide_swap)]
    all_to_all x1 -> x0, starting transfers between devices: 6.74 us -> none  [on_device(): message = lax.all_to_all(message, ('member', 'region'), 0, 0, tiled=True)]
    all_to_all x1 -> x0, waiting for transfers between devices: 2.92 us -> none  [on_device(): message = lax.all_to_all(message, ('member', 'region'), 0, 0, tiled=True)]
    pallas_call x3 -> x7, Pallas kernels: 8.53 us -> 9.92 us  [the longest x1 3.29 us: analysis(): pl.pallas_call(analysis_kernel, out_shape=exchange_shapes(rows), in_specs...]
    reshape x1 -> x0, local copies, waits for them, and re-layouts: 0.88 us -> none  [on_device(): return back.transpose(1, 2, 0, 3).reshape(members, levels, cells)]
  transfers between devices with their start and end apart: 3 -> 10, of which waited for: 3 -> 7; matrix products, arithmetic and copies ran while one was open for 0% -> 0% of each run, Pallas kernels for 7% -> 3%
where the time goes in v3:
time: 63.1 us; the launch traced here: 63 us
  waiting for transfers between devices  19.8 us (31%)
  starting transfers between devices  17.1 us (27%)
  blocking collectives  15.2 us (24%)
  Pallas kernels  10.8 us (17%)
    all_to_all x1, blocking collectives, on_device(): message = lax.all_to_all(message, ('member', 'region'), 0, 0, tiled=True)  15.2 us
    ppermute x1, waiting for transfers between devices, on_device(): wide_pair = lax.ppermute(wide_pair, 'region', wide_swap)  8.43 us
    ppermute x6, waiting for transfers between devices, exchange(): moved[shift - 1] = lax.ppermute(merged[shift - 1], 'member', edges)  8.15 us
    ppermute x6, starting transfers between devices, exchange(): moved[shift - 1] = lax.ppermute(merged[shift - 1], 'member', edges)  7.26 us
    ppermute x1, starting transfers between devices, on_device(): wide_pair = lax.ppermute(wide_pair, 'region', wide_swap)  6.85 us
    pallas_call x1, Pallas kernels, analysis(): pl.pallas_call(analysis_kernel, out_shape=exchange_shapes(rows), in_specs...  3.29 us
    pallas_call x1, Pallas kernels, forecast(): pl.pallas_call(forecast_kernel, out_shape=exchange_shapes(rows), in_specs...  3.24 us
    ppermute x2, starting transfers between devices, exchange(): lax.ppermute(parts[SHIFTS], 'member', [(i, i ^ 1) for i in range(groups)])  2.99 us
  transfers between devices with their start and end apart: 10, of which 7 were waited for; matrix products, arithmetic and copies ran while one was open for 0% of the time, Pallas kernels for 3%

profile of v3, /device:TPU:1, one launch (start us, length us, event | category | flops | bytes accessed | tf_op | source)
XLA Modules:
  0.0 63.0 jit_solution(17209552853972552690)
XLA Ops:
  0.0 1.3 %prepare.1 = (bf16[272,768]{1,0:T(8,128)(2,1)S(1)}, bf16[272,768]{1,0:T(8,128)(2,1)S(1)}, f32[256,1024]{1,0:T(8,128)S(1)}, f32[16,1024]{1,0:T(8,128)S(1)}) custom-call(f32[256,1024]{1,0:T(8,128)} %bitcast.13, s32[6,1024]{1,0:T(8,128)} %column_hbm.1, f32[6,1024]{1,0:T(8,128)} %rate_hbm.1, f32[1,1024]{1,0:T(1,128)} %bitcast.14), custom_call_target="tpu_custom_call" | custom-call | tf_op jit(solution)/shard_map/prepare/pallas_call | solution.py:149
  1.3 6.8 %collective-permute-start = (bf16[272,768]{1,0:T(8,128)(2,1)S(1)}, bf16[272,768]{1,0:T(8,128)(2,1)S(1)}, u32[]{:S(2)}, u32[]{:S(2)}) collective-permute-start(bf16[272,768]{1,0:T(8,128)(2,1)S(1)} %get-tuple-element.26), channel_id=1, source_target_pairs={{1,2},{2,1},{3,4},{4,3},{5,6},{6,5},{7,8},{8,7},{9,10},{10,9},{11,... | collective-permute-start | bytes 1253384 | tf_op jit(solution)/shard_map/ppermute | solution.py:505
  8.2 0.0 collective-permute-start.1
  8.2 0.9 %own_matrices.1.own_ref = bf16[4,768,256]{2,1,0:T(8,128)(2,1)S(1)} custom-call(f32[16,1024]{1,0:T(8,128)S(1)} %get-tuple-element.28.coef_ref.own_coef_ref), custom_call_target="tpu_custom_call" | custom-call | tf_op jit(solution)/shard_map/own_matrices/pallas_call | solution.py:179
  9.1 8.4 %collective-permute-done.wide_pair_ref = bf16[272,768]{1,0:T(8,128)(2,1)S(1)} collective-permute-done((bf16[272,768]{1,0:T(8,128)(2,1)S(1)}, bf16[272,768]{1,0:T(8,128)(2,1)S(1)}, u32[]{:S(2)}, u32[]{:S(2)}) %collective-permute-start) | collective-permute-done | bytes 417824 | tf_op jit(solution)/shard_map/ppermute | solution.py:505
  17.5 0.9 %collective-permute-done.1.near_pair_ref = bf16[272,768]{1,0:T(8,128)(2,1)S(1)} collective-permute-done((bf16[272,768]{1,0:T(8,128)(2,1)S(1)}, bf16[272,768]{1,0:T(8,128)(2,1)S(1)}, u32[]{:S(2)}, u32[]{:S(2)}) %collective-permute-start.1) | collective-permute-done | bytes 417824 | tf_op jit(solution)/shard_map/ppermute | solution.py:504
  18.4 3.2 %forecast.1 = (bf16[256,128]{1,0:T(8,128)(2,1)S(1)}, bf16[256,128]{1,0:T(8,128)(2,1)S(1)}, bf16[256,128]{1,0:T(8,128)(2,1)S(1)}, bf16[256,128]{1,0:T(8,128)(2,1)S(1)}, bf16[4,256,128]{2,1,0:T(8,128)(2,1)S(1)}) custom-call(f32[256,1024]{1,0:T(8,128)S(1)} %get-tuple-element.25.state_ref, bf16[272,768]{1,0:T(8,128)(2,1)S(1)} %collective-permute-done.wide_pair_ref, ...), custom_call_target="tpu_custom_call" | custom-call | tf_op jit(solution)/shard_map/forecast/pallas_call | solution.py:316
  21.7 1.9 %collective-permute-start.2 = (bf16[4,256,128]{2,1,0:T(8,128)(2,1)S(1)}, bf16[4,256,128]{2,1,0:T(8,128)(2,1)S(1)}, u32[]{:S(2)}, u32[]{:S(2)}) collective-permute-start(bf16[4,256,128]{2,1,0:T(8,128)(2,1)S(1)} %get-tuple-element.30), channel_id=1, source_target_pairs={{0,16},{16,0},{32,48},{48,32},{64,80},{80,64},{96,112},{112,96},{1... | collective-permute-start | bytes 786440 | tf_op jit(solution)/shard_map/ppermute | solution.py:342
  23.6 1.2 %collective-permute-done.2.got_ref = bf16[4,256,128]{2,1,0:T(8,128)(2,1)S(1)} collective-permute-done((bf16[4,256,128]{2,1,0:T(8,128)(2,1)S(1)}, bf16[4,256,128]{2,1,0:T(8,128)(2,1)S(1)}, u32[]{:S(2)}, u32[]{:S(2)}) %collective-permute-start.2) | collective-permute-done | bytes 262176 | tf_op jit(solution)/shard_map/ppermute | solution.py:342
  24.8 1.4 %collective-permute-start.3 = (bf16[2,256,128]{2,1,0:T(8,128)(2,1)S(1)}, bf16[2,256,128]{2,1,0:T(8,128)(2,1)S(1)}, u32[]{:S(2)}, u32[]{:S(2)}) collective-permute-start(bf16[2,256,128]{2,1,0:T(8,128)(2,1)S(1)} %get-tuple-element.34), channel_id=1, source_target_pairs={{0,32},{16,48},{32,64},{48,80},{64,96},{80,112},{96,0},{112,16},{1... | collective-permute-start | bytes 393224 | tf_op jit(solution)/shard_map/ppermute | solution.py:354
  26.1 2.6 %collective-permute-start.4 = (bf16[2,256,128]{2,1,0:T(8,128)(2,1)S(1)}, bf16[2,256,128]{2,1,0:T(8,128)(2,1)S(1)}, u32[]{:S(2)}, u32[]{:S(2)}) collective-permute-start(bf16[2,256,128]{2,1,0:T(8,128)(2,1)S(1)} %get-tuple-element.35), channel_id=1, source_target_pairs={{0,64},{16,80},{32,96},{48,112},{64,0},{80,16},{96,32},{112,48},{1... | collective-permute-start | bytes 393224 | tf_op jit(solution)/shard_map/ppermute | solution.py:354
  28.7 1.1 %collective-permute-start.5 = (bf16[2,256,128]{2,1,0:T(8,128)(2,1)S(1)}, bf16[2,256,128]{2,1,0:T(8,128)(2,1)S(1)}, u32[]{:S(2)}, u32[]{:S(2)}) collective-permute-start(bf16[2,256,128]{2,1,0:T(8,128)(2,1)S(1)} %get-tuple-element.36), channel_id=1, source_target_pairs={{0,96},{16,112},{32,0},{48,16},{64,32},{80,48},{96,64},{112,80},{1... | collective-permute-start | bytes 393224 | tf_op jit(solution)/shard_map/ppermute | solution.py:354
  29.8 1.2 %message.1 = f32[128,128]{1,0:T(8,128)S(1)} custom-call(s32[1,256]{1,0:T(1,128)} %bitcast.15, s32[1,256]{1,0:T(1,128)} %bitcast.16, f32[1,256]{1,0:T(1,128)} %bitcast.17, f32[1,256]{1,0:T(1,128)} %bitcast.18), custom_call_target="tpu_custom_call" | custom-call | tf_op jit(solution)/shard_map/message/pallas_call | solution.py:227
  31.0 15.2 %all_to_all.11 = f32[128,1,128]{2,1,0:T(1,128)S(1)} all-to-all(f32[128,1,128]{2,1,0:T(1,128)S(1)} %bitcast.12), channel_id=1, replica_groups=mesh['member'=8,'region'=16] {'member','region'}, dimensions={0} | all-to-all | bytes 131072 | tf_op jit(solution)/shard_map/all_to_all | solution.py:510
  46.1 0.0 collective-permute-done.3.from_1
  46.2 0.0 collective-permute-done.4.from_2
  46.2 0.0 collective-permute-done.5.from_3
  46.2 3.3 %analysis.1 = (bf16[256,128]{1,0:T(8,128)(2,1)S(1)}, bf16[256,128]{1,0:T(8,128)(2,1)S(1)}, bf16[256,128]{1,0:T(8,128)(2,1)S(1)}, bf16[256,128]{1,0:T(8,128)(2,1)S(1)}, bf16[4,256,128]{2,1,0:T(8,128)(2,1)S(1)}) custom-call(bf16[256,128]{1,0:T(8,128)(2,1)S(1)} %get-tuple-element.29.self_ref, bf16[4,256,128]{2,1,0:T(8,128)(2,1)S(1)} %collective-permute-done.2.got_ref, ...), custom_call_target="tpu_custom_call" | custom-call | tf_op jit(solution)/shard_map/analysis/pallas_call | solution.py:444
  49.5 1.1 %collective-permute-start.6 = (bf16[4,256,128]{2,1,0:T(8,128)(2,1)S(1)}, bf16[4,256,128]{2,1,0:T(8,128)(2,1)S(1)}, u32[]{:S(2)}, u32[]{:S(2)}) collective-permute-start(bf16[4,256,128]{2,1,0:T(8,128)(2,1)S(1)} %get-tuple-element.38), channel_id=1, source_target_pairs={{0,16},{16,0},{32,48},{48,32},{64,80},{80,64},{96,112},{112,96},{1... | collective-permute-start | bytes 786440 | tf_op jit(solution)/shard_map/ppermute | solution.py:342
  50.6 1.2 %collective-permute-done.6.got_ref = bf16[4,256,128]{2,1,0:T(8,128)(2,1)S(1)} collective-permute-done((bf16[4,256,128]{2,1,0:T(8,128)(2,1)S(1)}, bf16[4,256,128]{2,1,0:T(8,128)(2,1)S(1)}, u32[]{:S(2)}, u32[]{:S(2)}) %collective-permute-start.6) | collective-permute-done | bytes 262176 | tf_op jit(solution)/shard_map/ppermute | solution.py:342
  51.8 0.9 %collective-permute-start.7 = (bf16[2,256,128]{2,1,0:T(8,128)(2,1)S(1)}, bf16[2,256,128]{2,1,0:T(8,128)(2,1)S(1)}, u32[]{:S(2)}, u32[]{:S(2)}) collective-permute-start(bf16[2,256,128]{2,1,0:T(8,128)(2,1)S(1)} %get-tuple-element.42), channel_id=1, source_target_pairs={{0,96},{16,112},{32,0},{48,16},{64,32},{80,48},{96,64},{112,80},{1... | collective-permute-start | bytes 393224 | tf_op jit(solution)/shard_map/ppermute | solution.py:354
  52.6 1.3 %collective-permute-start.8 = (bf16[2,256,128]{2,1,0:T(8,128)(2,1)S(1)}, bf16[2,256,128]{2,1,0:T(8,128)(2,1)S(1)}, u32[]{:S(2)}, u32[]{:S(2)}) collective-permute-start(bf16[2,256,128]{2,1,0:T(8,128)(2,1)S(1)} %get-tuple-element.43), channel_id=1, source_target_pairs={{0,64},{16,80},{32,96},{48,112},{64,0},{80,16},{96,32},{112,48},{1... | collective-permute-start | bytes 393224 | tf_op jit(solution)/shard_map/ppermute | solution.py:354
  54.0 0.0 collective-permute-start.9
  54.0 2.5 %collective-permute-done.7.from_1 = bf16[2,256,128]{2,1,0:T(8,128)(2,1)S(1)} collective-permute-done((bf16[2,256,128]{2,1,0:T(8,128)(2,1)S(1)}, bf16[2,256,128]{2,1,0:T(8,128)(2,1)S(1)}, u32[]{:S(2)}, u32[]{:S(2)}) %collective-permute-start.7) | collective-permute-done | bytes 131104 | tf_op jit(solution)/shard_map/ppermute | solution.py:354
  56.5 2.0 %collective-permute-done.8.from_2 = bf16[2,256,128]{2,1,0:T(8,128)(2,1)S(1)} collective-permute-done((bf16[2,256,128]{2,1,0:T(8,128)(2,1)S(1)}, bf16[2,256,128]{2,1,0:T(8,128)(2,1)S(1)}, u32[]{:S(2)}, u32[]{:S(2)}) %collective-permute-start.8) | collective-permute-done | bytes 131104 | tf_op jit(solution)/shard_map/ppermute | solution.py:354
  58.5 3.6 %collective-permute-done.9.from_3 = bf16[2,256,128]{2,1,0:T(8,128)(2,1)S(1)} collective-permute-done((bf16[2,256,128]{2,1,0:T(8,128)(2,1)S(1)}, bf16[2,256,128]{2,1,0:T(8,128)(2,1)S(1)}, u32[]{:S(2)}, u32[]{:S(2)}) %collective-permute-start.9) | collective-permute-done | bytes 131104 | tf_op jit(solution)/shard_map/ppermute | solution.py:354
  62.1 0.8 %place.1 = bf16[256,1024]{1,0:T(8,128)(2,1)} custom-call(bf16[256,128]{1,0:T(8,128)(2,1)S(1)} %get-tuple-element.37.self_ref, bf16[4,256,128]{2,1,0:T(8,128)(2,1)S(1)} %collective-permute-done.6.got_ref, bf16[2,256,128]{2,1,0:T(8,128)(2,1)S(1)} %collective-permute-done.7.from_1, bf16[2,256,128]{2,1,0:T(8,128)(2,1)S(1)} %collective-permute-done.8.from_2, ...), custom_call_target="tpu_custom_call" | custom-call | tf_op jit(solution)/shard_map/place/pallas_call | solution.py:478
  (2 shorter events, 0.1 us)
Async XLA Ops:
  1.3 16.2 %collective-permute-start = (bf16[272,768]{1,0:T(8,128)(2,1)S(1)}, bf16[272,768]{1,0:T(8,128)(2,1)S(1)}, u32[]{:S(2)}, u32[]{:S(2)}) collective-permute-start(bf16[272,768]{1,0:T(8,128)(2,1)S(1)} %get-tuple-element.26), channel_id=1, source_target_pairs={{1,2},{2,1},{3,4},{4,3},{5,6},{6,5},{7,8},{8,7},{9,10},{10,9},{11,... | collective-permute-start | bytes 1253384 | tf_op jit(solution)/shard_map/ppermute | solution.py:505
  8.2 10.2 %collective-permute-start.1 = (bf16[272,768]{1,0:T(8,128)(2,1)S(1)}, bf16[272,768]{1,0:T(8,128)(2,1)S(1)}, u32[]{:S(2)}, u32[]{:S(2)}) collective-permute-start(bf16[272,768]{1,0:T(8,128)(2,1)S(1)} %get-tuple-element.27), channel_id=1, source_target_pairs={{0,1},{1,0},{2,3},{3,2},{4,5},{5,4},{6,7},{7,6},{8,9},{9,8},{10,11... | collective-permute-start | bytes 1253384 | tf_op jit(solution)/shard_map/ppermute | solution.py:504
  21.7 3.1 %collective-permute-start.2 = (bf16[4,256,128]{2,1,0:T(8,128)(2,1)S(1)}, bf16[4,256,128]{2,1,0:T(8,128)(2,1)S(1)}, u32[]{:S(2)}, u32[]{:S(2)}) collective-permute-start(bf16[4,256,128]{2,1,0:T(8,128)(2,1)S(1)} %get-tuple-element.30), channel_id=1, source_target_pairs={{0,16},{16,0},{32,48},{48,32},{64,80},{80,64},{96,112},{112,96},{1... | collective-permute-start | bytes 786440 | tf_op jit(solution)/shard_map/ppermute | solution.py:342
  24.8 21.4 %collective-permute-start.3 = (bf16[2,256,128]{2,1,0:T(8,128)(2,1)S(1)}, bf16[2,256,128]{2,1,0:T(8,128)(2,1)S(1)}, u32[]{:S(2)}, u32[]{:S(2)}) collective-permute-start(bf16[2,256,128]{2,1,0:T(8,128)(2,1)S(1)} %get-tuple-element.34), channel_id=1, source_target_pairs={{0,32},{16,48},{32,64},{48,80},{64,96},{80,112},{96,0},{112,16},{1... | collective-permute-start | bytes 393224 | tf_op jit(solution)/shard_map/ppermute | solution.py:354
  26.1 20.0 %collective-permute-start.4 = (bf16[2,256,128]{2,1,0:T(8,128)(2,1)S(1)}, bf16[2,256,128]{2,1,0:T(8,128)(2,1)S(1)}, u32[]{:S(2)}, u32[]{:S(2)}) collective-permute-start(bf16[2,256,128]{2,1,0:T(8,128)(2,1)S(1)} %get-tuple-element.35), channel_id=1, source_target_pairs={{0,64},{16,80},{32,96},{48,112},{64,0},{80,16},{96,32},{112,48},{1... | collective-permute-start | bytes 393224 | tf_op jit(solution)/shard_map/ppermute | solution.py:354
  28.7 17.4 %collective-permute-start.5 = (bf16[2,256,128]{2,1,0:T(8,128)(2,1)S(1)}, bf16[2,256,128]{2,1,0:T(8,128)(2,1)S(1)}, u32[]{:S(2)}, u32[]{:S(2)}) collective-permute-start(bf16[2,256,128]{2,1,0:T(8,128)(2,1)S(1)} %get-tuple-element.36), channel_id=1, source_target_pairs={{0,96},{16,112},{32,0},{48,16},{64,32},{80,48},{96,64},{112,80},{1... | collective-permute-start | bytes 393224 | tf_op jit(solution)/shard_map/ppermute | solution.py:354
  49.5 2.3 %collective-permute-start.6 = (bf16[4,256,128]{2,1,0:T(8,128)(2,1)S(1)}, bf16[4,256,128]{2,1,0:T(8,128)(2,1)S(1)}, u32[]{:S(2)}, u32[]{:S(2)}) collective-permute-start(bf16[4,256,128]{2,1,0:T(8,128)(2,1)S(1)} %get-tuple-element.38), channel_id=1, source_target_pairs={{0,16},{16,0},{32,48},{48,32},{64,80},{80,64},{96,112},{112,96},{1... | collective-permute-start | bytes 786440 | tf_op jit(solution)/shard_map/ppermute | solution.py:342
  51.8 4.8 %collective-permute-start.7 = (bf16[2,256,128]{2,1,0:T(8,128)(2,1)S(1)}, bf16[2,256,128]{2,1,0:T(8,128)(2,1)S(1)}, u32[]{:S(2)}, u32[]{:S(2)}) collective-permute-start(bf16[2,256,128]{2,1,0:T(8,128)(2,1)S(1)} %get-tuple-element.42), channel_id=1, source_target_pairs={{0,96},{16,112},{32,0},{48,16},{64,32},{80,48},{96,64},{112,80},{1... | collective-permute-start | bytes 393224 | tf_op jit(solution)/shard_map/ppermute | solution.py:354
  52.6 5.9 %collective-permute-start.8 = (bf16[2,256,128]{2,1,0:T(8,128)(2,1)S(1)}, bf16[2,256,128]{2,1,0:T(8,128)(2,1)S(1)}, u32[]{:S(2)}, u32[]{:S(2)}) collective-permute-start(bf16[2,256,128]{2,1,0:T(8,128)(2,1)S(1)} %get-tuple-element.43), channel_id=1, source_target_pairs={{0,64},{16,80},{32,96},{48,112},{64,0},{80,16},{96,32},{112,48},{1... | collective-permute-start | bytes 393224 | tf_op jit(solution)/shard_map/ppermute | solution.py:354
  54.0 8.2 %collective-permute-start.9 = (bf16[2,256,128]{2,1,0:T(8,128)(2,1)S(1)}, bf16[2,256,128]{2,1,0:T(8,128)(2,1)S(1)}, u32[]{:S(2)}, u32[]{:S(2)}) collective-permute-start(bf16[2,256,128]{2,1,0:T(8,128)(2,1)S(1)} %get-tuple-element.44), channel_id=1, source_target_pairs={{0,32},{16,48},{32,64},{48,80},{64,96},{80,112},{96,0},{112,16},{1... | collective-permute-start | bytes 393224 | tf_op jit(solution)/shard_map/ppermute | solution.py:354

commit v4 on v3

--- a/solution.py
+++ b/solution.py
@@ -82,12 +82,18 @@
 
 
 def prepare_kernel(
-    state_hbm, column_hbm, rate_hbm, speed_hbm, wide_pair_ref, near_pair_ref, state_ref, coef_ref,
-    column_ref, rate_ref, speed_ref, small_sem, state_sem, *, total,
+    state_hbm, column_hbm, rate_hbm, speed_hbm, patch_hbm, row_hbm, value_hbm, error_hbm,
+    up_ref, down_ref, state_ref, coef_ref, patch_ref, row_ref, value_ref, error_ref,
+    column_ref, rate_ref, speed_ref, small_sem, later_sem, state_sem, *, total,
 ):
     rows, cells = state_ref.shape
     small = fetches(
         (column_hbm, rate_hbm, speed_hbm), (column_ref, rate_ref, speed_ref), small_sem
+    )
+    later = fetches(
+        (patch_hbm, row_hbm, value_hbm, error_hbm),
+        (patch_ref, row_ref, value_ref, error_ref),
+        later_sem,
     )
     chunk = rows // STATE_CHUNKS
     large = [
@@ -98,15 +104,12 @@
         )
         for i in range(STATE_CHUNKS)
     ]
-    for copy in small + large:
+    for copy in small + large + later:
         copy.start()
     for copy in small:
         copy.wait()
     region = lax.axis_index("region")
-    odd = region % 2
     last = cells - HALO
-    wide_first = pl.multiple_of(odd * last, TILE)
-    near_first = pl.multiple_of((1 - odd) * last, TILE)
     offsets = cell_offsets(column_ref[...], region * cells, total).astype(jnp.float32)
     rates = rate_ref[...]
     rate_sum = jnp.sum(rates, axis=0, keepdims=True)
@@ -122,13 +125,15 @@
         ],
         axis=0,
     )
-    wide_pair_ref[rows:] = coef_ref[:, pl.ds(wide_first, HALO)].astype(jnp.bfloat16)
-    near_pair_ref[rows:] = coef_ref[:, pl.ds(near_first, HALO)].astype(jnp.bfloat16)
+    up_ref[rows:] = coef_ref[:, last:].astype(jnp.bfloat16)
+    down_ref[rows:] = coef_ref[:, :HALO].astype(jnp.bfloat16)
     for i, copy in enumerate(large):
         copy.wait()
         part = pl.ds(i * chunk, chunk)
-        wide_pair_ref[part] = state_ref[part, pl.ds(wide_first, HALO)].astype(jnp.bfloat16)
-        near_pair_ref[part] = state_ref[part, pl.ds(near_first, HALO)].astype(jnp.bfloat16)
+        up_ref[part] = state_ref[part, last:].astype(jnp.bfloat16)
+        down_ref[part] = state_ref[part, :HALO].astype(jnp.bfloat16)
+    for copy in later:
+        copy.wait()
 
 
 def vmem(count):
@@ -143,7 +148,7 @@
     return [pltpu.with_memory_space_constraint(value, pltpu.HBM) for value in values]
 
 
-def prepare(state, columns, rates, speed, total):
+def prepare(state, columns, rates, speed, patch, row, value, error, total):
     rows, cells = state.shape
     side = pltpu.VMEM((rows + COEF_ROWS, HALO), jnp.bfloat16)
     return pl.pallas_call(
@@ -153,19 +158,21 @@
             side,
             pltpu.VMEM((rows, cells), jnp.float32),
             pltpu.VMEM((COEF_ROWS, cells), jnp.float32),
+            *(pltpu.VMEM(item.shape, item.dtype) for item in (patch, row, value, error)),
         ),
-        in_specs=[pl.BlockSpec(memory_space=pltpu.HBM)] * 4,
-        out_specs=tuple(vmem(4)),
+        in_specs=[pl.BlockSpec(memory_space=pltpu.HBM)] * 8,
+        out_specs=tuple(vmem(8)),
         scratch_shapes=[
             pltpu.VMEM(columns.shape, jnp.int32),
             pltpu.VMEM(rates.shape, jnp.float32),
             pltpu.VMEM(speed.shape, jnp.float32),
             pltpu.SemaphoreType.DMA((3,)),
+            pltpu.SemaphoreType.DMA((4,)),
             pltpu.SemaphoreType.DMA((STATE_CHUNKS,)),
         ],
         compiler_params=pltpu.CompilerParams(vmem_limit_bytes=8 << 20),
         name="prepare",
-    )(*in_hbm(state, columns, rates, speed))
+    )(*in_hbm(state, columns, rates, speed, patch, row, value, error))
 
 
 def matrices_kernel(coef_ref, matrix_ref):
@@ -186,17 +193,7 @@
     )(*in_vmem(coef))
 
 
-def message_kernel(
-    patch_hbm, row_hbm, value_hbm, error_hbm, message_ref,
-    patch_ref, row_ref, value_ref, error_ref, sem, *, regions, groups,
-):
-    small = fetches(
-        (patch_hbm, row_hbm, value_hbm, error_hbm), (patch_ref, row_ref, value_ref, error_ref), sem
-    )
-    for copy in small:
-        copy.start()
-    for copy in small:
-        copy.wait()
+def message_kernel(patch_ref, row_ref, value_ref, error_ref, message_ref, *, regions, groups):
     devices, count = message_ref.shape[0], patch_ref.shape[1]
     target = lax.broadcasted_iota(jnp.int32, (devices, count), 0)
     wanted = target % regions * groups + target // regions
@@ -223,38 +220,28 @@
 
 
 def observation_message(patch, row, value, error, regions, groups):
-    count = patch.shape[1]
     return pl.pallas_call(
         functools.partial(message_kernel, regions=regions, groups=groups),
         out_shape=jax.ShapeDtypeStruct((regions * groups, TILE), jnp.float32),
-        in_specs=[pl.BlockSpec(memory_space=pltpu.HBM)] * 4,
+        in_specs=vmem(4),
         out_specs=vmem(1)[0],
-        scratch_shapes=[
-            pltpu.VMEM((1, count), jnp.int32),
-            pltpu.VMEM((1, count), jnp.int32),
-            pltpu.VMEM((1, count), jnp.float32),
-            pltpu.VMEM((1, count), jnp.float32),
-            pltpu.SemaphoreType.DMA((4,)),
-        ],
         compiler_params=pltpu.CompilerParams(vmem_limit_bytes=4 << 20),
         name="message",
-    )(*in_hbm(patch, row, value, error))
+    )(*in_vmem(patch, row, value, error))
 
 
 def forecast_kernel(
-    state_ref, wide_pair_ref, near_pair_ref, own_ref, own_coef_ref, own_0, own_1, own_2, own_3,
+    state_ref, left_ref, right_ref, own_ref, own_coef_ref, own_0, own_1, own_2, own_3,
     swap_ref, matrix_ref, coef_ref, field_a, field_b, wide_ref,
 ):
     rows, cells = state_ref.shape
     own_blocks = cells // BLOCK
     side_blocks = (STEPS - 1) * RIM // BLOCK
     blocks = own_blocks + 2 * side_blocks
-    odd = lax.axis_index("region") % 2
     far = HALO + cells
-    for ref, begin in ((wide_pair_ref, odd * far), (near_pair_ref, (1 - odd) * far)):
-        begin = pl.multiple_of(begin, TILE)
-        coef_ref[:, pl.ds(begin, HALO)] = ref[rows:].astype(jnp.float32)
-        field_a[:, pl.ds(begin, HALO)] = ref[:rows]
+    for ref, begin in ((left_ref, 0), (right_ref, far)):
+        coef_ref[:, begin : begin + HALO] = ref[rows:].astype(jnp.float32)
+        field_a[:, begin : begin + HALO] = ref[:rows]
     coef_ref[:, HALO:far] = own_coef_ref[...]
     field_a[:, HALO:far] = state_ref[...].astype(jnp.bfloat16)
     keep, speed, matrices = [], [], []
@@ -309,7 +296,7 @@
     )
 
 
-def forecast(state, wide_pair, near_pair, own, coef):
+def forecast(state, left, right, own, coef):
     rows, cells = state.shape
     sides = 2 * (STEPS - 1) * RIM // BLOCK
     padded = cells + 2 * HALO
@@ -327,7 +314,7 @@
         ],
         compiler_params=pltpu.CompilerParams(vmem_limit_bytes=16 << 20),
         name="forecast",
-    )(*in_vmem(state, wide_pair, near_pair, own, coef))
+    )(*in_vmem(state, left, right, own, coef))
 
 
 def merge_kernel(own_1, own_2, own_3, got_ref, out_1, out_2, out_3):
@@ -495,23 +482,20 @@
     groups = lax.axis_size("member")
     total = cells * regions
     flat = state.reshape(members * levels, cells)
-    wide_pair, near_pair, kept, coef = prepare(
-        flat, adjacent_columns, adjacent_rates, amplification_speed[None, :], total
-    )
-    pairs = [(i, (i + 1) % regions) for i in range(regions)]
-    wide_swap = [edge for i, j in pairs[1::2] for edge in ((i, j), (j, i))]
-    near_swap = [edge for i, j in pairs[0::2] for edge in ((i, j), (j, i))]
-    near_pair = lax.ppermute(near_pair, "region", near_swap)
-    wide_pair = lax.ppermute(wide_pair, "region", wide_swap)
-    message = observation_message(
-        obs_patch[None, :], obs_row[None, :], obs_value[None, :], obs_error[None, :],
-        regions, groups,
-    )
+    up_part, down_part, kept, coef, *observed = prepare(
+        flat, adjacent_columns, adjacent_rates, amplification_speed[None, :],
+        obs_patch[None, :], obs_row[None, :], obs_value[None, :], obs_error[None, :], total,
+    )
+    up = [(i, (i + 1) % regions) for i in range(regions)]
+    left = lax.ppermute(up_part, "region", up)
+    right = lax.ppermute(down_part, "region", [(j, i) for i, j in up])
+    message = observation_message(*observed, regions, groups)
     message = lax.all_to_all(message, ("member", "region"), 0, 0, tiled=True)
     own = own_matrices(coef)
-    parts = forecast(kept, wide_pair, near_pair, own, coef)
+    parts = forecast(kept, left, right, own, coef)
     received = exchange(parts, 1)
-    back = exchange(analysis(received, message), -1)
+    parts = analysis(received, message)
+    back = exchange(parts, -1)
     return place(back, cells).reshape(members, levels, cells)
 
 

time: 63.1 us -> 62.4 us (0.989)
  blocking collectives: 15.2 us -> 16.7 us
  waiting for transfers between devices: 19.8 us -> 18.8 us
  Pallas kernels: 10.8 us -> 10.1 us
    all_to_all x1, blocking collectives: 15.2 us -> 16.7 us  [on_device(): message = lax.all_to_all(message, ('member', 'region'), 0, 0, tiled=True)]
    ppermute x2, waiting for transfers between devices: 9.33 us -> 8.35 us  [the longest x1 8.35 us: on_device(): left = lax.ppermute(up_part, 'region', up)]
    pallas_call x1, Pallas kernels: 1.18 us -> 0.41 us  [observation_message(): pl.pallas_call(functools.partial(message_kernel, regions=regions, groups=...]
  transfers between devices with their start and end apart: 10 -> 10, of which waited for: 7 -> 6; matrix products, arithmetic and copies ran while one was open for 0% -> 0% of each run, Pallas kernels for 3% -> 2%
where the time goes in v4:
time: 62.4 us; the launch traced here: 62.3 us
  waiting for transfers between devices  18.8 us (30%)
  blocking collectives  16.7 us (27%)
  starting transfers between devices  16.6 us (27%)
  Pallas kernels  10.1 us (16%)
    all_to_all x1, blocking collectives, on_device(): message = lax.all_to_all(message, ('member', 'region'), 0, 0, tiled=True)  16.7 us
    ppermute x1, waiting for transfers between devices, on_device(): left = lax.ppermute(up_part, 'region', up)  8.35 us
    ppermute x6, waiting for transfers between devices, exchange(): moved[shift - 1] = lax.ppermute(merged[shift - 1], 'member', edges)  8.15 us
    ppermute x6, starting transfers between devices, exchange(): moved[shift - 1] = lax.ppermute(merged[shift - 1], 'member', edges)  7.26 us
    ppermute x1, starting transfers between devices, on_device(): right = lax.ppermute(down_part, 'region', [(j, i) for i, j in up])  4.4 us
    pallas_call x1, Pallas kernels, analysis(): pl.pallas_call(analysis_kernel, out_shape=exchange_shapes(rows), in_specs...  3.29 us
    pallas_call x1, Pallas kernels, forecast(): pl.pallas_call(forecast_kernel, out_shape=exchange_shapes(rows), in_specs...  3.21 us
    ppermute x1, starting transfers between devices, on_device(): left = lax.ppermute(up_part, 'region', up)  2.52 us
  transfers between devices with their start and end apart: 10, of which 6 were waited for; matrix products, arithmetic and copies ran while one was open for 0% of the time, Pallas kernels for 2%

profile of v4, /device:TPU:1, one launch (start us, length us, event | category | flops | bytes accessed | tf_op | source)
XLA Modules:
  0.0 62.3 jit_solution(9069855027957983396)
XLA Ops:
  0.0 1.4 %prepare.1 = (bf16[272,768]{1,0:T(8,128)(2,1)S(1)}, bf16[272,768]{1,0:T(8,128)(2,1)S(1)}, f32[256,1024]{1,0:T(8,128)S(1)}, f32[16,1024]{1,0:T(8,128)S(1)}, s32[1...) custom-call(f32[256,1024]{1,0:T(8,128)} %bitcast.13, ...), custom_call_target="tpu_custom_call" | custom-call | tf_op jit(solution)/shard_map/prepare/pallas_call | solution.py:154
  1.4 2.5 %collective-permute-start = (bf16[272,768]{1,0:T(8,128)(2,1)S(1)}, bf16[272,768]{1,0:T(8,128)(2,1)S(1)}, u32[]{:S(2)}, u32[]{:S(2)}) collective-permute-start(bf16[272,768]{1,0:T(8,128)(2,1)S(1)} %get-tuple-element.30), channel_id=1, source_target_pairs={{0,1},{1,2},{2,3},{3,4},{4,5},{5,6},{6,7},{7,8},{8,9},{9,10},{10,1... | collective-permute-start | bytes 1253384 | tf_op jit(solution)/shard_map/ppermute | solution.py:490
  3.9 4.4 %collective-permute-start.1 = (bf16[272,768]{1,0:T(8,128)(2,1)S(1)}, bf16[272,768]{1,0:T(8,128)(2,1)S(1)}, u32[]{:S(2)}, u32[]{:S(2)}) collective-permute-start(bf16[272,768]{1,0:T(8,128)(2,1)S(1)} %get-tuple-element.31), channel_id=1, source_target_pairs={{1,0},{2,1},{3,2},{4,3},{5,4},{6,5},{7,6},{8,7},{9,8},{10,9},{11,1... | collective-permute-start | bytes 1253384 | tf_op jit(solution)/shard_map/ppermute | solution.py:491
  8.3 0.9 %own_matrices.1.own_ref = bf16[4,768,256]{2,1,0:T(8,128)(2,1)S(1)} custom-call(f32[16,1024]{1,0:T(8,128)S(1)} %get-tuple-element.32.coef_ref.own_coef_ref), custom_call_target="tpu_custom_call" | custom-call | tf_op jit(solution)/shard_map/own_matrices/pallas_call | solution.py:186
  9.2 8.3 %collective-permute-done.left_ref = bf16[272,768]{1,0:T(8,128)(2,1)S(1)} collective-permute-done((bf16[272,768]{1,0:T(8,128)(2,1)S(1)}, bf16[272,768]{1,0:T(8,128)(2,1)S(1)}, u32[]{:S(2)}, u32[]{:S(2)}) %collective-permute-start) | collective-permute-done | bytes 417824 | tf_op jit(solution)/shard_map/ppermute | solution.py:490
  17.6 0.0 collective-permute-done.1.right_ref
  17.6 3.2 %forecast.1 = (bf16[256,128]{1,0:T(8,128)(2,1)S(1)}, bf16[256,128]{1,0:T(8,128)(2,1)S(1)}, bf16[256,128]{1,0:T(8,128)(2,1)S(1)}, bf16[256,128]{1,0:T(8,128)(2,1)S(1)}, bf16[4,256,128]{2,1,0:T(8,128)(2,1)S(1)}) custom-call(f32[256,1024]{1,0:T(8,128)S(1)} %get-tuple-element.29.state_ref, bf16[272,768]{1,0:T(8,128)(2,1)S(1)} %collective-permute-done.left_ref, ...), custom_call_target="tpu_custom_call" | custom-call | tf_op jit(solution)/shard_map/forecast/pallas_call | solution.py:303
  20.8 1.3 %collective-permute-start.2 = (bf16[4,256,128]{2,1,0:T(8,128)(2,1)S(1)}, bf16[4,256,128]{2,1,0:T(8,128)(2,1)S(1)}, u32[]{:S(2)}, u32[]{:S(2)}) collective-permute-start(bf16[4,256,128]{2,1,0:T(8,128)(2,1)S(1)} %get-tuple-element.34), channel_id=1, source_target_pairs={{0,16},{16,0},{32,48},{48,32},{64,80},{80,64},{96,112},{112,96},{1... | collective-permute-start | bytes 786440 | tf_op jit(solution)/shard_map/ppermute | solution.py:329
  22.1 1.2 %collective-permute-done.2.got_ref = bf16[4,256,128]{2,1,0:T(8,128)(2,1)S(1)} collective-permute-done((bf16[4,256,128]{2,1,0:T(8,128)(2,1)S(1)}, bf16[4,256,128]{2,1,0:T(8,128)(2,1)S(1)}, u32[]{:S(2)}, u32[]{:S(2)}) %collective-permute-start.2) | collective-permute-done | bytes 262176 | tf_op jit(solution)/shard_map/ppermute | solution.py:329
  23.3 1.4 %collective-permute-start.3 = (bf16[2,256,128]{2,1,0:T(8,128)(2,1)S(1)}, bf16[2,256,128]{2,1,0:T(8,128)(2,1)S(1)}, u32[]{:S(2)}, u32[]{:S(2)}) collective-permute-start(bf16[2,256,128]{2,1,0:T(8,128)(2,1)S(1)} %get-tuple-element.38), channel_id=1, source_target_pairs={{0,32},{16,48},{32,64},{48,80},{64,96},{80,112},{96,0},{112,16},{1... | collective-permute-start | bytes 393224 | tf_op jit(solution)/shard_map/ppermute | solution.py:341
  24.7 2.6 %collective-permute-start.4 = (bf16[2,256,128]{2,1,0:T(8,128)(2,1)S(1)}, bf16[2,256,128]{2,1,0:T(8,128)(2,1)S(1)}, u32[]{:S(2)}, u32[]{:S(2)}) collective-permute-start(bf16[2,256,128]{2,1,0:T(8,128)(2,1)S(1)} %get-tuple-element.39), channel_id=1, source_target_pairs={{0,64},{16,80},{32,96},{48,112},{64,0},{80,16},{96,32},{112,48},{1... | collective-permute-start | bytes 393224 | tf_op jit(solution)/shard_map/ppermute | solution.py:341
  27.3 1.1 %collective-permute-start.5 = (bf16[2,256,128]{2,1,0:T(8,128)(2,1)S(1)}, bf16[2,256,128]{2,1,0:T(8,128)(2,1)S(1)}, u32[]{:S(2)}, u32[]{:S(2)}) collective-permute-start(bf16[2,256,128]{2,1,0:T(8,128)(2,1)S(1)} %get-tuple-element.40), channel_id=1, source_target_pairs={{0,96},{16,112},{32,0},{48,16},{64,32},{80,48},{96,64},{112,80},{1... | collective-permute-start | bytes 393224 | tf_op jit(solution)/shard_map/ppermute | solution.py:341
  28.4 0.4 message.1
  28.8 16.7 %all_to_all.11 = f32[128,1,128]{2,1,0:T(1,128)S(1)} all-to-all(f32[128,1,128]{2,1,0:T(1,128)S(1)} %bitcast.12), channel_id=1, replica_groups=mesh['member'=8,'region'=16] {'member','region'}, dimensions={0} | all-to-all | bytes 131072 | tf_op jit(solution)/shard_map/all_to_all | solution.py:493
  45.5 0.0 collective-permute-done.3.from_1
  45.5 0.0 collective-permute-done.4.from_2
  45.5 0.0 collective-permute-done.5.from_3
  45.5 3.3 %analysis.1 = (bf16[256,128]{1,0:T(8,128)(2,1)S(1)}, bf16[256,128]{1,0:T(8,128)(2,1)S(1)}, bf16[256,128]{1,0:T(8,128)(2,1)S(1)}, bf16[256,128]{1,0:T(8,128)(2,1)S(1)}, bf16[4,256,128]{2,1,0:T(8,128)(2,1)S(1)}) custom-call(bf16[256,128]{1,0:T(8,128)(2,1)S(1)} %get-tuple-element.33.self_ref, bf16[4,256,128]{2,1,0:T(8,128)(2,1)S(1)} %collective-permute-done.2.got_ref, ...), custom_call_target="tpu_custom_call" | custom-call | tf_op jit(solution)/shard_map/analysis/pallas_call | solution.py:431
  48.8 1.1 %collective-permute-start.6 = (bf16[4,256,128]{2,1,0:T(8,128)(2,1)S(1)}, bf16[4,256,128]{2,1,0:T(8,128)(2,1)S(1)}, u32[]{:S(2)}, u32[]{:S(2)}) collective-permute-start(bf16[4,256,128]{2,1,0:T(8,128)(2,1)S(1)} %get-tuple-element.46), channel_id=1, source_target_pairs={{0,16},{16,0},{32,48},{48,32},{64,80},{80,64},{96,112},{112,96},{1... | collective-permute-start | bytes 786440 | tf_op jit(solution)/shard_map/ppermute | solution.py:329
  49.9 1.2 %collective-permute-done.6.got_ref = bf16[4,256,128]{2,1,0:T(8,128)(2,1)S(1)} collective-permute-done((bf16[4,256,128]{2,1,0:T(8,128)(2,1)S(1)}, bf16[4,256,128]{2,1,0:T(8,128)(2,1)S(1)}, u32[]{:S(2)}, u32[]{:S(2)}) %collective-permute-start.6) | collective-permute-done | bytes 262176 | tf_op jit(solution)/shard_map/ppermute | solution.py:329
  51.1 0.9 %collective-permute-start.7 = (bf16[2,256,128]{2,1,0:T(8,128)(2,1)S(1)}, bf16[2,256,128]{2,1,0:T(8,128)(2,1)S(1)}, u32[]{:S(2)}, u32[]{:S(2)}) collective-permute-start(bf16[2,256,128]{2,1,0:T(8,128)(2,1)S(1)} %get-tuple-element.50), channel_id=1, source_target_pairs={{0,96},{16,112},{32,0},{48,16},{64,32},{80,48},{96,64},{112,80},{1... | collective-permute-start | bytes 393224 | tf_op jit(solution)/shard_map/ppermute | solution.py:341
  52.0 1.3 %collective-permute-start.8 = (bf16[2,256,128]{2,1,0:T(8,128)(2,1)S(1)}, bf16[2,256,128]{2,1,0:T(8,128)(2,1)S(1)}, u32[]{:S(2)}, u32[]{:S(2)}) collective-permute-start(bf16[2,256,128]{2,1,0:T(8,128)(2,1)S(1)} %get-tuple-element.51), channel_id=1, source_target_pairs={{0,64},{16,80},{32,96},{48,112},{64,0},{80,16},{96,32},{112,48},{1... | collective-permute-start | bytes 393224 | tf_op jit(solution)/shard_map/ppermute | solution.py:341
  53.3 0.0 collective-permute-start.9
  53.3 2.5 %collective-permute-done.7.from_1 = bf16[2,256,128]{2,1,0:T(8,128)(2,1)S(1)} collective-permute-done((bf16[2,256,128]{2,1,0:T(8,128)(2,1)S(1)}, bf16[2,256,128]{2,1,0:T(8,128)(2,1)S(1)}, u32[]{:S(2)}, u32[]{:S(2)}) %collective-permute-start.7) | collective-permute-done | bytes 131104 | tf_op jit(solution)/shard_map/ppermute | solution.py:341
  55.9 2.0 %collective-permute-done.8.from_2 = bf16[2,256,128]{2,1,0:T(8,128)(2,1)S(1)} collective-permute-done((bf16[2,256,128]{2,1,0:T(8,128)(2,1)S(1)}, bf16[2,256,128]{2,1,0:T(8,128)(2,1)S(1)}, u32[]{:S(2)}, u32[]{:S(2)}) %collective-permute-start.8) | collective-permute-done | bytes 131104 | tf_op jit(solution)/shard_map/ppermute | solution.py:341
  57.9 3.6 %collective-permute-done.9.from_3 = bf16[2,256,128]{2,1,0:T(8,128)(2,1)S(1)} collective-permute-done((bf16[2,256,128]{2,1,0:T(8,128)(2,1)S(1)}, bf16[2,256,128]{2,1,0:T(8,128)(2,1)S(1)}, u32[]{:S(2)}, u32[]{:S(2)}) %collective-permute-start.9) | collective-permute-done | bytes 131104 | tf_op jit(solution)/shard_map/ppermute | solution.py:341
  61.5 0.8 %place.1 = bf16[256,1024]{1,0:T(8,128)(2,1)} custom-call(bf16[256,128]{1,0:T(8,128)(2,1)S(1)} %get-tuple-element.45.self_ref, bf16[4,256,128]{2,1,0:T(8,128)(2,1)S(1)} %collective-permute-done.6.got_ref, bf16[2,256,128]{2,1,0:T(8,128)(2,1)S(1)} %collective-permute-done.7.from_1, bf16[2,256,128]{2,1,0:T(8,128)(2,1)S(1)} %collective-permute-done.8.from_2, ...), custom_call_target="tpu_custom_call" | custom-call | tf_op jit(solution)/shard_map/place/pallas_call | solution.py:465
  (2 shorter events, 0.1 us)
Async XLA Ops:
  1.4 16.2 %collective-permute-start = (bf16[272,768]{1,0:T(8,128)(2,1)S(1)}, bf16[272,768]{1,0:T(8,128)(2,1)S(1)}, u32[]{:S(2)}, u32[]{:S(2)}) collective-permute-start(bf16[272,768]{1,0:T(8,128)(2,1)S(1)} %get-tuple-element.30), channel_id=1, source_target_pairs={{0,1},{1,2},{2,3},{3,4},{4,5},{5,6},{6,7},{7,8},{8,9},{9,10},{10,1... | collective-permute-start | bytes 1253384 | tf_op jit(solution)/shard_map/ppermute | solution.py:490
  3.9 13.7 %collective-permute-start.1 = (bf16[272,768]{1,0:T(8,128)(2,1)S(1)}, bf16[272,768]{1,0:T(8,128)(2,1)S(1)}, u32[]{:S(2)}, u32[]{:S(2)}) collective-permute-start(bf16[272,768]{1,0:T(8,128)(2,1)S(1)} %get-tuple-element.31), channel_id=1, source_target_pairs={{1,0},{2,1},{3,2},{4,3},{5,4},{6,5},{7,6},{8,7},{9,8},{10,9},{11,1... | collective-permute-start | bytes 1253384 | tf_op jit(solution)/shard_map/ppermute | solution.py:491
  20.8 2.5 %collective-permute-start.2 = (bf16[4,256,128]{2,1,0:T(8,128)(2,1)S(1)}, bf16[4,256,128]{2,1,0:T(8,128)(2,1)S(1)}, u32[]{:S(2)}, u32[]{:S(2)}) collective-permute-start(bf16[4,256,128]{2,1,0:T(8,128)(2,1)S(1)} %get-tuple-element.34), channel_id=1, source_target_pairs={{0,16},{16,0},{32,48},{48,32},{64,80},{80,64},{96,112},{112,96},{1... | collective-permute-start | bytes 786440 | tf_op jit(solution)/shard_map/ppermute | solution.py:329
  23.3 22.2 %collective-permute-start.3 = (bf16[2,256,128]{2,1,0:T(8,128)(2,1)S(1)}, bf16[2,256,128]{2,1,0:T(8,128)(2,1)S(1)}, u32[]{:S(2)}, u32[]{:S(2)}) collective-permute-start(bf16[2,256,128]{2,1,0:T(8,128)(2,1)S(1)} %get-tuple-element.38), channel_id=1, source_target_pairs={{0,32},{16,48},{32,64},{48,80},{64,96},{80,112},{96,0},{112,16},{1... | collective-permute-start | bytes 393224 | tf_op jit(solution)/shard_map/ppermute | solution.py:341
  24.7 20.8 %collective-permute-start.4 = (bf16[2,256,128]{2,1,0:T(8,128)(2,1)S(1)}, bf16[2,256,128]{2,1,0:T(8,128)(2,1)S(1)}, u32[]{:S(2)}, u32[]{:S(2)}) collective-permute-start(bf16[2,256,128]{2,1,0:T(8,128)(2,1)S(1)} %get-tuple-element.39), channel_id=1, source_target_pairs={{0,64},{16,80},{32,96},{48,112},{64,0},{80,16},{96,32},{112,48},{1... | collective-permute-start | bytes 393224 | tf_op jit(solution)/shard_map/ppermute | solution.py:341
  27.3 18.2 %collective-permute-start.5 = (bf16[2,256,128]{2,1,0:T(8,128)(2,1)S(1)}, bf16[2,256,128]{2,1,0:T(8,128)(2,1)S(1)}, u32[]{:S(2)}, u32[]{:S(2)}) collective-permute-start(bf16[2,256,128]{2,1,0:T(8,128)(2,1)S(1)} %get-tuple-element.40), channel_id=1, source_target_pairs={{0,96},{16,112},{32,0},{48,16},{64,32},{80,48},{96,64},{112,80},{1... | collective-permute-start | bytes 393224 | tf_op jit(solution)/shard_map/ppermute | solution.py:341
  48.8 2.3 %collective-permute-start.6 = (bf16[4,256,128]{2,1,0:T(8,128)(2,1)S(1)}, bf16[4,256,128]{2,1,0:T(8,128)(2,1)S(1)}, u32[]{:S(2)}, u32[]{:S(2)}) collective-permute-start(bf16[4,256,128]{2,1,0:T(8,128)(2,1)S(1)} %get-tuple-element.46), channel_id=1, source_target_pairs={{0,16},{16,0},{32,48},{48,32},{64,80},{80,64},{96,112},{112,96},{1... | collective-permute-start | bytes 786440 | tf_op jit(solution)/shard_map/ppermute | solution.py:329
  51.1 4.8 %collective-permute-start.7 = (bf16[2,256,128]{2,1,0:T(8,128)(2,1)S(1)}, bf16[2,256,128]{2,1,0:T(8,128)(2,1)S(1)}, u32[]{:S(2)}, u32[]{:S(2)}) collective-permute-start(bf16[2,256,128]{2,1,0:T(8,128)(2,1)S(1)} %get-tuple-element.50), channel_id=1, source_target_pairs={{0,96},{16,112},{32,0},{48,16},{64,32},{80,48},{96,64},{112,80},{1... | collective-permute-start | bytes 393224 | tf_op jit(solution)/shard_map/ppermute | solution.py:341
  52.0 5.9 %collective-permute-start.8 = (bf16[2,256,128]{2,1,0:T(8,128)(2,1)S(1)}, bf16[2,256,128]{2,1,0:T(8,128)(2,1)S(1)}, u32[]{:S(2)}, u32[]{:S(2)}) collective-permute-start(bf16[2,256,128]{2,1,0:T(8,128)(2,1)S(1)} %get-tuple-element.51), channel_id=1, source_target_pairs={{0,64},{16,80},{32,96},{48,112},{64,0},{80,16},{96,32},{112,48},{1... | collective-permute-start | bytes 393224 | tf_op jit(solution)/shard_map/ppermute | solution.py:341
  53.3 8.2 %collective-permute-start.9 = (bf16[2,256,128]{2,1,0:T(8,128)(2,1)S(1)}, bf16[2,256,128]{2,1,0:T(8,128)(2,1)S(1)}, u32[]{:S(2)}, u32[]{:S(2)}) collective-permute-start(bf16[2,256,128]{2,1,0:T(8,128)(2,1)S(1)} %get-tuple-element.52), channel_id=1, source_target_pairs={{0,32},{16,48},{32,64},{48,80},{64,96},{80,112},{96,0},{112,16},{1... | collective-permute-start | bytes 393224 | tf_op jit(solution)/shard_map/ppermute | solution.py:341

commit v5 on v4

--- a/solution.py
+++ b/solution.py
@@ -21,6 +21,7 @@
 TILE = 128
 STATE_CHUNKS = 4
 SHIFTS = 4
+REST = (0, 1, 3)
 
 
 def high(value):
@@ -46,32 +47,44 @@
     return jnp.where(offset < -(total // 2), offset + total, offset)
 
 
-def build_matrix(matrix_ref, index, offsets, rates):
+def matrix_tiles(matrix_ref, index, offsets, rates):
+    offset = [offsets[k : k + 1] for k in range(6)]
+    rate = [rates[k : k + 1] for k in range(6)]
+    for k in range(6):
+        for later in range(k + 1, 6):
+            same = offset[later] == offset[k]
+            rate[k] = rate[k] + jnp.where(same, rate[later], 0.0)
+            offset[later] = jnp.where(same, float(-4 * RIM), offset[later])
     zero = jnp.zeros((TILE, TILE), jnp.bfloat16)
     row = lax.broadcasted_iota(jnp.int32, (TILE, TILE), 0).astype(jnp.float32)
     row = row.astype(jnp.bfloat16)
     lane = lax.broadcasted_iota(jnp.int32, (1, TILE), 1).astype(jnp.float32)
     reach = (TILE + 2 * RIM) // TILE
+    steps = []
     for part in range(BLOCK // TILE):
         lanes = slice(part * TILE, (part + 1) * TILE)
-        local = offsets[:, lanes] + (lane + float(RIM))
-        rate = [
-            jnp.broadcast_to(rates[k : k + 1, lanes].astype(jnp.bfloat16), (TILE, TILE))
-            for k in range(6)
-        ]
+        local = [item[:, lanes] + (lane + float(RIM)) for item in offset]
+        spread = [item[:, lanes].astype(jnp.bfloat16) for item in rate]
         for tile in range(WINDOW // TILE):
-            rows = slice(tile * TILE, (tile + 1) * TILE)
-            step = tile - part
-            if step < 0 or step >= reach:
-                matrix_ref[index, rows, lanes] = zero
-                continue
-            total = None
-            for k in range(6):
-                near = (local[k : k + 1] - float(step * TILE)).astype(jnp.bfloat16)
-                hit = row == jnp.broadcast_to(near, (TILE, TILE))
-                term = jnp.where(hit, rate[k], zero)
-                total = term if total is None else total + term
-            matrix_ref[index, rows, lanes] = total
+
+            def write(tile=tile, part=part, lanes=lanes, local=local, spread=spread):
+                rows = slice(tile * TILE, (tile + 1) * TILE)
+                step = tile - part
+                total = zero
+                if 0 <= step < reach:
+                    for k in range(6):
+                        near = (local[k] - float(step * TILE)).astype(jnp.bfloat16)
+                        hit = row == jnp.broadcast_to(near, (TILE, TILE))
+                        total = jnp.where(hit, jnp.broadcast_to(spread[k], (TILE, TILE)), total)
+                matrix_ref[index, rows, lanes] = total
+
+            steps.append(write)
+    return steps
+
+
+def build_matrix(matrix_ref, index, offsets, rates):
+    for step in matrix_tiles(matrix_ref, index, offsets, rates):
+        step()
 
 
 def fetches(sources, targets, sem):
@@ -232,7 +245,7 @@
 
 def forecast_kernel(
     state_ref, left_ref, right_ref, own_ref, own_coef_ref, own_0, own_1, own_2, own_3,
-    swap_ref, matrix_ref, coef_ref, field_a, field_b, wide_ref,
+    first_swap, rest_swap, matrix_ref, coef_ref, field_a, field_b, wide_ref,
 ):
     rows, cells = state_ref.shape
     own_blocks = cells // BLOCK
@@ -287,13 +300,20 @@
         result = (blended + quick * jnp.tanh(blended)).astype(jnp.bfloat16)
         even, odd_half = result[:, :PATCH_CELLS], result[:, PATCH_CELLS:]
         own_out[...] = jnp.where(core == 0, even, odd_half)
-        swap_ref[shift] = jnp.where(core == 0, odd_half, even)
+        store_swap(shift, jnp.where(core == 0, odd_half, even), first_swap, rest_swap)
 
 
 def exchange_shapes(rows):
-    return (pltpu.VMEM((rows, PATCH_CELLS), jnp.bfloat16),) * SHIFTS + (
-        pltpu.VMEM((SHIFTS, rows, PATCH_CELLS), jnp.bfloat16),
-    )
+    return (pltpu.VMEM((rows, PATCH_CELLS), jnp.bfloat16),) * (SHIFTS + 1) + (
+        pltpu.VMEM((len(REST), rows, PATCH_CELLS), jnp.bfloat16),
+    )
+
+
+def store_swap(shift, value, first_ref, rest_ref):
+    if shift in REST:
+        rest_ref[REST.index(shift)] = value
+    else:
+        first_ref[...] = value
 
 
 def forecast(state, left, right, own, coef):
@@ -304,7 +324,7 @@
         forecast_kernel,
         out_shape=exchange_shapes(rows),
         in_specs=vmem(5),
-        out_specs=tuple(vmem(SHIFTS + 1)),
+        out_specs=tuple(vmem(SHIFTS + 2)),
         scratch_shapes=[
             pltpu.VMEM((sides, WINDOW, BLOCK), jnp.bfloat16),
             pltpu.VMEM((COEF_ROWS, padded), jnp.float32),
@@ -317,34 +337,47 @@
     )(*in_vmem(state, left, right, own, coef))
 
 
-def merge_kernel(own_1, own_2, own_3, got_ref, out_1, out_2, out_3):
-    for shift, own, out in ((1, own_1, out_1), (2, own_2, out_2), (3, own_3, out_3)):
+def merge_kernel(own_2, got_ref, out_2):
+    out_2[0] = own_2[...]
+    out_2[1] = got_ref[...]
+
+
+def merge_rest_kernel(own_1, own_3, got_ref, out_1, out_3):
+    for shift, own, out in ((1, own_1, out_1), (3, own_3, out_3)):
         out[0] = own[...]
-        out[1] = got_ref[shift]
+        out[1] = got_ref[REST.index(shift)]
+
+
+def merge(kernel, *parts):
+    rows = parts[0].shape[0]
+    count = len(parts) - 1
+    return pl.pallas_call(
+        kernel,
+        out_shape=(pltpu.VMEM((2, rows, PATCH_CELLS), jnp.bfloat16),) * count,
+        in_specs=vmem(count + 1),
+        out_specs=tuple(vmem(count)),
+        compiler_params=pltpu.CompilerParams(vmem_limit_bytes=2 << 20),
+    )(*in_vmem(*parts))
 
 
 def exchange(parts, sign):
-    rows = parts[0].shape[0]
     groups = lax.axis_size("member")
-    got = lax.ppermute(parts[SHIFTS], "member", [(i, i ^ 1) for i in range(groups)])
-    merged = pl.pallas_call(
-        merge_kernel,
-        out_shape=(pltpu.VMEM((2, rows, PATCH_CELLS), jnp.bfloat16),) * (SHIFTS - 1),
-        in_specs=vmem(SHIFTS),
-        out_specs=tuple(vmem(SHIFTS - 1)),
-        compiler_params=pltpu.CompilerParams(vmem_limit_bytes=2 << 20),
-        name="merge",
-    )(*in_vmem(*parts[1:SHIFTS], got))
-    moved = [None] * (SHIFTS - 1)
-    for shift in (2, 1, 3):
+    swap = [(i, i ^ 1) for i in range(groups)]
+    *own, first_swap, rest_swap = parts
+    got_first = lax.ppermute(first_swap, "member", swap)
+    got_rest = lax.ppermute(rest_swap, "member", swap)
+    (merged_2,) = merge(merge_kernel, own[2], got_first)
+    merged_1, merged_3 = merge(merge_rest_kernel, own[1], own[3], got_rest)
+    moved = {}
+    for shift, merged in ((2, merged_2), (1, merged_1), (3, merged_3)):
         edges = [(i, (i + sign * 2 * shift) % groups) for i in range(groups)]
-        moved[shift - 1] = lax.ppermute(merged[shift - 1], "member", edges)
-    return parts[0], got, *moved
+        moved[shift] = lax.ppermute(merged, "member", edges)
+    return own[0], got_rest, moved[1], moved[2], moved[3]
 
 
 def analysis_kernel(
-    self_ref, got_ref, from_1, from_2, from_3, message_ref, own_0, own_1, own_2, own_3, swap_ref,
-    wide_ref, x2_ref, select_ref,
+    self_ref, got_ref, from_1, from_2, from_3, message_ref, own_0, own_1, own_2, own_3,
+    first_swap, rest_swap, wide_ref, x2_ref, select_ref,
 ):
     rows = self_ref.shape[0]
     members = wide_ref.shape[0] // LEVELS
@@ -391,12 +424,20 @@
         if root is None:
             new_root = factor
         else:
-            new_root = z * factor + f * root + dot_f32(high(root), narrow)
+            new_root = z * factor + f * root
         if sweep < NS_ITERS - 1:
-            once = p * factor + f * both + dot_f32(high(both), narrow)
+            once = p * factor + f * both
+            if root is None:
+                once = once + dot_f32(high(both), narrow)
+            else:
+                stacked = dot_f32(jnp.concatenate([high(both), high(root)], axis=0), narrow)
+                once = once + stacked[:members]
+                new_root = new_root + stacked[members:]
             q = p * f
             both = q * factor + f * once + dot_f32(high(once), narrow)
             p = q * f
+        else:
+            new_root = new_root + dot_f32(high(root), narrow)
         root, z = new_root, z * f
     whole = root + z * diagonal
     inner = jnp.sum(whole * forcing, axis=0, keepdims=True)
@@ -420,7 +461,8 @@
     for shift, own in enumerate((own_0, own_1, own_2, own_3)):
         first = 2 * shift * rows
         own[...] = wide_ref[first : first + rows].astype(jnp.bfloat16)
-        swap_ref[shift] = wide_ref[first + rows : first + 2 * rows].astype(jnp.bfloat16)
+        other = wide_ref[first + rows : first + 2 * rows].astype(jnp.bfloat16)
+        store_swap(shift, other, first_swap, rest_swap)
 
 
 def analysis(received, message):
@@ -432,7 +474,7 @@
         analysis_kernel,
         out_shape=exchange_shapes(rows),
         in_specs=vmem(SHIFTS + 2),
-        out_specs=tuple(vmem(SHIFTS + 1)),
+        out_specs=tuple(vmem(SHIFTS + 2)),
         compiler_params=pltpu.CompilerParams(vmem_limit_bytes=12 << 20),
         scratch_shapes=[
             pltpu.VMEM((wide, PATCH_CELLS), jnp.float32),

time: 62.4 us -> 62.4 us (level)
  starting transfers between devices: 16.6 us -> 18.6 us
  waiting for transfers between devices: 18.8 us -> 17.2 us
    ppermute x8 -> x10, starting transfers between devices: 9.69 us -> 11.7 us  [the longest x6 9.04 us: exchange(): moved[shift] = lax.ppermute(merged, 'member', edges)]
    ppermute x8 -> x10, waiting for transfers between devices: 10.5 us -> 8.82 us  [the longest x6 6.49 us: exchange(): moved[shift] = lax.ppermute(merged, 'member', edges)]
  transfers between devices with their start and end apart: 10 -> 12, of which waited for: 6 -> 5; matrix products, arithmetic and copies ran while one was open for 0% -> 0% of each run, Pallas kernels for 2% -> 2%
where the time goes in v5:
time: 62.4 us; the launch traced here: 62.3 us
  starting transfers between devices  18.6 us (30%)
  waiting for transfers between devices  17.2 us (28%)
  blocking collectives  16.5 us (26%)
  Pallas kernels  9.96 us (16%)
    all_to_all x1, blocking collectives, on_device(): message = lax.all_to_all(message, ('member', 'region'), 0, 0, tiled=True)  16.5 us
    ppermute x6, starting transfers between devices, exchange(): moved[shift] = lax.ppermute(merged, 'member', edges)  9.04 us
    ppermute x1, waiting for transfers between devices, on_device(): left = lax.ppermute(up_part, 'region', up)  8.37 us
    ppermute x6, waiting for transfers between devices, exchange(): moved[shift] = lax.ppermute(merged, 'member', edges)  6.49 us
    ppermute x1, starting transfers between devices, on_device(): right = lax.ppermute(down_part, 'region', [(j, i) for i, j in up])  4.4 us
    pallas_call x1, Pallas kernels, forecast(): pl.pallas_call(forecast_kernel, out_shape=exchange_shapes(rows), in_specs...  3.2 us
    pallas_call x1, Pallas kernels, analysis(): pl.pallas_call(analysis_kernel, out_shape=exchange_shapes(rows), in_specs...  3.17 us
    ppermute x1, starting transfers between devices, on_device(): left = lax.ppermute(up_part, 'region', up)  2.52 us
  transfers between devices with their start and end apart: 12, of which 5 were waited for; matrix products, arithmetic and copies ran while one was open for 0% of the time, Pallas kernels for 2%

profile of v5, /device:TPU:1, one launch (start us, length us, event | category | flops | bytes accessed | tf_op | source)
XLA Modules:
  0.0 62.3 jit_solution(9796756610029596670)
XLA Ops:
  0.0 1.4 %prepare.1 = (bf16[272,768]{1,0:T(8,128)(2,1)S(1)}, bf16[272,768]{1,0:T(8,128)(2,1)S(1)}, f32[256,1024]{1,0:T(8,128)S(1)}, f32[16,1024]{1,0:T(8,128)S(1)}, s32[1...) custom-call(f32[256,1024]{1,0:T(8,128)} %bitcast.13, ...), custom_call_target="tpu_custom_call" | custom-call | tf_op jit(solution)/shard_map/prepare/pallas_call | solution.py:167
  1.4 2.5 %collective-permute-start = (bf16[272,768]{1,0:T(8,128)(2,1)S(1)}, bf16[272,768]{1,0:T(8,128)(2,1)S(1)}, u32[]{:S(2)}, u32[]{:S(2)}) collective-permute-start(bf16[272,768]{1,0:T(8,128)(2,1)S(1)} %get-tuple-element.30), channel_id=1, source_target_pairs={{0,1},{1,2},{2,3},{3,4},{4,5},{5,6},{6,7},{7,8},{8,9},{9,10},{10,1... | collective-permute-start | bytes 1253384 | tf_op jit(solution)/shard_map/ppermute | solution.py:532
  3.9 4.4 %collective-permute-start.1 = (bf16[272,768]{1,0:T(8,128)(2,1)S(1)}, bf16[272,768]{1,0:T(8,128)(2,1)S(1)}, u32[]{:S(2)}, u32[]{:S(2)}) collective-permute-start(bf16[272,768]{1,0:T(8,128)(2,1)S(1)} %get-tuple-element.31), channel_id=1, source_target_pairs={{1,0},{2,1},{3,2},{4,3},{5,4},{6,5},{7,6},{8,7},{9,8},{10,9},{11,1... | collective-permute-start | bytes 1253384 | tf_op jit(solution)/shard_map/ppermute | solution.py:533
  8.3 0.9 %own_matrices.1.own_ref = bf16[4,768,256]{2,1,0:T(8,128)(2,1)S(1)} custom-call(f32[16,1024]{1,0:T(8,128)S(1)} %get-tuple-element.32.coef_ref.own_coef_ref), custom_call_target="tpu_custom_call" | custom-call | tf_op jit(solution)/shard_map/own_matrices/pallas_call | solution.py:199
  9.2 8.4 %collective-permute-done.left_ref = bf16[272,768]{1,0:T(8,128)(2,1)S(1)} collective-permute-done((bf16[272,768]{1,0:T(8,128)(2,1)S(1)}, bf16[272,768]{1,0:T(8,128)(2,1)S(1)}, u32[]{:S(2)}, u32[]{:S(2)}) %collective-permute-start) | collective-permute-done | bytes 417824 | tf_op jit(solution)/shard_map/ppermute | solution.py:532
  17.6 0.0 collective-permute-done.1.right_ref
  17.6 3.2 %forecast.1 = (bf16[256,128]{1,0:T(8,128)(2,1)S(1)}, bf16[256,128]{1,0:T(8,128)(2,1)S(1)}, bf16[256,128]{1,0:T(8,128)(2,1)S(1)}, bf16[256,128]{1,0:T(8,128)(2,1)...) custom-call(f32[256,1024]{1,0:T(8,128)S(1)} %get-tuple-element.29.state_ref, ...), custom_call_target="tpu_custom_call" | custom-call | tf_op jit(solution)/shard_map/forecast/pallas_call | solution.py:323
  20.8 1.3 %collective-permute-start.2 = (bf16[3,256,128]{2,1,0:T(8,128)(2,1)S(1)}, bf16[3,256,128]{2,1,0:T(8,128)(2,1)S(1)}, u32[]{:S(2)}, u32[]{:S(2)}) collective-permute-start(bf16[3,256,128]{2,1,0:T(8,128)(2,1)S(1)} %get-tuple-element.34), channel_id=1, source_target_pairs={{0,16},{16,0},{32,48},{48,32},{64,80},{80,64},{96,112},{112,96},{1... | collective-permute-start | bytes 589832 | tf_op jit(solution)/shard_map/ppermute | solution.py:368
  22.1 0.1 collective-permute-start.4
  22.2 1.2 %collective-permute-done.4.got_ref = bf16[256,128]{1,0:T(8,128)(2,1)S(1)} collective-permute-done((bf16[256,128]{1,0:T(8,128)(2,1)S(1)}, bf16[256,128]{1,0:T(8,128)(2,1)S(1)}, u32[]{:S(2)}, u32[]{:S(2)}) %collective-permute-start.4) | collective-permute-done | bytes 65568 | tf_op jit(solution)/shard_map/ppermute | solution.py:367
  23.4 3.0 %collective-permute-start.5 = (bf16[2,256,128]{2,1,0:T(8,128)(2,1)S(1)}, bf16[2,256,128]{2,1,0:T(8,128)(2,1)S(1)}, u32[]{:S(2)}, u32[]{:S(2)}) collective-permute-start(bf16[2,256,128]{2,1,0:T(8,128)(2,1)S(1)} %shard_map.83), channel_id=1, source_target_pairs={{0,64},{16,80},{32,96},{48,112},{64,0},{80,16},{96,32},{112,48},{1... | collective-permute-start | bytes 393224 | tf_op jit(solution)/shard_map/ppermute | solution.py:374
  26.4 0.0 collective-permute-done.2.got_ref
  26.4 0.5 collective-permute-start.3
  26.9 2.3 %collective-permute-start.6 = (bf16[2,256,128]{2,1,0:T(8,128)(2,1)S(1)}, bf16[2,256,128]{2,1,0:T(8,128)(2,1)S(1)}, u32[]{:S(2)}, u32[]{:S(2)}) collective-permute-start(bf16[2,256,128]{2,1,0:T(8,128)(2,1)S(1)} %get-tuple-element.40), channel_id=1, source_target_pairs={{0,96},{16,112},{32,0},{48,16},{64,32},{80,48},{96,64},{112,80},{1... | collective-permute-start | bytes 393224 | tf_op jit(solution)/shard_map/ppermute | solution.py:374
  29.2 0.4 message.1
  29.6 16.5 %all_to_all.11 = f32[128,1,128]{2,1,0:T(1,128)S(1)} all-to-all(f32[128,1,128]{2,1,0:T(1,128)S(1)} %bitcast.11), channel_id=1, replica_groups=mesh['member'=8,'region'=16] {'member','region'}, dimensions={0} | all-to-all | bytes 131072 | tf_op jit(solution)/shard_map/all_to_all | solution.py:535
  46.1 0.0 collective-permute-done.5.from_2
  46.1 0.0 collective-permute-done.3.from_1
  46.1 0.0 collective-permute-done.6.from_3
  46.1 3.2 %analysis.1 = (bf16[256,128]{1,0:T(8,128)(2,1)S(1)}, bf16[256,128]{1,0:T(8,128)(2,1)S(1)}, bf16[256,128]{1,0:T(8,128)(2,1)S(1)}, bf16[256,128]{1,0:T(8,128)(2,1)...) custom-call(bf16[256,128]{1,0:T(8,128)(2,1)S(1)} %get-tuple-element.33.self_ref, ...), custom_call_target="tpu_custom_call" | custom-call | tf_op jit(solution)/shard_map/analysis/pallas_call | solution.py:473
  49.3 1.1 %collective-permute-start.7 = (bf16[3,256,128]{2,1,0:T(8,128)(2,1)S(1)}, bf16[3,256,128]{2,1,0:T(8,128)(2,1)S(1)}, u32[]{:S(2)}, u32[]{:S(2)}) collective-permute-start(bf16[3,256,128]{2,1,0:T(8,128)(2,1)S(1)} %get-tuple-element.46), channel_id=1, source_target_pairs={{0,16},{16,0},{32,48},{48,32},{64,80},{80,64},{96,112},{112,96},{1... | collective-permute-start | bytes 589832 | tf_op jit(solution)/shard_map/ppermute | solution.py:368
  50.4 0.1 collective-permute-start.9
  50.4 1.2 %collective-permute-done.9.got_ref = bf16[256,128]{1,0:T(8,128)(2,1)S(1)} collective-permute-done((bf16[256,128]{1,0:T(8,128)(2,1)S(1)}, bf16[256,128]{1,0:T(8,128)(2,1)S(1)}, u32[]{:S(2)}, u32[]{:S(2)}) %collective-permute-start.9) | collective-permute-done | bytes 65568 | tf_op jit(solution)/shard_map/ppermute | solution.py:367
  51.6 0.6 collective-permute-start.10
  52.2 0.0 collective-permute-done.7.got_ref
  52.2 1.0 %collective-permute-start.11 = (bf16[2,256,128]{2,1,0:T(8,128)(2,1)S(1)}, bf16[2,256,128]{2,1,0:T(8,128)(2,1)S(1)}, u32[]{:S(2)}, u32[]{:S(2)}) collective-permute-start(bf16[2,256,128]{2,1,0:T(8,128)(2,1)S(1)} %get-tuple-element.52), channel_id=1, source_target_pairs={{0,32},{16,48},{32,64},{48,80},{64,96},{80,112},{96,0},{112,16},{1... | collective-permute-start | bytes 393224 | tf_op jit(solution)/shard_map/ppermute | solution.py:374
  53.2 1.7 %collective-permute-start.8 = (bf16[2,256,128]{2,1,0:T(8,128)(2,1)S(1)}, bf16[2,256,128]{2,1,0:T(8,128)(2,1)S(1)}, u32[]{:S(2)}, u32[]{:S(2)}) collective-permute-start(bf16[2,256,128]{2,1,0:T(8,128)(2,1)S(1)} %get-tuple-element.49), channel_id=1, source_target_pairs={{0,96},{16,112},{32,0},{48,16},{64,32},{80,48},{96,64},{112,80},{1... | collective-permute-start | bytes 393224 | tf_op jit(solution)/shard_map/ppermute | solution.py:374
  55.0 3.1 %collective-permute-done.10.from_2 = bf16[2,256,128]{2,1,0:T(8,128)(2,1)S(1)} collective-permute-done((bf16[2,256,128]{2,1,0:T(8,128)(2,1)S(1)}, bf16[2,256,128]{2,1,0:T(8,128)(2,1)S(1)}, u32[]{:S(2)}, u32[]{:S(2)}) %collective-permute-start.10) | collective-permute-done | bytes 131104 | tf_op jit(solution)/shard_map/ppermute | solution.py:374
  58.0 3.4 %collective-permute-done.11.from_3 = bf16[2,256,128]{2,1,0:T(8,128)(2,1)S(1)} collective-permute-done((bf16[2,256,128]{2,1,0:T(8,128)(2,1)S(1)}, bf16[2,256,128]{2,1,0:T(8,128)(2,1)S(1)}, u32[]{:S(2)}, u32[]{:S(2)}) %collective-permute-start.11) | collective-permute-done | bytes 131104 | tf_op jit(solution)/shard_map/ppermute | solution.py:374
  61.4 0.0 collective-permute-done.8.from_1
  61.4 0.8 %place.1 = bf16[256,1024]{1,0:T(8,128)(2,1)} custom-call(bf16[256,128]{1,0:T(8,128)(2,1)S(1)} %get-tuple-element.45.self_ref, bf16[3,256,128]{2,1,0:T(8,128)(2,1)S(1)} %collective-permute-done.7.got_ref, bf16[2,256,128]{2,1,0:T(8,128)(2,1)S(1)} %collective-permute-done.8.from_1, bf16[2,256,128]{2,1,0:T(8,128)(2,1)S(1)} %collective-permute-done.10.from_2, ...), custom_call_target="tpu_custom_call" | custom-call | tf_op jit(solution)/shard_map/place/pallas_call | solution.py:507
  (4 shorter events, 0.1 us)
Async XLA Ops:
  1.4 16.2 %collective-permute-start = (bf16[272,768]{1,0:T(8,128)(2,1)S(1)}, bf16[272,768]{1,0:T(8,128)(2,1)S(1)}, u32[]{:S(2)}, u32[]{:S(2)}) collective-permute-start(bf16[272,768]{1,0:T(8,128)(2,1)S(1)} %get-tuple-element.30), channel_id=1, source_target_pairs={{0,1},{1,2},{2,3},{3,4},{4,5},{5,6},{6,7},{7,8},{8,9},{9,10},{10,1... | collective-permute-start | bytes 1253384 | tf_op jit(solution)/shard_map/ppermute | solution.py:532
  3.9 13.7 %collective-permute-start.1 = (bf16[272,768]{1,0:T(8,128)(2,1)S(1)}, bf16[272,768]{1,0:T(8,128)(2,1)S(1)}, u32[]{:S(2)}, u32[]{:S(2)}) collective-permute-start(bf16[272,768]{1,0:T(8,128)(2,1)S(1)} %get-tuple-element.31), channel_id=1, source_target_pairs={{1,0},{2,1},{3,2},{4,3},{5,4},{6,5},{7,6},{8,7},{9,8},{10,9},{11,1... | collective-permute-start | bytes 1253384 | tf_op jit(solution)/shard_map/ppermute | solution.py:533
  20.8 5.6 %collective-permute-start.2 = (bf16[3,256,128]{2,1,0:T(8,128)(2,1)S(1)}, bf16[3,256,128]{2,1,0:T(8,128)(2,1)S(1)}, u32[]{:S(2)}, u32[]{:S(2)}) collective-permute-start(bf16[3,256,128]{2,1,0:T(8,128)(2,1)S(1)} %get-tuple-element.34), channel_id=1, source_target_pairs={{0,16},{16,0},{32,48},{48,32},{64,80},{80,64},{96,112},{112,96},{1... | collective-permute-start | bytes 589832 | tf_op jit(solution)/shard_map/ppermute | solution.py:368
  22.1 1.3 %collective-permute-start.4 = (bf16[256,128]{1,0:T(8,128)(2,1)S(1)}, bf16[256,128]{1,0:T(8,128)(2,1)S(1)}, u32[]{:S(2)}, u32[]{:S(2)}) collective-permute-start(bf16[256,128]{1,0:T(8,128)(2,1)S(1)} %get-tuple-element.39), channel_id=1, source_target_pairs={{0,16},{16,0},{32,48},{48,32},{64,80},{80,64},{96,112},{112,96},{1... | collective-permute-start | bytes 196616 | tf_op jit(solution)/shard_map/ppermute | solution.py:367
  23.4 22.7 %collective-permute-start.5 = (bf16[2,256,128]{2,1,0:T(8,128)(2,1)S(1)}, bf16[2,256,128]{2,1,0:T(8,128)(2,1)S(1)}, u32[]{:S(2)}, u32[]{:S(2)}) collective-permute-start(bf16[2,256,128]{2,1,0:T(8,128)(2,1)S(1)} %shard_map.83), channel_id=1, source_target_pairs={{0,64},{16,80},{32,96},{48,112},{64,0},{80,16},{96,32},{112,48},{1... | collective-permute-start | bytes 393224 | tf_op jit(solution)/shard_map/ppermute | solution.py:374
  26.4 19.7 %collective-permute-start.3 = (bf16[2,256,128]{2,1,0:T(8,128)(2,1)S(1)}, bf16[2,256,128]{2,1,0:T(8,128)(2,1)S(1)}, u32[]{:S(2)}, u32[]{:S(2)}) collective-permute-start(bf16[2,256,128]{2,1,0:T(8,128)(2,1)S(1)} %get-tuple-element.37), channel_id=1, source_target_pairs={{0,32},{16,48},{32,64},{48,80},{64,96},{80,112},{96,0},{112,16},{1... | collective-permute-start | bytes 393224 | tf_op jit(solution)/shard_map/ppermute | solution.py:374
  26.9 19.2 %collective-permute-start.6 = (bf16[2,256,128]{2,1,0:T(8,128)(2,1)S(1)}, bf16[2,256,128]{2,1,0:T(8,128)(2,1)S(1)}, u32[]{:S(2)}, u32[]{:S(2)}) collective-permute-start(bf16[2,256,128]{2,1,0:T(8,128)(2,1)S(1)} %get-tuple-element.40), channel_id=1, source_target_pairs={{0,96},{16,112},{32,0},{48,16},{64,32},{80,48},{96,64},{112,80},{1... | collective-permute-start | bytes 393224 | tf_op jit(solution)/shard_map/ppermute | solution.py:374
  49.3 2.9 %collective-permute-start.7 = (bf16[3,256,128]{2,1,0:T(8,128)(2,1)S(1)}, bf16[3,256,128]{2,1,0:T(8,128)(2,1)S(1)}, u32[]{:S(2)}, u32[]{:S(2)}) collective-permute-start(bf16[3,256,128]{2,1,0:T(8,128)(2,1)S(1)} %get-tuple-element.46), channel_id=1, source_target_pairs={{0,16},{16,0},{32,48},{48,32},{64,80},{80,64},{96,112},{112,96},{1... | collective-permute-start | bytes 589832 | tf_op jit(solution)/shard_map/ppermute | solution.py:368
  50.4 1.3 %collective-permute-start.9 = (bf16[256,128]{1,0:T(8,128)(2,1)S(1)}, bf16[256,128]{1,0:T(8,128)(2,1)S(1)}, u32[]{:S(2)}, u32[]{:S(2)}) collective-permute-start(bf16[256,128]{1,0:T(8,128)(2,1)S(1)} %get-tuple-element.51), channel_id=1, source_target_pairs={{0,16},{16,0},{32,48},{48,32},{64,80},{80,64},{96,112},{112,96},{1... | collective-permute-start | bytes 196616 | tf_op jit(solution)/shard_map/ppermute | solution.py:367
  51.6 6.4 %collective-permute-start.10 = (bf16[2,256,128]{2,1,0:T(8,128)(2,1)S(1)}, bf16[2,256,128]{2,1,0:T(8,128)(2,1)S(1)}, u32[]{:S(2)}, u32[]{:S(2)}) collective-permute-start(bf16[2,256,128]{2,1,0:T(8,128)(2,1)S(1)} %shard_map.85), channel_id=1, source_target_pairs={{0,64},{16,80},{32,96},{48,112},{64,0},{80,16},{96,32},{112,48},{1... | collective-permute-start | bytes 393224 | tf_op jit(solution)/shard_map/ppermute | solution.py:374
  52.2 9.2 %collective-permute-start.11 = (bf16[2,256,128]{2,1,0:T(8,128)(2,1)S(1)}, bf16[2,256,128]{2,1,0:T(8,128)(2,1)S(1)}, u32[]{:S(2)}, u32[]{:S(2)}) collective-permute-start(bf16[2,256,128]{2,1,0:T(8,128)(2,1)S(1)} %get-tuple-element.52), channel_id=1, source_target_pairs={{0,32},{16,48},{32,64},{48,80},{64,96},{80,112},{96,0},{112,16},{1... | collective-permute-start | bytes 393224 | tf_op jit(solution)/shard_map/ppermute | solution.py:374
  53.2 8.2 %collective-permute-start.8 = (bf16[2,256,128]{2,1,0:T(8,128)(2,1)S(1)}, bf16[2,256,128]{2,1,0:T(8,128)(2,1)S(1)}, u32[]{:S(2)}, u32[]{:S(2)}) collective-permute-start(bf16[2,256,128]{2,1,0:T(8,128)(2,1)S(1)} %get-tuple-element.49), channel_id=1, source_target_pairs={{0,96},{16,112},{32,0},{48,16},{64,32},{80,48},{96,64},{112,80},{1... | collective-permute-start | bytes 393224 | tf_op jit(solution)/shard_map/ppermute | solution.py:374

commit v6 on v5

--- a/solution.py
+++ b/solution.py
@@ -206,6 +206,26 @@
     )(*in_vmem(coef))
 
 
+def right_kernel(right_ref, matrix_ref):
+    rows = right_ref.shape[0] - COEF_ROWS
+    for b in range(matrix_ref.shape[0]):
+        part = slice(b * BLOCK, (b + 1) * BLOCK)
+        coef = right_ref[rows:, part].astype(jnp.float32)
+        build_matrix(matrix_ref, b, coef[0:6], coef[6:12])
+
+
+def right_matrices(right):
+    shape = ((STEPS - 1) * RIM // BLOCK, WINDOW, BLOCK)
+    return pl.pallas_call(
+        right_kernel,
+        out_shape=pltpu.VMEM(shape, jnp.bfloat16),
+        in_specs=vmem(1),
+        out_specs=vmem(1)[0],
+        compiler_params=pltpu.CompilerParams(vmem_limit_bytes=3 << 20),
+        name="right_matrices",
+    )(*in_vmem(right))
+
+
 def message_kernel(patch_ref, row_ref, value_ref, error_ref, message_ref, *, regions, groups):
     devices, count = message_ref.shape[0], patch_ref.shape[1]
     target = lax.broadcasted_iota(jnp.int32, (devices, count), 0)
@@ -244,7 +264,7 @@
 
 
 def forecast_kernel(
-    state_ref, left_ref, right_ref, own_ref, own_coef_ref, own_0, own_1, own_2, own_3,
+    state_ref, left_ref, right_ref, own_ref, side_ref, own_coef_ref, own_0, own_1, own_2, own_3,
     first_swap, rest_swap, matrix_ref, coef_ref, field_a, field_b, wide_ref,
 ):
     rows, cells = state_ref.shape
@@ -260,12 +280,13 @@
     keep, speed, matrices = [], [], []
     for b in range(blocks):
         part = slice(RIM + b * BLOCK, RIM + (b + 1) * BLOCK)
-        if side_blocks <= b < side_blocks + own_blocks:
+        if b >= side_blocks + own_blocks:
+            matrices.append((side_ref, b - side_blocks - own_blocks))
+        elif b >= side_blocks:
             matrices.append((own_ref, b - side_blocks))
         else:
-            index = b if b < side_blocks else b - own_blocks
-            build_matrix(matrix_ref, index, coef_ref[0:6, part], coef_ref[6:12, part])
-            matrices.append((matrix_ref, index))
+            build_matrix(matrix_ref, b, coef_ref[0:6, part], coef_ref[6:12, part])
+            matrices.append((matrix_ref, b))
         keep.append(1.0 - (coef_ref[12:13, part] + coef_ref[13:14, part]))
         speed.append(coef_ref[14:15, part] + coef_ref[15:16, part])
     source, target = field_a, field_b
@@ -316,14 +337,14 @@
         first_ref[...] = value
 
 
-def forecast(state, left, right, own, coef):
+def forecast(state, left, right, own, side, coef):
     rows, cells = state.shape
-    sides = 2 * (STEPS - 1) * RIM // BLOCK
+    sides = (STEPS - 1) * RIM // BLOCK
     padded = cells + 2 * HALO
     return pl.pallas_call(
         forecast_kernel,
         out_shape=exchange_shapes(rows),
-        in_specs=vmem(5),
+        in_specs=vmem(6),
         out_specs=tuple(vmem(SHIFTS + 2)),
         scratch_shapes=[
             pltpu.VMEM((sides, WINDOW, BLOCK), jnp.bfloat16),
@@ -334,7 +355,7 @@
         ],
         compiler_params=pltpu.CompilerParams(vmem_limit_bytes=16 << 20),
         name="forecast",
-    )(*in_vmem(state, left, right, own, coef))
+    )(*in_vmem(state, left, right, own, side, coef))
 
 
 def merge_kernel(own_2, got_ref, out_2):
@@ -534,7 +555,7 @@
     message = observation_message(*observed, regions, groups)
     message = lax.all_to_all(message, ("member", "region"), 0, 0, tiled=True)
     own = own_matrices(coef)
-    parts = forecast(kept, left, right, own, coef)
+    parts = forecast(kept, left, right, own, right_matrices(right), coef)
     received = exchange(parts, 1)
     parts = analysis(received, message)
     back = exchange(parts, -1)

time: 62.4 us -> 63.9 us (1.024)
  waiting for transfers between devices: 17.2 us -> 21 us
  blocking collectives: 16.5 us -> 13.6 us
    ppermute x1, waiting for transfers between devices: 0.01 us -> 7.43 us  [on_device(): right = lax.ppermute(down_part, 'region', [(j, i) for i, j in up])]
    ppermute x1, waiting for transfers between devices: 8.37 us -> 4.79 us  [on_device(): left = lax.ppermute(up_part, 'region', up)]
    all_to_all x1, blocking collectives: 16.5 us -> 13.6 us  [on_device(): message = lax.all_to_all(message, ('member', 'region'), 0, 0, tiled=True)]
    ppermute x1, starting transfers between devices: 2.52 us -> 0.01 us  [on_device(): left = lax.ppermute(up_part, 'region', up)]
    ppermute x1, starting transfers between devices: 4.4 us -> 6.84 us  [on_device(): right = lax.ppermute(down_part, 'region', [(j, i) for i, j in up])]
  transfers between devices with their start and end apart: 12 -> 12, of which waited for: 5 -> 6; matrix products, arithmetic and copies ran while one was open for 0% -> 0% of each run, Pallas kernels for 2% -> 3%
where the time goes in v6:
time: 63.9 us; the launch traced here: 63.7 us
  waiting for transfers between devices  21 us (33%)
  starting transfers between devices  19 us (30%)
  blocking collectives  13.6 us (21%)
  Pallas kernels  10 us (16%)
    all_to_all x1, blocking collectives, on_device(): message = lax.all_to_all(message, ('member', 'region'), 0, 0, tiled=True)  13.6 us
    ppermute x6, starting transfers between devices, exchange(): moved[shift] = lax.ppermute(merged, 'member', edges)  9.04 us
    ppermute x1, waiting for transfers between devices, on_device(): right = lax.ppermute(down_part, 'region', [(j, i) for i, j in up])  7.43 us
    ppermute x1, starting transfers between devices, on_device(): right = lax.ppermute(down_part, 'region', [(j, i) for i, j in up])  6.84 us
    ppermute x6, waiting for transfers between devices, exchange(): moved[shift] = lax.ppermute(merged, 'member', edges)  6.5 us
    ppermute x1, waiting for transfers between devices, on_device(): left = lax.ppermute(up_part, 'region', up)  4.79 us
    pallas_call x1, Pallas kernels, analysis(): pl.pallas_call(analysis_kernel, out_shape=exchange_shapes(rows), in_specs...  3.18 us
    ppermute x2, starting transfers between devices, exchange(): got_rest = lax.ppermute(rest_swap, 'member', swap)  2.98 us
  transfers between devices with their start and end apart: 12, of which 6 were waited for; matrix products, arithmetic and copies ran while one was open for 0% of the time, Pallas kernels for 3%

profile of v6, /device:TPU:1, one launch (start us, length us, event | category | flops | bytes accessed | tf_op | source)
XLA Modules:
  0.0 63.7 jit_solution(9966692255636586892)
XLA Ops:
  0.0 1.4 %prepare.1 = (bf16[272,768]{1,0:T(8,128)(2,1)S(1)}, bf16[272,768]{1,0:T(8,128)(2,1)S(1)}, f32[256,1024]{1,0:T(8,128)S(1)}, f32[16,1024]{1,0:T(8,128)S(1)}, s32[1...) custom-call(f32[256,1024]{1,0:T(8,128)} %bitcast.13, ...), custom_call_target="tpu_custom_call" | custom-call | tf_op jit(solution)/shard_map/prepare/pallas_call | solution.py:167
  1.4 6.8 %collective-permute-start.1 = (bf16[272,768]{1,0:T(8,128)(2,1)S(1)}, bf16[272,768]{1,0:T(8,128)(2,1)S(1)}, u32[]{:S(2)}, u32[]{:S(2)}) collective-permute-start(bf16[272,768]{1,0:T(8,128)(2,1)S(1)} %get-tuple-element.31), channel_id=1, source_target_pairs={{1,0},{2,1},{3,2},{4,3},{5,4},{6,5},{7,6},{8,7},{9,8},{10,9},{11,1... | collective-permute-start | bytes 1253384 | tf_op jit(solution)/shard_map/ppermute | solution.py:554
  8.2 0.0 collective-permute-start
  8.2 0.9 %own_matrices.1.own_ref = bf16[4,768,256]{2,1,0:T(8,128)(2,1)S(1)} custom-call(f32[16,1024]{1,0:T(8,128)S(1)} %get-tuple-element.32.coef_ref.own_coef_ref), custom_call_target="tpu_custom_call" | custom-call | tf_op jit(solution)/shard_map/own_matrices/pallas_call | solution.py:199
  9.1 7.4 %collective-permute-done.1.right_ref = bf16[272,768]{1,0:T(8,128)(2,1)S(1)} collective-permute-done((bf16[272,768]{1,0:T(8,128)(2,1)S(1)}, bf16[272,768]{1,0:T(8,128)(2,1)S(1)}, u32[]{:S(2)}, u32[]{:S(2)}) %collective-permute-start.1) | collective-permute-done | bytes 417824 | tf_op jit(solution)/shard_map/ppermute | solution.py:554
  16.6 0.4 right_matrices.1.side_ref
  17.0 4.8 %collective-permute-done.left_ref = bf16[272,768]{1,0:T(8,128)(2,1)S(1)} collective-permute-done((bf16[272,768]{1,0:T(8,128)(2,1)S(1)}, bf16[272,768]{1,0:T(8,128)(2,1)S(1)}, u32[]{:S(2)}, u32[]{:S(2)}) %collective-permute-start) | collective-permute-done | bytes 417824 | tf_op jit(solution)/shard_map/ppermute | solution.py:553
  21.8 2.8 %forecast.1 = (bf16[256,128]{1,0:T(8,128)(2,1)S(1)}, bf16[256,128]{1,0:T(8,128)(2,1)S(1)}, bf16[256,128]{1,0:T(8,128)(2,1)S(1)}, bf16[256,128]{1,0:T(8,128)(2,1)...) custom-call(f32[256,1024]{1,0:T(8,128)S(1)} %get-tuple-element.29.state_ref, ...), custom_call_target="tpu_custom_call" | custom-call | tf_op jit(solution)/shard_map/forecast/pallas_call | solution.py:344
  24.6 1.9 %collective-permute-start.2 = (bf16[3,256,128]{2,1,0:T(8,128)(2,1)S(1)}, bf16[3,256,128]{2,1,0:T(8,128)(2,1)S(1)}, u32[]{:S(2)}, u32[]{:S(2)}) collective-permute-start(bf16[3,256,128]{2,1,0:T(8,128)(2,1)S(1)} %get-tuple-element.34), channel_id=1, source_target_pairs={{0,16},{16,0},{32,48},{48,32},{64,80},{80,64},{96,112},{112,96},{1... | collective-permute-start | bytes 589832 | tf_op jit(solution)/shard_map/ppermute | solution.py:389
  26.5 0.1 collective-permute-start.4
  26.6 1.2 %collective-permute-done.4.got_ref = bf16[256,128]{1,0:T(8,128)(2,1)S(1)} collective-permute-done((bf16[256,128]{1,0:T(8,128)(2,1)S(1)}, bf16[256,128]{1,0:T(8,128)(2,1)S(1)}, u32[]{:S(2)}, u32[]{:S(2)}) %collective-permute-start.4) | collective-permute-done | bytes 65568 | tf_op jit(solution)/shard_map/ppermute | solution.py:388
  27.7 3.0 %collective-permute-start.5 = (bf16[2,256,128]{2,1,0:T(8,128)(2,1)S(1)}, bf16[2,256,128]{2,1,0:T(8,128)(2,1)S(1)}, u32[]{:S(2)}, u32[]{:S(2)}) collective-permute-start(bf16[2,256,128]{2,1,0:T(8,128)(2,1)S(1)} %shard_map.83), channel_id=1, source_target_pairs={{0,64},{16,80},{32,96},{48,112},{64,0},{80,16},{96,32},{112,48},{1... | collective-permute-start | bytes 393224 | tf_op jit(solution)/shard_map/ppermute | solution.py:395
  30.7 0.0 collective-permute-done.2.got_ref
  30.8 0.5 collective-permute-start.3
  31.2 2.3 %collective-permute-start.6 = (bf16[2,256,128]{2,1,0:T(8,128)(2,1)S(1)}, bf16[2,256,128]{2,1,0:T(8,128)(2,1)S(1)}, u32[]{:S(2)}, u32[]{:S(2)}) collective-permute-start(bf16[2,256,128]{2,1,0:T(8,128)(2,1)S(1)} %get-tuple-element.40), channel_id=1, source_target_pairs={{0,96},{16,112},{32,0},{48,16},{64,32},{80,48},{96,64},{112,80},{1... | collective-permute-start | bytes 393224 | tf_op jit(solution)/shard_map/ppermute | solution.py:395
  33.5 0.4 message.1
  33.9 13.6 %all_to_all.11 = f32[128,1,128]{2,1,0:T(1,128)S(1)} all-to-all(f32[128,1,128]{2,1,0:T(1,128)S(1)} %bitcast.11), channel_id=1, replica_groups=mesh['member'=8,'region'=16] {'member','region'}, dimensions={0} | all-to-all | bytes 131072 | tf_op jit(solution)/shard_map/all_to_all | solution.py:556
  47.5 0.0 collective-permute-done.5.from_2
  47.5 0.0 collective-permute-done.3.from_1
  47.5 0.0 collective-permute-done.6.from_3
  47.5 3.2 %analysis.1 = (bf16[256,128]{1,0:T(8,128)(2,1)S(1)}, bf16[256,128]{1,0:T(8,128)(2,1)S(1)}, bf16[256,128]{1,0:T(8,128)(2,1)S(1)}, bf16[256,128]{1,0:T(8,128)(2,1)...) custom-call(bf16[256,128]{1,0:T(8,128)(2,1)S(1)} %get-tuple-element.33.self_ref, ...), custom_call_target="tpu_custom_call" | custom-call | tf_op jit(solution)/shard_map/analysis/pallas_call | solution.py:494
  50.7 1.1 %collective-permute-start.7 = (bf16[3,256,128]{2,1,0:T(8,128)(2,1)S(1)}, bf16[3,256,128]{2,1,0:T(8,128)(2,1)S(1)}, u32[]{:S(2)}, u32[]{:S(2)}) collective-permute-start(bf16[3,256,128]{2,1,0:T(8,128)(2,1)S(1)} %get-tuple-element.46), channel_id=1, source_target_pairs={{0,16},{16,0},{32,48},{48,32},{64,80},{80,64},{96,112},{112,96},{1... | collective-permute-start | bytes 589832 | tf_op jit(solution)/shard_map/ppermute | solution.py:389
  51.8 0.1 collective-permute-start.9
  51.9 1.2 %collective-permute-done.9.got_ref = bf16[256,128]{1,0:T(8,128)(2,1)S(1)} collective-permute-done((bf16[256,128]{1,0:T(8,128)(2,1)S(1)}, bf16[256,128]{1,0:T(8,128)(2,1)S(1)}, u32[]{:S(2)}, u32[]{:S(2)}) %collective-permute-start.9) | collective-permute-done | bytes 65568 | tf_op jit(solution)/shard_map/ppermute | solution.py:388
  53.1 0.6 collective-permute-start.10
  53.6 0.0 collective-permute-done.7.got_ref
  53.7 1.0 %collective-permute-start.11 = (bf16[2,256,128]{2,1,0:T(8,128)(2,1)S(1)}, bf16[2,256,128]{2,1,0:T(8,128)(2,1)S(1)}, u32[]{:S(2)}, u32[]{:S(2)}) collective-permute-start(bf16[2,256,128]{2,1,0:T(8,128)(2,1)S(1)} %get-tuple-element.52), channel_id=1, source_target_pairs={{0,32},{16,48},{32,64},{48,80},{64,96},{80,112},{96,0},{112,16},{1... | collective-permute-start | bytes 393224 | tf_op jit(solution)/shard_map/ppermute | solution.py:395
  54.7 1.7 %collective-permute-start.8 = (bf16[2,256,128]{2,1,0:T(8,128)(2,1)S(1)}, bf16[2,256,128]{2,1,0:T(8,128)(2,1)S(1)}, u32[]{:S(2)}, u32[]{:S(2)}) collective-permute-start(bf16[2,256,128]{2,1,0:T(8,128)(2,1)S(1)} %get-tuple-element.49), channel_id=1, source_target_pairs={{0,96},{16,112},{32,0},{48,16},{64,32},{80,48},{96,64},{112,80},{1... | collective-permute-start | bytes 393224 | tf_op jit(solution)/shard_map/ppermute | solution.py:395
  56.4 3.1 %collective-permute-done.10.from_2 = bf16[2,256,128]{2,1,0:T(8,128)(2,1)S(1)} collective-permute-done((bf16[2,256,128]{2,1,0:T(8,128)(2,1)S(1)}, bf16[2,256,128]{2,1,0:T(8,128)(2,1)S(1)}, u32[]{:S(2)}, u32[]{:S(2)}) %collective-permute-start.10) | collective-permute-done | bytes 131104 | tf_op jit(solution)/shard_map/ppermute | solution.py:395
  59.5 3.4 %collective-permute-done.11.from_3 = bf16[2,256,128]{2,1,0:T(8,128)(2,1)S(1)} collective-permute-done((bf16[2,256,128]{2,1,0:T(8,128)(2,1)S(1)}, bf16[2,256,128]{2,1,0:T(8,128)(2,1)S(1)}, u32[]{:S(2)}, u32[]{:S(2)}) %collective-permute-start.11) | collective-permute-done | bytes 131104 | tf_op jit(solution)/shard_map/ppermute | solution.py:395
  62.9 0.0 collective-permute-done.8.from_1
  62.9 0.8 %place.1 = bf16[256,1024]{1,0:T(8,128)(2,1)} custom-call(bf16[256,128]{1,0:T(8,128)(2,1)S(1)} %get-tuple-element.45.self_ref, bf16[3,256,128]{2,1,0:T(8,128)(2,1)S(1)} %collective-permute-done.7.got_ref, bf16[2,256,128]{2,1,0:T(8,128)(2,1)S(1)} %collective-permute-done.8.from_1, bf16[2,256,128]{2,1,0:T(8,128)(2,1)S(1)} %collective-permute-done.10.from_2, ...), custom_call_target="tpu_custom_call" | custom-call | tf_op jit(solution)/shard_map/place/pallas_call | solution.py:528
  (4 shorter events, 0.1 us)
Async XLA Ops:
  1.4 15.2 %collective-permute-start.1 = (bf16[272,768]{1,0:T(8,128)(2,1)S(1)}, bf16[272,768]{1,0:T(8,128)(2,1)S(1)}, u32[]{:S(2)}, u32[]{:S(2)}) collective-permute-start(bf16[272,768]{1,0:T(8,128)(2,1)S(1)} %get-tuple-element.31), channel_id=1, source_target_pairs={{1,0},{2,1},{3,2},{4,3},{5,4},{6,5},{7,6},{8,7},{9,8},{10,9},{11,1... | collective-permute-start | bytes 1253384 | tf_op jit(solution)/shard_map/ppermute | solution.py:554
  8.2 13.6 %collective-permute-start = (bf16[272,768]{1,0:T(8,128)(2,1)S(1)}, bf16[272,768]{1,0:T(8,128)(2,1)S(1)}, u32[]{:S(2)}, u32[]{:S(2)}) collective-permute-start(bf16[272,768]{1,0:T(8,128)(2,1)S(1)} %get-tuple-element.30), channel_id=1, source_target_pairs={{0,1},{1,2},{2,3},{3,4},{4,5},{5,6},{6,7},{7,8},{8,9},{9,10},{10,1... | collective-permute-start | bytes 1253384 | tf_op jit(solution)/shard_map/ppermute | solution.py:553
  24.6 6.2 %collective-permute-start.2 = (bf16[3,256,128]{2,1,0:T(8,128)(2,1)S(1)}, bf16[3,256,128]{2,1,0:T(8,128)(2,1)S(1)}, u32[]{:S(2)}, u32[]{:S(2)}) collective-permute-start(bf16[3,256,128]{2,1,0:T(8,128)(2,1)S(1)} %get-tuple-element.34), channel_id=1, source_target_pairs={{0,16},{16,0},{32,48},{48,32},{64,80},{80,64},{96,112},{112,96},{1... | collective-permute-start | bytes 589832 | tf_op jit(solution)/shard_map/ppermute | solution.py:389
  26.5 1.3 %collective-permute-start.4 = (bf16[256,128]{1,0:T(8,128)(2,1)S(1)}, bf16[256,128]{1,0:T(8,128)(2,1)S(1)}, u32[]{:S(2)}, u32[]{:S(2)}) collective-permute-start(bf16[256,128]{1,0:T(8,128)(2,1)S(1)} %get-tuple-element.39), channel_id=1, source_target_pairs={{0,16},{16,0},{32,48},{48,32},{64,80},{80,64},{96,112},{112,96},{1... | collective-permute-start | bytes 196616 | tf_op jit(solution)/shard_map/ppermute | solution.py:388
  27.7 19.8 %collective-permute-start.5 = (bf16[2,256,128]{2,1,0:T(8,128)(2,1)S(1)}, bf16[2,256,128]{2,1,0:T(8,128)(2,1)S(1)}, u32[]{:S(2)}, u32[]{:S(2)}) collective-permute-start(bf16[2,256,128]{2,1,0:T(8,128)(2,1)S(1)} %shard_map.83), channel_id=1, source_target_pairs={{0,64},{16,80},{32,96},{48,112},{64,0},{80,16},{96,32},{112,48},{1... | collective-permute-start | bytes 393224 | tf_op jit(solution)/shard_map/ppermute | solution.py:395
  30.8 16.8 %collective-permute-start.3 = (bf16[2,256,128]{2,1,0:T(8,128)(2,1)S(1)}, bf16[2,256,128]{2,1,0:T(8,128)(2,1)S(1)}, u32[]{:S(2)}, u32[]{:S(2)}) collective-permute-start(bf16[2,256,128]{2,1,0:T(8,128)(2,1)S(1)} %get-tuple-element.37), channel_id=1, source_target_pairs={{0,32},{16,48},{32,64},{48,80},{64,96},{80,112},{96,0},{112,16},{1... | collective-permute-start | bytes 393224 | tf_op jit(solution)/shard_map/ppermute | solution.py:395
  31.2 16.3 %collective-permute-start.6 = (bf16[2,256,128]{2,1,0:T(8,128)(2,1)S(1)}, bf16[2,256,128]{2,1,0:T(8,128)(2,1)S(1)}, u32[]{:S(2)}, u32[]{:S(2)}) collective-permute-start(bf16[2,256,128]{2,1,0:T(8,128)(2,1)S(1)} %get-tuple-element.40), channel_id=1, source_target_pairs={{0,96},{16,112},{32,0},{48,16},{64,32},{80,48},{96,64},{112,80},{1... | collective-permute-start | bytes 393224 | tf_op jit(solution)/shard_map/ppermute | solution.py:395
  50.7 2.9 %collective-permute-start.7 = (bf16[3,256,128]{2,1,0:T(8,128)(2,1)S(1)}, bf16[3,256,128]{2,1,0:T(8,128)(2,1)S(1)}, u32[]{:S(2)}, u32[]{:S(2)}) collective-permute-start(bf16[3,256,128]{2,1,0:T(8,128)(2,1)S(1)} %get-tuple-element.46), channel_id=1, source_target_pairs={{0,16},{16,0},{32,48},{48,32},{64,80},{80,64},{96,112},{112,96},{1... | collective-permute-start | bytes 589832 | tf_op jit(solution)/shard_map/ppermute | solution.py:389
  51.8 1.3 %collective-permute-start.9 = (bf16[256,128]{1,0:T(8,128)(2,1)S(1)}, bf16[256,128]{1,0:T(8,128)(2,1)S(1)}, u32[]{:S(2)}, u32[]{:S(2)}) collective-permute-start(bf16[256,128]{1,0:T(8,128)(2,1)S(1)} %get-tuple-element.51), channel_id=1, source_target_pairs={{0,16},{16,0},{32,48},{48,32},{64,80},{80,64},{96,112},{112,96},{1... | collective-permute-start | bytes 196616 | tf_op jit(solution)/shard_map/ppermute | solution.py:388
  53.1 6.4 %collective-permute-start.10 = (bf16[2,256,128]{2,1,0:T(8,128)(2,1)S(1)}, bf16[2,256,128]{2,1,0:T(8,128)(2,1)S(1)}, u32[]{:S(2)}, u32[]{:S(2)}) collective-permute-start(bf16[2,256,128]{2,1,0:T(8,128)(2,1)S(1)} %shard_map.85), channel_id=1, source_target_pairs={{0,64},{16,80},{32,96},{48,112},{64,0},{80,16},{96,32},{112,48},{1... | collective-permute-start | bytes 393224 | tf_op jit(solution)/shard_map/ppermute | solution.py:395
  53.7 9.2 %collective-permute-start.11 = (bf16[2,256,128]{2,1,0:T(8,128)(2,1)S(1)}, bf16[2,256,128]{2,1,0:T(8,128)(2,1)S(1)}, u32[]{:S(2)}, u32[]{:S(2)}) collective-permute-start(bf16[2,256,128]{2,1,0:T(8,128)(2,1)S(1)} %get-tuple-element.52), channel_id=1, source_target_pairs={{0,32},{16,48},{32,64},{48,80},{64,96},{80,112},{96,0},{112,16},{1... | collective-permute-start | bytes 393224 | tf_op jit(solution)/shard_map/ppermute | solution.py:395
  54.7 8.2 %collective-permute-start.8 = (bf16[2,256,128]{2,1,0:T(8,128)(2,1)S(1)}, bf16[2,256,128]{2,1,0:T(8,128)(2,1)S(1)}, u32[]{:S(2)}, u32[]{:S(2)}) collective-permute-start(bf16[2,256,128]{2,1,0:T(8,128)(2,1)S(1)} %get-tuple-element.49), channel_id=1, source_target_pairs={{0,96},{16,112},{32,0},{48,16},{64,32},{80,48},{96,64},{112,80},{1... | collective-permute-start | bytes 393224 | tf_op jit(solution)/shard_map/ppermute | solution.py:395

commit v7 on v6

--- a/solution.py
+++ b/solution.py
@@ -188,22 +188,34 @@
     )(*in_hbm(state, columns, rates, speed, patch, row, value, error))
 
 
-def matrices_kernel(coef_ref, matrix_ref):
-    for b in range(matrix_ref.shape[0]):
+def matrices_kernel(coef_ref, state_ref, matrix_ref, inner_ref):
+    blocks = matrix_ref.shape[0]
+    for b in range(blocks):
         part = slice(b * BLOCK, (b + 1) * BLOCK)
         build_matrix(matrix_ref, b, coef_ref[0:6, part], coef_ref[6:12, part])
-
-
-def own_matrices(coef):
-    shape = (coef.shape[1] // BLOCK, WINDOW, BLOCK)
+    for b in range(1, blocks - 1):
+        part = slice(b * BLOCK, (b + 1) * BLOCK)
+        window = state_ref[:, part.start - RIM : part.stop + RIM].astype(jnp.bfloat16)
+        summed = dot_f32(window, matrix_ref[b])
+        keep = 1.0 - (coef_ref[12:13, part] + coef_ref[13:14, part])
+        blended = state_ref[:, part] * keep + summed
+        quick = coef_ref[14:15, part] + coef_ref[15:16, part]
+        inner_ref[:, part.start - RIM : part.stop - RIM] = blended + quick * jnp.tanh(blended)
+
+
+def own_matrices(coef, state):
+    rows, cells = state.shape
     return pl.pallas_call(
         matrices_kernel,
-        out_shape=pltpu.VMEM(shape, jnp.bfloat16),
-        in_specs=vmem(1),
-        out_specs=vmem(1)[0],
+        out_shape=(
+            pltpu.VMEM((cells // BLOCK, WINDOW, BLOCK), jnp.bfloat16),
+            pltpu.VMEM((rows, cells - 2 * RIM), jnp.float32),
+        ),
+        in_specs=vmem(2),
+        out_specs=tuple(vmem(2)),
         compiler_params=pltpu.CompilerParams(vmem_limit_bytes=4 << 20),
         name="own_matrices",
-    )(*in_vmem(coef))
+    )(*in_vmem(coef, state))
 
 
 def right_kernel(right_ref, matrix_ref):
@@ -264,7 +276,7 @@
 
 
 def forecast_kernel(
-    state_ref, left_ref, right_ref, own_ref, side_ref, own_coef_ref, own_0, own_1, own_2, own_3,
+    state_ref, left_ref, right_ref, own_ref, side_ref, own_coef_ref, inner_ref, own_0, own_1, own_2, own_3,
     first_swap, rest_swap, matrix_ref, coef_ref, field_a, field_b, wide_ref,
 ):
     rows, cells = state_ref.shape
@@ -294,6 +306,12 @@
         for b in range(step, blocks - step):
             first = b * BLOCK
             middle = slice(first + RIM, first + RIM + BLOCK)
+            if step == 0 and side_blocks < b < side_blocks + own_blocks - 1:
+                start = (b - side_blocks) * BLOCK - RIM
+                result = inner_ref[:, start : start + BLOCK]
+                wide_ref[:, middle] = result
+                target[:, middle] = result.astype(jnp.bfloat16)
+                continue
             holder, index = matrices[b]
             summed = dot_f32(source[:, first : first + WINDOW], holder[index])
             if step > 0:
@@ -337,14 +355,14 @@
         first_ref[...] = value
 
 
-def forecast(state, left, right, own, side, coef):
+def forecast(state, left, right, own, side, coef, inner):
     rows, cells = state.shape
     sides = (STEPS - 1) * RIM // BLOCK
     padded = cells + 2 * HALO
     return pl.pallas_call(
         forecast_kernel,
         out_shape=exchange_shapes(rows),
-        in_specs=vmem(6),
+        in_specs=vmem(7),
         out_specs=tuple(vmem(SHIFTS + 2)),
         scratch_shapes=[
             pltpu.VMEM((sides, WINDOW, BLOCK), jnp.bfloat16),
@@ -355,7 +373,7 @@
         ],
         compiler_params=pltpu.CompilerParams(vmem_limit_bytes=16 << 20),
         name="forecast",
-    )(*in_vmem(state, left, right, own, side, coef))
+    )(*in_vmem(state, left, right, own, side, coef, inner))
 
 
 def merge_kernel(own_2, got_ref, out_2):
@@ -554,8 +572,8 @@
     right = lax.ppermute(down_part, "region", [(j, i) for i, j in up])
     message = observation_message(*observed, regions, groups)
     message = lax.all_to_all(message, ("member", "region"), 0, 0, tiled=True)
-    own = own_matrices(coef)
-    parts = forecast(kept, left, right, own, right_matrices(right), coef)
+    own, inner = own_matrices(coef, kept)
+    parts = forecast(kept, left, right, own, right_matrices(right), coef, inner)
     received = exchange(parts, 1)
     parts = analysis(received, message)
     back = exchange(parts, -1)

time: 63.9 us -> 63.7 us (level)
  no operation moved by 1% of the time
where the time goes in v7:
time: 63.7 us; the launch traced here: 63.6 us
  waiting for transfers between devices  20.7 us (32%)
  starting transfers between devices  19 us (30%)
  blocking collectives  13.6 us (21%)
  Pallas kernels  10.2 us (16%)
    all_to_all x1, blocking collectives, on_device(): message = lax.all_to_all(message, ('member', 'region'), 0, 0, tiled=True)  13.6 us
    ppermute x6, starting transfers between devices, exchange(): moved[shift] = lax.ppermute(merged, 'member', edges)  9.04 us
    ppermute x1, waiting for transfers between devices, on_device(): right = lax.ppermute(down_part, 'region', [(j, i) for i, j in up])  7.09 us
    ppermute x1, starting transfers between devices, on_device(): right = lax.ppermute(down_part, 'region', [(j, i) for i, j in up])  6.84 us
    ppermute x6, waiting for transfers between devices, exchange(): moved[shift] = lax.ppermute(merged, 'member', edges)  6.5 us
    ppermute x1, waiting for transfers between devices, on_device(): left = lax.ppermute(up_part, 'region', up)  4.79 us
    pallas_call x1, Pallas kernels, analysis(): pl.pallas_call(analysis_kernel, out_shape=exchange_shapes(rows), in_specs...  3.18 us
    ppermute x2, starting transfers between devices, exchange(): got_rest = lax.ppermute(rest_swap, 'member', swap)  2.98 us
  transfers between devices with their start and end apart: 12, of which 6 were waited for; matrix products, arithmetic and copies ran while one was open for 0% of the time, Pallas kernels for 3%

profile of v7, /device:TPU:1, one launch (start us, length us, event | category | flops | bytes accessed | tf_op | source)
XLA Modules:
  0.0 63.6 jit_solution(17366269955452779258)
XLA Ops:
  0.0 1.4 %prepare.1 = (bf16[272,768]{1,0:T(8,128)(2,1)S(1)}, bf16[272,768]{1,0:T(8,128)(2,1)S(1)}, f32[256,1024]{1,0:T(8,128)S(1)}, f32[16,1024]{1,0:T(8,128)S(1)}, s32[1...) custom-call(f32[256,1024]{1,0:T(8,128)} %bitcast.13, ...), custom_call_target="tpu_custom_call" | custom-call | tf_op jit(solution)/shard_map/prepare/pallas_call | solution.py:167
  1.4 6.8 %collective-permute-start.1 = (bf16[272,768]{1,0:T(8,128)(2,1)S(1)}, bf16[272,768]{1,0:T(8,128)(2,1)S(1)}, u32[]{:S(2)}, u32[]{:S(2)}) collective-permute-start(bf16[272,768]{1,0:T(8,128)(2,1)S(1)} %get-tuple-element.33), channel_id=1, source_target_pairs={{1,0},{2,1},{3,2},{4,3},{5,4},{6,5},{7,6},{8,7},{9,8},{10,9},{11,1... | collective-permute-start | bytes 1253384 | tf_op jit(solution)/shard_map/ppermute | solution.py:572
  8.2 0.0 collective-permute-start
  8.2 1.2 %own_matrices.1 = (bf16[4,768,256]{2,1,0:T(8,128)(2,1)S(1)}, f32[256,512]{1,0:T(8,128)S(1)}) custom-call(f32[16,1024]{1,0:T(8,128)S(1)} %get-tuple-element.34.coef_ref.own_coef_ref, f32[256,1024]{1,0:T(8,128)S(1)} %get-tuple-element.31.state_ref), custom_call_target="tpu_custom_call" | custom-call | tf_op jit(solution)/shard_map/own_matrices/pallas_call | solution.py:208
  9.5 7.1 %collective-permute-done.1.right_ref = bf16[272,768]{1,0:T(8,128)(2,1)S(1)} collective-permute-done((bf16[272,768]{1,0:T(8,128)(2,1)S(1)}, bf16[272,768]{1,0:T(8,128)(2,1)S(1)}, u32[]{:S(2)}, u32[]{:S(2)}) %collective-permute-start.1) | collective-permute-done | bytes 417824 | tf_op jit(solution)/shard_map/ppermute | solution.py:572
  16.6 0.4 right_matrices.1.side_ref
  17.0 4.8 %collective-permute-done.left_ref = bf16[272,768]{1,0:T(8,128)(2,1)S(1)} collective-permute-done((bf16[272,768]{1,0:T(8,128)(2,1)S(1)}, bf16[272,768]{1,0:T(8,128)(2,1)S(1)}, u32[]{:S(2)}, u32[]{:S(2)}) %collective-permute-start) | collective-permute-done | bytes 417824 | tf_op jit(solution)/shard_map/ppermute | solution.py:571
  21.8 2.6 %forecast.1 = (bf16[256,128]{1,0:T(8,128)(2,1)S(1)}, bf16[256,128]{1,0:T(8,128)(2,1)S(1)}, bf16[256,128]{1,0:T(8,128)(2,1)S(1)}, bf16[256,128]{1,0:T(8,128)(2,1)...) custom-call(f32[256,1024]{1,0:T(8,128)S(1)} %get-tuple-element.31.state_ref, ...), custom_call_target="tpu_custom_call" | custom-call | tf_op jit(solution)/shard_map/forecast/pallas_call | solution.py:362
  24.4 1.9 %collective-permute-start.2 = (bf16[3,256,128]{2,1,0:T(8,128)(2,1)S(1)}, bf16[3,256,128]{2,1,0:T(8,128)(2,1)S(1)}, u32[]{:S(2)}, u32[]{:S(2)}) collective-permute-start(bf16[3,256,128]{2,1,0:T(8,128)(2,1)S(1)} %get-tuple-element.38), channel_id=1, source_target_pairs={{0,16},{16,0},{32,48},{48,32},{64,80},{80,64},{96,112},{112,96},{1... | collective-permute-start | bytes 589832 | tf_op jit(solution)/shard_map/ppermute | solution.py:407
  26.3 0.1 collective-permute-start.4
  26.4 1.2 %collective-permute-done.4.got_ref = bf16[256,128]{1,0:T(8,128)(2,1)S(1)} collective-permute-done((bf16[256,128]{1,0:T(8,128)(2,1)S(1)}, bf16[256,128]{1,0:T(8,128)(2,1)S(1)}, u32[]{:S(2)}, u32[]{:S(2)}) %collective-permute-start.4) | collective-permute-done | bytes 65568 | tf_op jit(solution)/shard_map/ppermute | solution.py:406
  27.6 3.0 %collective-permute-start.5 = (bf16[2,256,128]{2,1,0:T(8,128)(2,1)S(1)}, bf16[2,256,128]{2,1,0:T(8,128)(2,1)S(1)}, u32[]{:S(2)}, u32[]{:S(2)}) collective-permute-start(bf16[2,256,128]{2,1,0:T(8,128)(2,1)S(1)} %shard_map.83), channel_id=1, source_target_pairs={{0,64},{16,80},{32,96},{48,112},{64,0},{80,16},{96,32},{112,48},{1... | collective-permute-start | bytes 393224 | tf_op jit(solution)/shard_map/ppermute | solution.py:413
  30.6 0.0 collective-permute-done.2.got_ref
  30.6 0.5 collective-permute-start.3
  31.1 2.3 %collective-permute-start.6 = (bf16[2,256,128]{2,1,0:T(8,128)(2,1)S(1)}, bf16[2,256,128]{2,1,0:T(8,128)(2,1)S(1)}, u32[]{:S(2)}, u32[]{:S(2)}) collective-permute-start(bf16[2,256,128]{2,1,0:T(8,128)(2,1)S(1)} %get-tuple-element.44), channel_id=1, source_target_pairs={{0,96},{16,112},{32,0},{48,16},{64,32},{80,48},{96,64},{112,80},{1... | collective-permute-start | bytes 393224 | tf_op jit(solution)/shard_map/ppermute | solution.py:413
  33.3 0.4 message.1
  33.8 13.6 %all_to_all.11 = f32[128,1,128]{2,1,0:T(1,128)S(1)} all-to-all(f32[128,1,128]{2,1,0:T(1,128)S(1)} %bitcast.11), channel_id=1, replica_groups=mesh['member'=8,'region'=16] {'member','region'}, dimensions={0} | all-to-all | bytes 131072 | tf_op jit(solution)/shard_map/all_to_all | solution.py:574
  47.3 0.0 collective-permute-done.5.from_2
  47.3 0.0 collective-permute-done.3.from_1
  47.4 0.0 collective-permute-done.6.from_3
  47.4 3.2 %analysis.1 = (bf16[256,128]{1,0:T(8,128)(2,1)S(1)}, bf16[256,128]{1,0:T(8,128)(2,1)S(1)}, bf16[256,128]{1,0:T(8,128)(2,1)S(1)}, bf16[256,128]{1,0:T(8,128)(2,1)...) custom-call(bf16[256,128]{1,0:T(8,128)(2,1)S(1)} %get-tuple-element.37.self_ref, ...), custom_call_target="tpu_custom_call" | custom-call | tf_op jit(solution)/shard_map/analysis/pallas_call | solution.py:512
  50.5 1.1 %collective-permute-start.7 = (bf16[3,256,128]{2,1,0:T(8,128)(2,1)S(1)}, bf16[3,256,128]{2,1,0:T(8,128)(2,1)S(1)}, u32[]{:S(2)}, u32[]{:S(2)}) collective-permute-start(bf16[3,256,128]{2,1,0:T(8,128)(2,1)S(1)} %get-tuple-element.50), channel_id=1, source_target_pairs={{0,16},{16,0},{32,48},{48,32},{64,80},{80,64},{96,112},{112,96},{1... | collective-permute-start | bytes 589832 | tf_op jit(solution)/shard_map/ppermute | solution.py:407
  51.6 0.1 collective-permute-start.9
  51.7 1.2 %collective-permute-done.9.got_ref = bf16[256,128]{1,0:T(8,128)(2,1)S(1)} collective-permute-done((bf16[256,128]{1,0:T(8,128)(2,1)S(1)}, bf16[256,128]{1,0:T(8,128)(2,1)S(1)}, u32[]{:S(2)}, u32[]{:S(2)}) %collective-permute-start.9) | collective-permute-done | bytes 65568 | tf_op jit(solution)/shard_map/ppermute | solution.py:406
  52.9 0.6 collective-permute-start.10
  53.5 0.0 collective-permute-done.7.got_ref
  53.5 1.0 %collective-permute-start.11 = (bf16[2,256,128]{2,1,0:T(8,128)(2,1)S(1)}, bf16[2,256,128]{2,1,0:T(8,128)(2,1)S(1)}, u32[]{:S(2)}, u32[]{:S(2)}) collective-permute-start(bf16[2,256,128]{2,1,0:T(8,128)(2,1)S(1)} %get-tuple-element.56), channel_id=1, source_target_pairs={{0,32},{16,48},{32,64},{48,80},{64,96},{80,112},{96,0},{112,16},{1... | collective-permute-start | bytes 393224 | tf_op jit(solution)/shard_map/ppermute | solution.py:413
  54.5 1.7 %collective-permute-start.8 = (bf16[2,256,128]{2,1,0:T(8,128)(2,1)S(1)}, bf16[2,256,128]{2,1,0:T(8,128)(2,1)S(1)}, u32[]{:S(2)}, u32[]{:S(2)}) collective-permute-start(bf16[2,256,128]{2,1,0:T(8,128)(2,1)S(1)} %get-tuple-element.53), channel_id=1, source_target_pairs={{0,96},{16,112},{32,0},{48,16},{64,32},{80,48},{96,64},{112,80},{1... | collective-permute-start | bytes 393224 | tf_op jit(solution)/shard_map/ppermute | solution.py:413
  56.2 3.1 %collective-permute-done.10.from_2 = bf16[2,256,128]{2,1,0:T(8,128)(2,1)S(1)} collective-permute-done((bf16[2,256,128]{2,1,0:T(8,128)(2,1)S(1)}, bf16[2,256,128]{2,1,0:T(8,128)(2,1)S(1)}, u32[]{:S(2)}, u32[]{:S(2)}) %collective-permute-start.10) | collective-permute-done | bytes 131104 | tf_op jit(solution)/shard_map/ppermute | solution.py:413
  59.3 3.4 %collective-permute-done.11.from_3 = bf16[2,256,128]{2,1,0:T(8,128)(2,1)S(1)} collective-permute-done((bf16[2,256,128]{2,1,0:T(8,128)(2,1)S(1)}, bf16[2,256,128]{2,1,0:T(8,128)(2,1)S(1)}, u32[]{:S(2)}, u32[]{:S(2)}) %collective-permute-start.11) | collective-permute-done | bytes 131104 | tf_op jit(solution)/shard_map/ppermute | solution.py:413
  62.7 0.0 collective-permute-done.8.from_1
  62.7 0.8 %place.1 = bf16[256,1024]{1,0:T(8,128)(2,1)} custom-call(bf16[256,128]{1,0:T(8,128)(2,1)S(1)} %get-tuple-element.49.self_ref, bf16[3,256,128]{2,1,0:T(8,128)(2,1)S(1)} %collective-permute-done.7.got_ref, bf16[2,256,128]{2,1,0:T(8,128)(2,1)S(1)} %collective-permute-done.8.from_1, bf16[2,256,128]{2,1,0:T(8,128)(2,1)S(1)} %collective-permute-done.10.from_2, ...), custom_call_target="tpu_custom_call" | custom-call | tf_op jit(solution)/shard_map/place/pallas_call | solution.py:546
  (4 shorter events, 0.1 us)
Async XLA Ops:
  1.4 15.2 %collective-permute-start.1 = (bf16[272,768]{1,0:T(8,128)(2,1)S(1)}, bf16[272,768]{1,0:T(8,128)(2,1)S(1)}, u32[]{:S(2)}, u32[]{:S(2)}) collective-permute-start(bf16[272,768]{1,0:T(8,128)(2,1)S(1)} %get-tuple-element.33), channel_id=1, source_target_pairs={{1,0},{2,1},{3,2},{4,3},{5,4},{6,5},{7,6},{8,7},{9,8},{10,9},{11,1... | collective-permute-start | bytes 1253384 | tf_op jit(solution)/shard_map/ppermute | solution.py:572
  8.2 13.6 %collective-permute-start = (bf16[272,768]{1,0:T(8,128)(2,1)S(1)}, bf16[272,768]{1,0:T(8,128)(2,1)S(1)}, u32[]{:S(2)}, u32[]{:S(2)}) collective-permute-start(bf16[272,768]{1,0:T(8,128)(2,1)S(1)} %get-tuple-element.32), channel_id=1, source_target_pairs={{0,1},{1,2},{2,3},{3,4},{4,5},{5,6},{6,7},{7,8},{8,9},{9,10},{10,1... | collective-permute-start | bytes 1253384 | tf_op jit(solution)/shard_map/ppermute | solution.py:571
  24.4 6.2 %collective-permute-start.2 = (bf16[3,256,128]{2,1,0:T(8,128)(2,1)S(1)}, bf16[3,256,128]{2,1,0:T(8,128)(2,1)S(1)}, u32[]{:S(2)}, u32[]{:S(2)}) collective-permute-start(bf16[3,256,128]{2,1,0:T(8,128)(2,1)S(1)} %get-tuple-element.38), channel_id=1, source_target_pairs={{0,16},{16,0},{32,48},{48,32},{64,80},{80,64},{96,112},{112,96},{1... | collective-permute-start | bytes 589832 | tf_op jit(solution)/shard_map/ppermute | solution.py:407
  26.3 1.3 %collective-permute-start.4 = (bf16[256,128]{1,0:T(8,128)(2,1)S(1)}, bf16[256,128]{1,0:T(8,128)(2,1)S(1)}, u32[]{:S(2)}, u32[]{:S(2)}) collective-permute-start(bf16[256,128]{1,0:T(8,128)(2,1)S(1)} %get-tuple-element.43), channel_id=1, source_target_pairs={{0,16},{16,0},{32,48},{48,32},{64,80},{80,64},{96,112},{112,96},{1... | collective-permute-start | bytes 196616 | tf_op jit(solution)/shard_map/ppermute | solution.py:406
  27.6 19.8 %collective-permute-start.5 = (bf16[2,256,128]{2,1,0:T(8,128)(2,1)S(1)}, bf16[2,256,128]{2,1,0:T(8,128)(2,1)S(1)}, u32[]{:S(2)}, u32[]{:S(2)}) collective-permute-start(bf16[2,256,128]{2,1,0:T(8,128)(2,1)S(1)} %shard_map.83), channel_id=1, source_target_pairs={{0,64},{16,80},{32,96},{48,112},{64,0},{80,16},{96,32},{112,48},{1... | collective-permute-start | bytes 393224 | tf_op jit(solution)/shard_map/ppermute | solution.py:413
  30.6 16.8 %collective-permute-start.3 = (bf16[2,256,128]{2,1,0:T(8,128)(2,1)S(1)}, bf16[2,256,128]{2,1,0:T(8,128)(2,1)S(1)}, u32[]{:S(2)}, u32[]{:S(2)}) collective-permute-start(bf16[2,256,128]{2,1,0:T(8,128)(2,1)S(1)} %get-tuple-element.41), channel_id=1, source_target_pairs={{0,32},{16,48},{32,64},{48,80},{64,96},{80,112},{96,0},{112,16},{1... | collective-permute-start | bytes 393224 | tf_op jit(solution)/shard_map/ppermute | solution.py:413
  31.1 16.3 %collective-permute-start.6 = (bf16[2,256,128]{2,1,0:T(8,128)(2,1)S(1)}, bf16[2,256,128]{2,1,0:T(8,128)(2,1)S(1)}, u32[]{:S(2)}, u32[]{:S(2)}) collective-permute-start(bf16[2,256,128]{2,1,0:T(8,128)(2,1)S(1)} %get-tuple-element.44), channel_id=1, source_target_pairs={{0,96},{16,112},{32,0},{48,16},{64,32},{80,48},{96,64},{112,80},{1... | collective-permute-start | bytes 393224 | tf_op jit(solution)/shard_map/ppermute | solution.py:413
  50.5 2.9 %collective-permute-start.7 = (bf16[3,256,128]{2,1,0:T(8,128)(2,1)S(1)}, bf16[3,256,128]{2,1,0:T(8,128)(2,1)S(1)}, u32[]{:S(2)}, u32[]{:S(2)}) collective-permute-start(bf16[3,256,128]{2,1,0:T(8,128)(2,1)S(1)} %get-tuple-element.50), channel_id=1, source_target_pairs={{0,16},{16,0},{32,48},{48,32},{64,80},{80,64},{96,112},{112,96},{1... | collective-permute-start | bytes 589832 | tf_op jit(solution)/shard_map/ppermute | solution.py:407
  51.6 1.3 %collective-permute-start.9 = (bf16[256,128]{1,0:T(8,128)(2,1)S(1)}, bf16[256,128]{1,0:T(8,128)(2,1)S(1)}, u32[]{:S(2)}, u32[]{:S(2)}) collective-permute-start(bf16[256,128]{1,0:T(8,128)(2,1)S(1)} %get-tuple-element.55), channel_id=1, source_target_pairs={{0,16},{16,0},{32,48},{48,32},{64,80},{80,64},{96,112},{112,96},{1... | collective-permute-start | bytes 196616 | tf_op jit(solution)/shard_map/ppermute | solution.py:406
  52.9 6.4 %collective-permute-start.10 = (bf16[2,256,128]{2,1,0:T(8,128)(2,1)S(1)}, bf16[2,256,128]{2,1,0:T(8,128)(2,1)S(1)}, u32[]{:S(2)}, u32[]{:S(2)}) collective-permute-start(bf16[2,256,128]{2,1,0:T(8,128)(2,1)S(1)} %shard_map.85), channel_id=1, source_target_pairs={{0,64},{16,80},{32,96},{48,112},{64,0},{80,16},{96,32},{112,48},{1... | collective-permute-start | bytes 393224 | tf_op jit(solution)/shard_map/ppermute | solution.py:413
  53.5 9.2 %collective-permute-start.11 = (bf16[2,256,128]{2,1,0:T(8,128)(2,1)S(1)}, bf16[2,256,128]{2,1,0:T(8,128)(2,1)S(1)}, u32[]{:S(2)}, u32[]{:S(2)}) collective-permute-start(bf16[2,256,128]{2,1,0:T(8,128)(2,1)S(1)} %get-tuple-element.56), channel_id=1, source_target_pairs={{0,32},{16,48},{32,64},{48,80},{64,96},{80,112},{96,0},{112,16},{1... | collective-permute-start | bytes 393224 | tf_op jit(solution)/shard_map/ppermute | solution.py:413
  54.5 8.2 %collective-permute-start.8 = (bf16[2,256,128]{2,1,0:T(8,128)(2,1)S(1)}, bf16[2,256,128]{2,1,0:T(8,128)(2,1)S(1)}, u32[]{:S(2)}, u32[]{:S(2)}) collective-permute-start(bf16[2,256,128]{2,1,0:T(8,128)(2,1)S(1)} %get-tuple-element.53), channel_id=1, source_target_pairs={{0,96},{16,112},{32,0},{48,16},{64,32},{80,48},{96,64},{112,80},{1... | collective-permute-start | bytes 393224 | tf_op jit(solution)/shard_map/ppermute | solution.py:413
